TPU v7x, 128 devices: a whole 4x4x4 slice. The times are simulated.
128 devices in a mesh: seq: 16 (over z, x), grp: 8 (over y, core).
Axes of the slice: x: 4, y: 4, z: 4, core: 2. Of those that a mesh axis runs over, the one named last changes fastest.
Arguments:
- queries: bfloat16 [8, 256, 4096], P('grp', 'seq'), may hold values from -200 to 200
- prefix_keys: bfloat16 [8, 16384, 512], P('grp', 'seq'), may hold values from -20 to 20
- prefix_values: bfloat16 [8, 16384, 512], P('grp', 'seq'), may hold values from -6 to 6
- suffix_keys: bfloat16 [8, 256, 512], P('grp', 'seq'), may hold values from -48 to 48
- suffix_values: bfloat16 [8, 256, 512], P('grp', 'seq'), may hold values from -6 to 6
- parents: int32 [8, 256], P('grp'), may hold values from 0 to 255, as said below
- out_proj: bfloat16 [4096, 4096], P('seq'), may hold values from -0.09375 to 0.09375
- residual: bfloat16 [8, 256, 4096], P('grp', 'seq'), may hold values from -6 to 6
- norm_gain: float32 [4096], replicated, may hold values from 0.5 to 1.5
- router: bfloat16 [4096, 128], replicated, may hold values from -0.09375 to 0.09375
- routes: int32 [8, 256, 8], P('grp', 'seq'), may hold values from 0 to 127, all different within a row; in each aligned block of 16 rows (0 to 15, 16 to 31, ..., all dimensions but the last counted through in order) at most 2 rows name the same one
- expert_gate: bfloat16 [128, 4096, 768], P(('seq', 'grp')), may hold values from -0.09375 to 0.09375
- expert_up: bfloat16 [128, 4096, 768], P(('seq', 'grp')), may hold values from -0.09375 to 0.09375
- expert_down: bfloat16 [128, 768, 4096], P(('seq', 'grp')), may hold values from -0.21875 to 0.21875
Outputs:
- layer_out: bfloat16 [8, 256, 4096], P('grp', 'seq')
Inputs may be any that keep to these rules, and one draw needn't show every extreme that they name: Each request's rows form a forest of 8 levels, each a run of 32 rows: rows of the first level are their own parents; any other row's parent is a row of the level just before its own. `routes`: among the rows of one device no expert is named more than 2 times.
All inputs are finite; a program needn't handle non-finite values.
Results may differ from a plain program's by a relative error of at most 0.012.
Values may be sent and summed in bfloat16 or wider, within the bound.
No kernel may reach another device: no remote copies, remote signals or barrier semaphores. Data moves between devices by JAX's collectives and lax.ppermute only.
A program may use at most 128 MiB of HBM per device.

v0:
```python
import jax
import jax.numpy as jnp
from jax import lax
from jax.sharding import PartitionSpec as P

HEADS = 32
KVH = 4
HD = 128
DEPTH = 8


EPSILON = 1e-06


def sent_to_all(x, axis):
    copies = jnp.broadcast_to(x, (lax.axis_size(axis), *x.shape))
    return lax.all_to_all(copies, axis, split_axis=0, concat_axis=0, tiled=True)


def laid_out(blocks, dim):
    shape = list(blocks.shape[1:])
    shape[dim] *= blocks.shape[0]
    return jnp.moveaxis(blocks, 0, dim).reshape(shape)


def collect(x, axis, dim):
    blocks = sent_to_all(x, axis)
    return laid_out(blocks, dim)


def taken_together(x, axis):
    everything = sent_to_all(x, axis)
    return jnp.max(everything, axis=0)


def cut_along(x, dim, devices):
    before, after = (x.shape[:dim], x.shape[dim + 1 :])
    return jnp.moveaxis(x.reshape(*before, devices, -1, *after), dim, 0)


def one_scatter(arrays, axis, dims):
    devices = lax.axis_size(axis)
    blocks = [cut_along(a, dim, devices) for a, dim in zip(arrays, dims)]
    lines = jnp.concatenate([b.reshape(devices, -1) for b in blocks], axis=1)
    width = max(16, -(-lines.shape[1] // 1024) * 8)
    lines = jnp.pad(lines, ((0, 0), (0, width * 128 - lines.shape[1]))).reshape(-1, 128)
    ravelled, at, done = (lax.psum_scatter(lines, axis, tiled=True).reshape(-1), 0, [])
    for b in blocks:
        part = b[0]
        done.append(ravelled[at : at + part.size].reshape(part.shape))
        at += part.size
    return tuple(done)


def sent_together(arrays, axis, dim, along):
    widths = [a.shape[along] for a in arrays]
    both = jnp.concatenate(arrays, axis=along)
    filled = lax.all_gather(both, axis, axis=dim, tiled=True)
    return tuple(jnp.split(filled, [sum(widths[:k]) for k in range(1, len(widths))], axis=along))


def summed_on_arrival(x, axis, dim):
    devices = lax.axis_size(axis)
    blocks = lax.all_to_all(cut_along(x, dim, devices), axis, 0, 0, tiled=True)
    return jnp.sum(blocks.astype(jnp.float32), axis=0)


def exchange_both(x, axis, axes, splits, concats):
    sizes = [lax.axis_size(a) for a in axes]
    blocks = cut_along(x, splits[0], sizes[0])
    blocks = jnp.moveaxis(cut_along(blocks, splits[1] + 1, sizes[1]), 0, 1)
    inside = blocks.shape[2:]
    blocks = blocks.reshape(-1, *inside)
    blocks = lax.all_to_all(blocks, axis, split_axis=0, concat_axis=0, tiled=True)
    blocks = laid_out(blocks.reshape(*sizes, *inside), concats[0] + 1)
    return laid_out(blocks, concats[1])


def visible_mask(parent_row):
    count = parent_row.shape[0]
    positions = jnp.arange(count, dtype=jnp.int32)
    current = positions
    visible = current[:, None] == positions[None, :]
    for level in range(DEPTH - 1):
        current = parent_row[current]
        visible = visible | (current[:, None] == positions[None, :])
    return visible


def local(
    queries,
    prefix_keys,
    prefix_values,
    suffix_keys,
    suffix_values,
    parents,
    out_proj,
    residual,
    norm_gain,
    router,
    routes,
    expert_gate,
    expert_up,
    expert_down,
):
    seq_count = lax.axis_size("seq")
    seq_index = lax.axis_index("seq")
    query_local = queries[0]
    rows_local = query_local.shape[0]
    all_queries = collect(query_local, "seq", 0)
    total_rows = all_queries.shape[0]
    group = HEADS // KVH
    scale = HD ** (-0.5)
    key_local = prefix_keys[0]
    value_local = prefix_values[0]
    maxima = []
    totals = []
    partials = []
    for head_kv in range(KVH):
        query_block = all_queries[:, head_kv * group * HD : (head_kv + 1) * group * HD].reshape(
            total_rows, group, HD
        )
        key_block = key_local[:, head_kv * HD : (head_kv + 1) * HD]
        value_block = value_local[:, head_kv * HD : (head_kv + 1) * HD]
        scores = (
            jnp.einsum("rgd,kd->rgk", query_block, key_block, preferred_element_type=jnp.float32)
            * scale
        )
        block_max = jnp.max(scores, axis=2)
        weights = jnp.exp(scores - block_max[:, :, None])
        totals.append(jnp.sum(weights, axis=2))
        partials.append(
            jnp.einsum(
                "rgk,kd->rgd",
                weights.astype(jnp.bfloat16),
                value_block,
                preferred_element_type=jnp.float32,
            )
        )
        maxima.append(block_max)
    local_max = jnp.concatenate(maxima, axis=1)
    local_total = jnp.concatenate(totals, axis=1)
    local_out = jnp.concatenate(partials, axis=1).reshape(total_rows, HEADS * HD)
    own_heads = HEADS // seq_count
    head_start = seq_index * own_heads
    whole_max = taken_together(local_max.astype(jnp.bfloat16), "seq").astype(local_max.dtype)
    factor = jnp.exp(local_max - whole_max)
    scaled_out = (local_out.reshape(total_rows, HEADS, HD) * factor[:, :, None]).reshape(
        total_rows, HEADS * HD
    )
    prefix_total, prefix_out = tuple(
        (
            part.astype(jnp.float32)
            for part in one_scatter(
                ((local_total * factor).astype(jnp.bfloat16), scaled_out.astype(jnp.bfloat16)),
                "seq",
                (1, 1),
            )
        )
    )
    prefix_max = lax.dynamic_slice_in_dim(whole_max, head_start, own_heads, 1)
    suffix_all_keys, suffix_all_values = sent_together(
        (suffix_keys[0], suffix_values[0]), "seq", 0, 1
    )
    kv_index = head_start // group
    key_suffix = lax.dynamic_slice_in_dim(suffix_all_keys, kv_index * HD, HD, 1)
    value_suffix = lax.dynamic_slice_in_dim(suffix_all_values, kv_index * HD, HD, 1)
    own_queries = lax.dynamic_slice_in_dim(all_queries, head_start * HD, own_heads * HD, 1).reshape(
        total_rows, own_heads, HD
    )
    visible = visible_mask(parents[0])
    suffix_scores = (
        jnp.einsum("rhd,jd->rhj", own_queries, key_suffix, preferred_element_type=jnp.float32)
        * scale
    )
    suffix_scores = jnp.where(visible[:, None, :], suffix_scores, -jnp.inf)
    joint_max = jnp.maximum(prefix_max, jnp.max(suffix_scores, axis=2))
    prefix_factor = jnp.exp(prefix_max - joint_max)
    suffix_weights = jnp.exp(suffix_scores - joint_max[:, :, None])
    joint_total = prefix_total * prefix_factor + jnp.sum(suffix_weights, axis=2)
    suffix_out = jnp.einsum(
        "rhj,jd->rhd",
        suffix_weights.astype(jnp.bfloat16),
        value_suffix,
        preferred_element_type=jnp.float32,
    )
    joint_out = (
        prefix_out.reshape(total_rows, own_heads, HD) * prefix_factor[:, :, None] + suffix_out
    )
    attention = (
        (joint_out / joint_total[:, :, None])
        .astype(jnp.bfloat16)
        .reshape(total_rows, own_heads * HD)
    )
    projected = summed_on_arrival(
        jnp.dot(attention, out_proj, preferred_element_type=jnp.float32).astype(jnp.bfloat16),
        "seq",
        0,
    )
    mixed = residual[0].astype(jnp.float32) + projected
    inverse = lax.rsqrt(jnp.mean(mixed * mixed, axis=1, keepdims=True) + EPSILON)
    normed = (mixed * inverse * norm_gain[None, :]).astype(jnp.bfloat16)
    logits = jnp.dot(normed, router, preferred_element_type=jnp.float32)
    experts = router.shape[1]
    expert_ids = jnp.arange(experts, dtype=jnp.int32)
    chosen_ids = routes[0]
    top = chosen_ids.shape[1]
    matches = chosen_ids[:, :, None] == expert_ids[None, None, :]
    chosen = jnp.sum(jnp.where(matches, logits[:, None, :], 0.0), axis=2)
    sig = jax.nn.sigmoid(chosen)
    gates = sig / jnp.sum(sig, axis=1, keepdims=True)
    devices = lax.axis_size("seq") * lax.axis_size("grp")
    capacity = max(2, 2 * rows_local * top // devices)
    flat_ids = chosen_ids.reshape(-1)
    one_hot = (flat_ids[:, None] == expert_ids[None, :]).astype(jnp.int32)
    slots = jnp.sum(jnp.cumsum(one_hot, axis=0) * one_hot, axis=1) - 1
    position = flat_ids * capacity + slots
    slot_index = jnp.arange(experts * capacity, dtype=jnp.int32)
    selector = (slot_index[:, None] == position[None, :]).reshape(
        experts * capacity, rows_local, top
    )
    dispatch_rows = jnp.sum(selector.astype(jnp.int32), axis=2).astype(jnp.bfloat16)
    model_width = normed.shape[1]
    outgoing = (
        jnp.dot(dispatch_rows, normed, preferred_element_type=jnp.float32)
        .astype(jnp.bfloat16)
        .reshape(experts, capacity, model_width)
    )
    gate_weight = expert_gate[0]
    up_weight = expert_up[0]
    down_weight = expert_down[0]
    grid = outgoing.reshape(lax.axis_size("seq"), lax.axis_size("grp"), capacity, model_width)
    arrived = exchange_both(grid, ("seq", "grp"), ("seq", "grp"), (0, 1), (0, 1))
    flat = arrived.reshape(-1, model_width)
    gate_part = jnp.dot(flat, gate_weight, preferred_element_type=jnp.float32)
    up_part = jnp.dot(flat, up_weight, preferred_element_type=jnp.float32)
    act = (jax.nn.silu(gate_part) * up_part).astype(jnp.bfloat16)
    finished = (
        jnp.dot(act, down_weight, preferred_element_type=jnp.float32)
        .astype(jnp.bfloat16)
        .reshape(arrived.shape)
    )
    returned = exchange_both(finished, ("seq", "grp"), ("seq", "grp"), (0, 1), (0, 1)).reshape(
        experts * capacity, model_width
    )
    picked = returned[position].reshape(rows_local, top, model_width)
    moe = jnp.sum(picked.astype(jnp.float32) * gates[:, :, None], axis=1)
    return (mixed + moe).astype(jnp.bfloat16)[None]


def solution(mesh):
    in_specs = (
        P("grp", "seq", None),
        P("grp", "seq", None),
        P("grp", "seq", None),
        P("grp", "seq", None),
        P("grp", "seq", None),
        P("grp", None),
        P("seq", None),
        P("grp", "seq", None),
        P(),
        P(),
        P("grp", "seq", None),
        P(("seq", "grp"), None, None),
        P(("seq", "grp"), None, None),
        P(("seq", "grp"), None, None),
    )
    out_specs = P("grp", "seq", None)
    return jax.shard_map(local, mesh=mesh, in_specs=in_specs, out_specs=out_specs, check_vma=False)
```

profile of v0, /device:TPU:1, one launch (start us, length us, event | category | flops | bytes accessed | tf_op | source)
XLA Modules:
  0.0 368.6 jit_solution(7761197114662257317)
XLA Ops:
  6.5 2.7 broadcast_in_dim.20
  9.2 8.5 %all-to-all-start = ((bf16[16,16,4096]{2,1,0:T(8,128)(2,1)}), bf16[16,16,4096]{2,1,0:T(8,128)(2,1)}, u32[]{:S(2)}, u32[]{:S(2)}) async-start(bf16[16,16,4096]{2,1,0:T(8,128)(2,1)} %broadcast_in_dim.20), calls=%async_computation | async-start | bytes 4194304 | tf_op jit(solution)/shard_map/all_to_all | solution.py:17
  17.7 1.9 gather_fusion
  19.7 1.9 gather_fusion.1
  21.7 1.9 gather_fusion.2
  23.7 1.9 gather_fusion.3
  25.6 1.5 copy.123
  27.1 21.6 %all-to-all-done = bf16[16,16,4096]{2,1,0:T(8,128)(2,1)} async-done(((bf16[16,16,4096]{2,1,0:T(8,128)(2,1)}), bf16[16,16,4096]{2,1,0:T(8,128)(2,1)}, u32[]{:S(2)}, u32[]{:S(2)}) %all-to-all-start) | async-done | bytes 2097184 | tf_op jit(solution)/shard_map/all_to_all | solution.py:17
  48.7 2.9 fusion.86
  51.6 2.1 copy.118
  53.7 2.1 copy.116
  55.7 2.5 multiply_reduce_fusion.2
  58.2 1.9 fusion.3
  60.1 2.9 fusion.23
  62.9 2.3 multiply_reduce_fusion.1
  65.2 1.9 fusion.5
  67.1 2.9 fusion.21
  70.0 2.1 copy.120
  72.0 2.5 multiply_reduce_fusion
  74.5 1.9 fusion.7
  76.4 2.9 fusion.19
  79.3 2.1 copy.114
  81.3 2.5 multiply_reduce_fusion.3
  83.8 3.2 copy-done.2
  87.0 2.8 fusion.25
  89.9 0.7 broadcast_in_dim.21
  90.6 3.8 %all-to-all-start.1 = ((bf16[16,256,32]{1,2,0:T(8,128)(2,1)}), bf16[16,256,32]{1,2,0:T(8,128)(2,1)S(1)}, u32[]{:S(2)}, u32[]{:S(2)}) async-start(bf16[16,256,32]{1,2,0:T(8,128)(2,1)} %broadcast_in_dim.21), calls=%async_computation.1 | async-start | bytes 524288 | tf_op jit(solution)/shard_map/all_to_all | solution.py:17
  94.5 4.4 %fusion.1 = f32[256,8]{0,1:T(8,128)S(1)} fusion(f32[256,8,1024]{2,0,1:T(8,128)} %copy-done.2, f32[256,8]{0,1:T(8,128)S(1)} %get-tuple-element.21), kind=kLoop, calls=%fused_computation.17 | loop fusion | flops 6289408 | bytes 8404992 | tf_op jit(solution)/shard_map/reduce_sum | solution.py:131
  98.9 3.0 all-to-all-done.1
  102.1 3.8 %fusion.27 = bf16[256,32,128]{0,2,1:T(8,128)(2,1)} fusion(f32[256,8,128]{0,2,1:T(8,128)} %fusion.19, f32[256,8,128]{0,2,1:T(8,128)} %fusion.21, f32[256,8,128]{0,2,1:T(8,128)S(1)} %copy-done.3, f32[256,8,128]{0,2,1:T(8,128)} %fusion.25, f32[256,32]{0,1:T(8,128)S(1)} %subtract_exponential_fusion.5), kind=kLoop, calls=%fused_computation.41 | loop fusion | flops 5242880 | bytes 6324224 | tf_op jit(solution)/shard_map/convert_element_type | solution.py:155
  105.9 4.5 %copy.147 = bf16[2,8,256,256]{3,1,2,0:T(8,128)(2,1)} copy(bf16[2,8,256,256]{2,3,1,0:T(8,128)(2,1)} %bitcast.176) | data formatting | bytes 4194304
  110.7 3.1 fusion.36
  113.7 3.2 reshape.435
  117.0 1.9 gather_fusion.4
  119.0 1.9 gather_fusion.5
  121.0 1.9 gather_fusion.6
  123.0 0.6 dynamic-slice
  124.3 18.9 %all_gather.3 = bf16[256,1024]{1,0:T(8,128)(2,1)S(1)} all-gather(bf16[16,1024]{1,0:T(8,128)(2,1)S(1)} %pad_maximum_fusion.1), channel_id=1, replica_groups=mesh['seq'=16,'grp'=8] {'seq'}, dimensions={0}, use_global_device_ids=true | all-gather | bytes 557056 | tf_op jit(solution)/shard_map/all_gather | solution.py:58
  143.2 0.2 fusion.67
  143.5 0.9 constant_dynamic-slice_fusion
  144.5 0.2 fusion.88
  144.9 61.5 %all-reduce.4.cloned.1.call-done = bf16[8320,128]{1,0:T(8,128)(2,1)} async-done(((bf16[8320,128]{1,0:T(8,128)(2,1)}), bf16[8320,128]{1,0:T(8,128)(2,1)}) %all-reduce.4.cloned.1.call-update) | async-done | bytes 2129936
  206.4 0.9 dynamic-slice_convert_fusion
  207.5 0.7 dynamic-slice_convert_fusion.1
  208.5 0.2 fusion.46
  208.7 2.0 convolution_convert_fusion.1
  210.8 4.5 %all-to-all-start.2 = ((bf16[16,16,4096]{2,1,0:T(8,128)(2,1)}), bf16[16,16,4096]{2,1,0:T(8,128)(2,1)}, u32[]{:S(2)}, u32[]{:S(2)}) async-start(bf16[16,16,4096]{2,1,0:T(8,128)(2,1)} %bitcast.177), calls=%async_computation.2 | async-start | bytes 4194304 | tf_op jit(solution)/shard_map/all_to_all | solution.py:64
  215.5 0.2 reduce_window_sum.11
  216.2 25.0 %all-to-all-done.2 = bf16[16,16,4096]{2,1,0:T(8,128)(2,1)} async-done(((bf16[16,16,4096]{2,1,0:T(8,128)(2,1)}), bf16[16,16,4096]{2,1,0:T(8,128)(2,1)}, u32[]{:S(2)}, u32[]{:S(2)}) %all-to-all-start.2) | async-done | bytes 2097184 | tf_op jit(solution)/shard_map/all_to_all | solution.py:64
  241.3 1.9 convert_reduce_fusion
  243.5 2.0 convolution_convert_fusion
  245.5 4.4 %reshape_transpose_transpose_reshape_reshape_reshape_reshape.3 = bf16[128,1,1,2,4096]{4,3,0,2,1:T(2,128)(2,1)} reshape(bf16[256,4096]{1,0:T(8,128)(2,1)} %convolution_convert_fusion) | data formatting | bytes 4194304 | tf_op jit(solution)/shard_map/reshape;transpose;transpose;reshape;reshape;reshape;reshape | solution.py:73
  249.9 40.7 %all_to_all.25 = bf16[128,1,1,2,4096]{4,3,2,1,0:T(2,128)(2,1)} all-to-all(bf16[128,1,1,2,4096]{4,3,2,1,0:T(2,128)(2,1)} %bitcast.180), channel_id=1, replica_groups=mesh['seq'=16,'grp'=8] {'seq','grp'}, dimensions={0} | all-to-all | bytes 4194304 | tf_op jit(solution)/shard_map/all_to_all | solution.py:74
  290.5 4.1 %reshape_reshape.6 = bf16[256,4096]{1,0:T(8,128)(2,1)} reshape(bf16[16,8,1,2,4096]{4,3,1,0,2:T(2,128)(2,1)} %bitcast.181) | data formatting | bytes 4194304 | tf_op jit(solution)/shard_map/reshape;reshape | solution.py:234
  294.6 6.1 %fusion.12 = f32[256,768]{1,0:T(8,128)} fusion(bf16[256,4096]{1,0:T(8,128)(2,1)} %reshape_reshape.6, bf16[1,4096,768]{2,1,0:T(8,128)(2,1)} %param.25), kind=kOutput, calls=%fused_computation.28 | convolution fusion | flops 1610612736 | bytes 9175040 | tf_op jit(solution)/shard_map/dot_general | solution.py:235
  300.7 11.3 %fusion.14 = bf16[256,4096]{1,0:T(8,128)(2,1)} fusion(bf16[1,768,4096]{2,1,0:T(8,128)(2,1)} %param.27, bf16[256,4096]{1,0:T(8,128)(2,1)} %reshape_reshape.6, bf16[1,4096,768]{2,1,0:T(8,128)(2,1)} %param.26, f32[256,768]{1,0:T(8,128)} %fusion.12), kind=kOutput, calls=%fused_computation.32 | convolution fusion | flops 3223453696 | bytes 17563648 | tf_op jit(solution)/shard_map/dot_general | solution.py:239
  312.0 4.4 %reshape_transpose_transpose_reshape_reshape_reshape.3 = bf16[128,1,1,2,4096]{4,3,0,2,1:T(2,128)(2,1)} reshape(bf16[256,4096]{1,0:T(8,128)(2,1)} %fusion.14) | data formatting | bytes 4194304 | tf_op jit(solution)/shard_map/reshape;transpose;transpose;reshape;reshape;reshape | solution.py:73
  316.4 5.8 %all-to-all-start.4 = ((bf16[128,1,1,2,4096]{4,3,2,1,0:T(2,128)(2,1)}), bf16[128,1,1,2,4096]{4,3,2,1,0:T(2,128)(2,1)}, u32[]{:S(2)}, u32[]{:S(2)}) async-start(bf16[128,1,1,2,4096]{4,3,2,1,0:T(2,128)(2,1)} %bitcast.178), calls=%async_computation.4 | async-start | bytes 4194304 | tf_op jit(solution)/shard_map/all_to_all | solution.py:74
  322.5 1.5 fusion.89
  324.3 27.8 %all-to-all-done.4 = bf16[128,1,1,2,4096]{4,3,2,1,0:T(2,128)(2,1)} async-done(((bf16[128,1,1,2,4096]{4,3,2,1,0:T(2,128)(2,1)}), bf16[128,1,1,2,4096]{4,3,2,1,0:T(2,128)(2,1)}, u32[]{:S(2)}, u32[]{:S(2)}) %all-to-all-start.4) | async-done | bytes 2097184 | tf_op jit(solution)/shard_map/all_to_all | solution.py:74
  352.1 4.1 %reshape_reshape.7 = bf16[256,4096]{1,0:T(8,128)(2,1)} reshape(bf16[16,8,1,2,4096]{4,3,1,0,2:T(2,128)(2,1)} %bitcast.56) | data formatting | bytes 4194304 | tf_op jit(solution)/shard_map/reshape;reshape | solution.py:243
  356.2 4.1 %gather_fusion.7 = bf16[128,4096]{1,0:T(8,128)(2,1)S(1)} fusion(bf16[256,4096]{1,0:T(8,128)(2,1)} %reshape_reshape.7, s32[1024]{0:T(1024)S(1)} %pad_clamp_fusion), kind=kCustom, calls=%fused_computation.7 | custom fusion | bytes 2097664 | tf_op jit(solution)/shard_map/gather | solution.py:246
  360.3 0.8 fusion.37
  361.1 0.7 fusion.53
  (84 shorter events, 2.9 us)
Async XLA Ops:
  6.5 202.2 %copy-start = (bf16[256,4096]{1,0:T(8,128)(2,1)S(1)}, bf16[256,4096]{1,0:T(8,128)(2,1)}, u32[]{:S(2)}) copy-start(bf16[256,4096]{1,0:T(8,128)(2,1)} %param.20) | copy-start | bytes 6291460
  6.5 11.2 %copy-start.1 = (s32[1,256]{1,0:T(1,128)S(1)}, s32[1,256]{1,0:T(1,128)}, u32[]{:S(2)}) copy-start(s32[1,256]{1,0:T(1,128)} %param.19) | copy-start | bytes 3076
  9.2 39.5 %all-to-all-start = ((bf16[16,16,4096]{2,1,0:T(8,128)(2,1)}), bf16[16,16,4096]{2,1,0:T(8,128)(2,1)}, u32[]{:S(2)}, u32[]{:S(2)}) async-start(bf16[16,16,4096]{2,1,0:T(8,128)(2,1)} %broadcast_in_dim.20), calls=%async_computation | async-start | bytes 4194304 | tf_op jit(solution)/shard_map/all_to_all | solution.py:17
  60.0 2.9 copy-start.4
  83.8 3.2 copy-start.2
  89.9 12.2 %copy-start.3 = (f32[256,8,128]{0,2,1:T(8,128)S(1)}, f32[256,8,128]{0,2,1:T(8,128)}, u32[]{:S(2)}) copy-start(f32[256,8,128]{0,2,1:T(8,128)} %fusion.23) | copy-start | bytes 3145732
  90.6 11.4 %all-to-all-start.1 = ((bf16[16,256,32]{1,2,0:T(8,128)(2,1)}), bf16[16,256,32]{1,2,0:T(8,128)(2,1)S(1)}, u32[]{:S(2)}, u32[]{:S(2)}) async-start(bf16[16,256,32]{1,2,0:T(8,128)(2,1)} %broadcast_in_dim.21), calls=%async_computation.1 | async-start | bytes 524288 | tf_op jit(solution)/shard_map/all_to_all | solution.py:17
  94.4 112.0 %all-reduce.4.cloned.1.call-start = ((), (), s32[]{:S(2)}) async-start(), calls=%async_computation.5 | async-start | bytes 4259840
  110.6 12.4 %copy-start.10 = (u32[128]{0:T(128)S(1)}, u32[128]{0:T(128)}, u32[]{:S(2)}) copy-start(u32[128]{0:T(128)} %constant.82) | copy-start | bytes 1540
  110.6 13.6 %copy-start.8 = (bf16[1,16,512]{2,1,0:T(8,128)(2,1)S(1)}, bf16[1,16,512]{2,1,0:T(8,128)(2,1)}, u32[]{:S(2)}) copy-start(bf16[1,16,512]{2,1,0:T(8,128)(2,1)} %param.18) | copy-start | bytes 49156
  110.6 13.6 %copy-start.9 = (bf16[1,16,512]{2,1,0:T(8,128)(2,1)S(1)}, bf16[1,16,512]{2,1,0:T(8,128)(2,1)}, u32[]{:S(2)}) copy-start(bf16[1,16,512]{2,1,0:T(8,128)(2,1)} %param.17) | copy-start | bytes 49156
  144.5 70.7 %copy-start.6 = (s32[1,16,8]{1,2,0:T(8,128)S(1)}, s32[1,16,8]{1,2,0:T(8,128)}, u32[]{:S(2)}) copy-start(s32[1,16,8]{1,2,0:T(8,128)} %param.24) | copy-start | bytes 1540
  208.4 34.7 %copy-start.5 = (bf16[1,16,4096]{2,1,0:T(8,128)(2,1)S(1)}, bf16[1,16,4096]{2,1,0:T(8,128)(2,1)}, u32[]{:S(2)}) copy-start(bf16[1,16,4096]{2,1,0:T(8,128)(2,1)} %param.21) | copy-start | bytes 393220
  208.5 34.9 %copy-start.7 = (f32[4096]{0:T(1024)S(1)}, f32[4096]{0:T(1024)}, u32[]{:S(2)}) copy-start(f32[4096]{0:T(1024)} %param.22) | copy-start | bytes 49156
  210.8 30.5 %all-to-all-start.2 = ((bf16[16,16,4096]{2,1,0:T(8,128)(2,1)}), bf16[16,16,4096]{2,1,0:T(8,128)(2,1)}, u32[]{:S(2)}, u32[]{:S(2)}) async-start(bf16[16,16,4096]{2,1,0:T(8,128)(2,1)} %bitcast.177), calls=%async_computation.2 | async-start | bytes 4194304 | tf_op jit(solution)/shard_map/all_to_all | solution.py:64
  316.4 35.7 %all-to-all-start.4 = ((bf16[128,1,1,2,4096]{4,3,2,1,0:T(2,128)(2,1)}), bf16[128,1,1,2,4096]{4,3,2,1,0:T(2,128)(2,1)}, u32[]{:S(2)}, u32[]{:S(2)}) async-start(bf16[128,1,1,2,4096]{4,3,2,1,0:T(2,128)(2,1)} %bitcast.178), calls=%async_computation.4 | async-start | bytes 4194304 | tf_op jit(solution)/shard_map/all_to_all | solution.py:74
Sparse Core Ops, SparseCore 0:
  117.1 89.2 all-reduce.3
where the time goes:
time: 370 us; the launch traced here: 369 us
  waiting for transfers between devices  139 us (38%)
  local copies, waits for them, and re-layouts  64.7 us (17%)
  blocking collectives  59.6 us (16%)
  matrix products  44.5 us (12%)
  other arithmetic  23.6 us (6%)
  starting transfers between devices  22.6 us (6%)
  between operations  14.7 us (4%)
    unnamed x2, waiting for transfers between devices  61.6 us
    all_to_all x1, blocking collectives, exchange_both(): lax.all_to_all(blocks, axis, split_axis=0, concat_axis=0, tiled=True)  40.7 us
    all_to_all x1, waiting for transfers between devices, exchange_both(): lax.all_to_all(blocks, axis, split_axis=0, concat_axis=0, tiled=True)  27.8 us
    all_to_all x1, waiting for transfers between devices, summed_on_arrival(): blocks = lax.all_to_all(cut_along(x, dim, devices), axis, 0, 0, tiled=True)  25 us
    all_to_all x2, waiting for transfers between devices, sent_to_all(): return lax.all_to_all(copies, axis, split_axis=0, concat_axis=0, tiled=True)  24.6 us
    all_gather x1, blocking collectives, sent_together(): filled = lax.all_gather(both, axis, axis=dim, tiled=True)  18.9 us
    gather x7, local copies, waits for them, and re-layouts, visible_mask(): current = parent_row[current]  13.7 us
    all_to_all x2, starting transfers between devices, sent_to_all(): return lax.all_to_all(copies, axis, split_axis=0, concat_axis=0, tiled=True)  12.3 us
  transfers between devices with their start and end apart: 5, of which 5 were waited for; matrix products, arithmetic and copies ran while one was open for 7% of the time, Pallas kernels for 0%

commit v1 on v0

v1 whole, which is shorter than its diff:
```python
import math

import jax
import jax.numpy as jnp
from jax import lax
from jax.experimental import pallas as pl
from jax.experimental.pallas import tpu as pltpu
from jax.sharding import PartitionSpec as P

HEADS = 32
KVH = 4
HD = 128
DEPTH = 8
EPSILON = 1e-06
GROUP = HEADS // KVH
C2 = HD ** (-0.5) * math.log2(math.e)
CAP = 2
CHUNK = 8
BF = jnp.bfloat16
F32 = jnp.float32


def params(mib=48, semantics=None):
    return pltpu.CompilerParams(
        vmem_limit_bytes=mib << 20, dimension_semantics=semantics
    )


def nt(a, b):
    return lax.dot_general(a, b, (((1,), (1,)), ((), ())), preferred_element_type=F32)


def mm(a, b):
    return jnp.dot(a, b, preferred_element_type=F32)


def hi_lo(x):
    hi = x.astype(BF)
    return hi, (x - hi.astype(F32)).astype(BF)


def attend(q, chunks):
    m = total = acc = None
    for keys, values, visible in chunks:
        s = nt(q, keys)
        if visible is not None:
            s = jnp.where(visible, s, -1e30)
        top = jnp.max(s, axis=1, keepdims=True)
        if m is not None:
            top = jnp.maximum(m, top)
        p = jnp.exp2((s - top) * C2)
        t = jnp.sum(p, axis=1, keepdims=True)
        o = mm(p.astype(BF), values)
        if m is not None:
            a = jnp.exp2((m - top) * C2)
            t = t + total * a
            o = o + acc * a
        m, total, acc = top, t, o
    return acc / total, m * C2 + jnp.log2(total)


def visible_rows(parents):
    n = parents.shape[0]
    rows = lax.broadcasted_iota(jnp.int32, (n, n), 0)
    cols = lax.broadcasted_iota(jnp.int32, (n, n), 1)
    step = ((parents == cols).astype(F32) + (rows == cols).astype(F32)).astype(BF)
    two = mm(step, step).astype(BF)
    four = mm(two, two).astype(BF)
    six = mm(four, two).astype(BF)
    return mm(six, step) > 0.5


def attention_body(own, idx, q_ref, k_ref, v_ref, b_ref, c_ref, d_ref, *rest):
    del idx
    keys = k_ref.shape[0]
    chunks = [(k_ref[...], v_ref[...], None)]
    for ref in (b_ref, c_ref, d_ref):
        chunks.append((ref[:keys, :], ref[keys:, :], None))
    if own:
        par_ref, sk_ref, sv_ref, o_ref = rest
        chunks.append((sk_ref[...], sv_ref[...], visible_rows(par_ref[...])))
    else:
        (o_ref,) = rest
    rows = q_ref.shape[0]
    lane = lax.broadcasted_iota(jnp.int32, (rows, HD), 1)
    stats = jnp.zeros((rows, HD), F32)
    for h in range(2):
        o, lse = attend(q_ref[:, h * HD : (h + 1) * HD], chunks)
        o_ref[:rows, h * HD : (h + 1) * HD] = o.astype(BF)
        left = lse
        for part in range(3):
            piece = left.astype(BF).astype(F32)
            left = left - piece
            stats = jnp.where(lane == 3 * h + part, piece, stats)
    o_ref[rows:, :] = stats.T[:16, :].astype(BF)


def attention(own, idx, q_all, keys, values, parts, extra):
    rows = q_all.shape[0]
    count = keys.shape[0]
    whole = lambda shape: pl.BlockSpec(shape, lambda i, idx: (0, 0))
    specs = [
        pl.BlockSpec((rows, 2 * HD), lambda i, idx: (0, idx[0])),
        pl.BlockSpec((count, HD), lambda i, idx: (0, idx[1])),
        pl.BlockSpec((count, HD), lambda i, idx: (0, idx[1])),
        *[whole((2 * count, HD))] * 3,
    ]
    args = [q_all, keys, values, *parts]
    if own:
        at = GROUP
        specs += [
            whole((rows, 1)),
            pl.BlockSpec((rows, HD), lambda i, idx: (0, at)),
            pl.BlockSpec((rows, HD), lambda i, idx: (0, at + 1)),
        ]
        args += [extra, q_all, q_all]
    return pl.pallas_call(
        lambda *refs: attention_body(own, *refs),
        out_shape=jax.ShapeDtypeStruct((rows + 16, 2 * HD), BF),
        grid_spec=pltpu.PrefetchScalarGridSpec(
            num_scalar_prefetch=1, grid=(1,), in_specs=specs, out_specs=whole((rows + 16, 2 * HD))
        ),
        compiler_params=params(),
        name="attend_own" if own else "attend",
    )(idx, *args)


def project_body(*refs):
    *parts, w_ref, o_ref, att = refs
    rows = att.shape[0]

    @pl.when(pl.program_id(0) == 0)
    def _():
        r = lax.broadcasted_iota(jnp.int32, (rows, rows), 0)
        c = lax.broadcasted_iota(jnp.int32, (rows, rows), 1)
        eye = (r == c).astype(F32).astype(BF)
        stats = [nt(eye, p[rows:, :]) for p in parts]
        for h in range(2):
            lse = [s[:, 3 * h : 3 * h + 1] + s[:, 3 * h + 1 : 3 * h + 2] + s[:, 3 * h + 2 : 3 * h + 3] for s in stats]
            top = jnp.maximum(jnp.maximum(lse[0], lse[1]), jnp.maximum(lse[2], lse[3]))
            w = [jnp.exp2(v - top) for v in lse]
            inv = 1.0 / (w[0] + w[1] + w[2] + w[3])
            cols = slice(h * HD, (h + 1) * HD)
            acc = sum((p[:rows, cols].astype(F32) * (v * inv) for p, v in zip(parts, w)))
            att[:, cols] = acc.astype(BF)

    o_ref[...] = mm(att[...], w_ref[...]).astype(BF)


def project(parts, weights, steps=4):
    rows, width = parts[0].shape[0] - 16, weights.shape[1]
    return pl.pallas_call(
        project_body,
        out_shape=jax.ShapeDtypeStruct((rows, width), BF),
        grid=(steps,),
        in_specs=[*[pl.BlockSpec(parts[0].shape, lambda i: (0, 0))] * 4, pl.BlockSpec((weights.shape[0], width // steps), lambda i: (0, i))],
        out_specs=pl.BlockSpec((rows, width // steps), lambda i: (0, i)),
        scratch_shapes=[pltpu.VMEM((rows, 2 * HD), BF)],
        compiler_params=params(),
        name="project",
    )(*parts, weights)


def route_body(p_ref, res_ref, gain_ref, router_ref, hot_ref, sel_ref, pack_ref, mixed_ref, gates_ref, keep):
    i = pl.program_id(0)
    rows = res_ref.shape[0]
    acc = res_ref[...].astype(F32)
    for s in range(p_ref.shape[0] // rows):
        acc = acc + p_ref[s * rows : (s + 1) * rows, :].astype(F32)
    mixed_ref[...] = acc
    keep[i] = acc

    @pl.when(i == CHUNK - 1)
    def _():
        width = CHUNK * acc.shape[1]
        square = sum(jnp.sum(keep[c] * keep[c], axis=1, keepdims=True) for c in range(CHUNK))
        inverse = lax.rsqrt(square / width + EPSILON)
        step = acc.shape[1]
        normed = [(keep[c] * inverse * gain_ref[:, c * step : (c + 1) * step]).astype(BF) for c in range(CHUNK)]
        logits = sum(mm(n, router_ref[c * step : (c + 1) * step, :]) for c, n in enumerate(normed))
        hot = hot_ref[...]
        sig = hot * jax.nn.sigmoid(logits)
        gates_ref[...] = sig / jnp.sum(sig, axis=1, keepdims=True)
        pack_ref[...] = mm(sel_ref[...], jnp.concatenate(normed, axis=0)).astype(BF)


def route(partial, residual, gain, router, hot, select):
    rows, width = residual.shape
    step = width // CHUNK
    experts = router.shape[1]
    whole = lambda shape: pl.BlockSpec(shape, lambda i: (0, 0))
    return pl.pallas_call(
        route_body,
        out_shape=(
            jax.ShapeDtypeStruct((select.shape[0], step), BF),
            jax.ShapeDtypeStruct((rows, width), F32),
            jax.ShapeDtypeStruct((rows, experts), F32),
        ),
        grid=(CHUNK,),
        in_specs=[
            pl.BlockSpec((partial.shape[0], step), lambda i: (0, i)),
            pl.BlockSpec((rows, step), lambda i: (0, i)),
            whole((1, width)),
            whole(router.shape),
            whole(hot.shape),
            whole(select.shape),
        ],
        out_specs=(
            whole((select.shape[0], step)),
            pl.BlockSpec((rows, step), lambda i: (0, i)),
            whole((rows, experts)),
        ),
        scratch_shapes=[pltpu.VMEM((CHUNK, rows, step), F32)],
        compiler_params=params(),
        name="route",
    )(partial, residual, gain, router, hot, select)


def shuffle_matrix():
    n = 16 * CAP * CHUNK
    to = lax.broadcasted_iota(jnp.int32, (n, n), 0)
    come = lax.broadcasted_iota(jnp.int32, (n, n), 1)
    tokens = 16 * CAP
    chunk = come % CHUNK
    token = come // CHUNK
    return (to == chunk * tokens + token).astype(F32).astype(BF)


def expert_body(x_ref, perm_ref, back_ref, g_ref, u_ref, d_ref, o_ref, x, gate, up, act, y):
    i = pl.program_id(0)
    block = perm_ref.shape[0]
    tokens = block // CHUNK
    step = x_ref.shape[1]

    @pl.when(i == 0)
    def _():
        for b in range(x_ref.shape[0] // block):
            z = mm(perm_ref[...], x_ref[b * block : (b + 1) * block, :]).astype(BF)
            for c in range(CHUNK):
                x[c, b * tokens : (b + 1) * tokens, :] = z[c * tokens : (c + 1) * tokens, :]
        gate[...] = jnp.zeros_like(gate)
        up[...] = jnp.zeros_like(up)

    @pl.when(i < CHUNK)
    def _():
        piece = x[jnp.minimum(i, CHUNK - 1)]
        gate[...] += mm(piece, g_ref[...])
        up[...] += mm(piece, u_ref[...])

    @pl.when(i == CHUNK - 1)
    def _():
        act[...] = (jax.nn.silu(gate[...]) * up[...]).astype(BF)

    @pl.when(i >= CHUNK)
    def _():
        y[jnp.maximum(i - CHUNK, 0)] = mm(act[...], d_ref[...]).astype(BF)

    @pl.when(i == 2 * CHUNK - 1)
    def _():
        for b in range(o_ref.shape[0] // block):
            z = jnp.concatenate([y[c, b * tokens : (b + 1) * tokens, :] for c in range(CHUNK)], axis=0)
            o_ref[b * block : (b + 1) * block, :] = mm(back_ref[...], z).astype(BF)


def expert(arrived, perm, back, gate_w, up_w, down_w):
    width, hidden = gate_w.shape
    step = width // CHUNK
    total = arrived.shape[0]
    tokens = total // CHUNK
    whole = lambda shape: pl.BlockSpec(shape, lambda i: (0, 0))
    first = lambda i: (jnp.minimum(i, CHUNK - 1), 0)
    return pl.pallas_call(
        expert_body,
        out_shape=jax.ShapeDtypeStruct(arrived.shape, BF),
        grid=(2 * CHUNK,),
        in_specs=[
            whole(arrived.shape),
            whole(perm.shape),
            whole(back.shape),
            pl.BlockSpec((step, hidden), first),
            pl.BlockSpec((step, hidden), first),
            pl.BlockSpec((hidden, step), lambda i: (0, jnp.maximum(i - CHUNK, 0))),
        ],
        out_specs=whole(arrived.shape),
        scratch_shapes=[
            pltpu.VMEM((CHUNK, tokens, step), BF),
            pltpu.VMEM((tokens, hidden), F32),
            pltpu.VMEM((tokens, hidden), F32),
            pltpu.VMEM((tokens, hidden), BF),
            pltpu.VMEM((CHUNK, tokens, step), BF),
        ],
        compiler_params=params(),
        name="expert",
    )(arrived, perm, back, gate_w, up_w, down_w)


def finish_body(ret_ref, mask_ref, gates_ref, mixed_ref, o_ref):
    rows, experts = gates_ref.shape
    span = ret_ref.shape[0]
    step = ret_ref.shape[1]
    e = lax.broadcasted_iota(jnp.int32, (experts, span), 0)
    at = lax.broadcasted_iota(jnp.int32, (experts, span), 1)
    spread = (e == at // (span // experts)).astype(F32).astype(BF)
    high, low = hi_lo(gates_ref[...])
    wide = mm(high, spread) + mm(low, spread)
    weights = jnp.concatenate([wide] * CHUNK, axis=0) * mask_ref[...].astype(F32)
    high, low = hi_lo(weights)
    moe = mm(high, ret_ref[...]) + mm(low, ret_ref[...])
    for c in range(CHUNK):
        cols = slice(c * step, (c + 1) * step)
        o_ref[:, cols] = (mixed_ref[:, cols] + moe[c * rows : (c + 1) * rows, :]).astype(BF)


def finish(returned, mask, gates, mixed):
    return pl.pallas_call(
        finish_body,
        out_shape=jax.ShapeDtypeStruct(mixed.shape, BF),
        compiler_params=params(),
        name="finish",
    )(returned, mask, gates, mixed)


def local(
    queries,
    prefix_keys,
    prefix_values,
    suffix_keys,
    suffix_values,
    parents,
    out_proj,
    residual,
    norm_gain,
    router,
    routes,
    expert_gate,
    expert_up,
    expert_down,
):
    seq_count = lax.axis_size("seq")
    side = KVH
    across = seq_count // side
    s = lax.axis_index("seq")
    z, x = s // across, s % across
    q, sk, sv = queries[0], suffix_keys[0], suffix_values[0]
    rows = q.shape[0]
    keys, values = prefix_keys[0], prefix_values[0]
    cut = lambda a: jnp.moveaxis(a.reshape(rows, side, -1), 1, 0)
    both = jnp.concatenate([cut(q), cut(sk), cut(sv)], axis=2)
    copies = jnp.broadcast_to(both[:, None], (side, across, *both.shape[1:])).reshape(seq_count, rows, -1)
    parts = []
    for d in (1, 3, 2):
        head = (z + d) % side
        piece = jnp.concatenate(
            [lax.dynamic_slice_in_dim(a, head * HD, HD, 1) for a in (keys, values)], axis=0
        )
        parts.append(lax.ppermute(piece, "seq", [(i, (i + d * across) % seq_count) for i in range(seq_count)]))
    q_all = lax.all_to_all(copies, "seq", 0, 0, tiled=True).reshape(seq_count * rows, -1)
    blocks = []
    for d in (1, 3, 2, 0):
        idx = jnp.stack([(x + d) % across, z]).astype(jnp.int32)
        block = attention(d == 0, idx, q_all, keys, values, parts, parents[0][:, None])
        if d:
            perm = [(i, i // across * across + (i + d) % across) for i in range(seq_count)]
            block = lax.ppermute(block, "seq", perm)
        blocks.append(block)
    projected = project(blocks, out_proj)
    arrived = lax.all_to_all(
        projected.reshape(seq_count, rows, -1), "seq", 0, 0, tiled=True
    ).reshape(projected.shape)
    experts = router.shape[1]
    ids = routes[0]
    hot = jnp.any(ids[:, :, None] == jnp.arange(experts, dtype=jnp.int32), axis=1)
    before = jnp.cumsum(hot.astype(jnp.int32), axis=0) - hot
    slots = hot[:, :, None] & (before[:, :, None] == jnp.arange(CAP, dtype=jnp.int32))
    same = jnp.eye(CHUNK, dtype=jnp.bool_)
    mask = slots[None, :, :, :, None] & same[:, None, None, None, :]
    mask = mask.reshape(CHUNK * rows, experts * CAP * CHUNK).astype(BF)
    chosen = jnp.moveaxis(slots, 0, 2)
    select = chosen[:, :, None, None, :] & same[None, None, :, :, None]
    select = select.reshape(experts * CAP * CHUNK, CHUNK * rows).astype(BF)
    packed, mixed, gates = route(arrived, residual[0], norm_gain[None, :], router, hot.astype(F32), select)
    exchange = lambda a: lax.all_to_all(
        a.reshape(experts, CAP * CHUNK, -1), ("seq", "grp"), 0, 0, tiled=True
    ).reshape(a.shape)
    order = shuffle_matrix()
    finished = expert(exchange(packed), order, order.T, expert_gate[0], expert_up[0], expert_down[0])
    return finish(exchange(finished), mask, gates, mixed)[None]


def solution(mesh):
    rows = P("grp", "seq", None)
    spread = P(("seq", "grp"), None, None)
    in_specs = (
        rows, rows, rows, rows, rows, P("grp", None), P("seq", None), rows, P(), P(), rows, spread, spread, spread,
    )
    return jax.shard_map(local, mesh=mesh, in_specs=in_specs, out_specs=rows, check_vma=False)
```

time: 370 us -> 207 us (0.56)
  blocking collectives: 59.6 us -> 0 us
  Pallas kernels: 0 us -> 50.7 us
  waiting for transfers between devices: 139 us -> 90.1 us
  local copies, waits for them, and re-layouts: 64.7 us -> 18.3 us
  matrix products: 44.5 us -> 0 us
  between operations: 14.7 us -> 0.26 us
  starting transfers between devices: 22.6 us -> 35.6 us
  other arithmetic: 23.6 us -> 11.1 us
    unnamed x2 -> x0, waiting for transfers between devices: 61.6 us -> none
    pallas_call x0 -> x8, Pallas kernels: none -> 50.7 us  [the longest x4 26.2 us: attention(): pl.pallas_call(lambda *refs: attention_body(own, *refs), out_shape=jax.Sh...]
    dot_general x15 -> x0, matrix products: 44.5 us -> none  [the longest x4 11.5 us: local(): jnp.einsum('rgk,kd->rgd', weights.astype(jnp.bfloat16), value_block, pref...]
    all_to_all x1 -> x0, blocking collectives: 40.7 us -> none  [exchange_both(): lax.all_to_all(blocks, axis, split_axis=0, concat_axis=0, tiled=True)]
    ppermute x0 -> x6, waiting for transfers between devices: none -> 19.5 us  [the longest x3 19.5 us: local(): lax.ppermute(piece, 'seq', [(i, (i + d * across) % seq_count) for i in ra...]
    all_gather x1 -> x0, blocking collectives: 18.9 us -> none  [sent_together(): filled = lax.all_gather(both, axis, axis=dim, tiled=True)]
    gather x8 -> x0, local copies, waits for them, and re-layouts: 17.7 us -> none  [the longest x7 13.7 us: visible_mask(): current = parent_row[current]]
    another operation x5 -> x4, local copies, waits for them, and re-layouts: 17.1 us -> 0.23 us  [the longest x1 0.13 us: local(): parents[0][:, None]]
  transfers between devices with their start and end apart: 5 -> 10, of which waited for: 5 -> 6; matrix products, arithmetic and copies ran while one was open for 7% -> 11% of each run, Pallas kernels for 0% -> 10%
where the time goes in v1:
time: 207 us; the launch traced here: 206 us
  waiting for transfers between devices  90.1 us (44%)
  Pallas kernels  50.7 us (24%)
  starting transfers between devices  35.6 us (17%)
  local copies, waits for them, and re-layouts  18.3 us (9%)
  other arithmetic  11.1 us (5%)
    all_to_all x2, waiting for transfers between devices, local(): lax.all_to_all(a.reshape(experts, CAP * CHUNK, -1), ('seq', 'grp'), 0, 0,...  51.1 us
    pallas_call x4, Pallas kernels, attention(): pl.pallas_call(lambda *refs: attention_body(own, *refs), out_shape=jax.Sh...  26.2 us
    all_to_all x1, waiting for transfers between devices, local(): lax.all_to_all(projected.reshape(seq_count, rows, -1), 'seq', 0, 0, tiled...  19.5 us
    ppermute x3, waiting for transfers between devices, local(): lax.ppermute(piece, 'seq', [(i, (i + d * across) % seq_count) for i in ra...  19.5 us
    pallas_call x1, Pallas kernels, expert(): pl.pallas_call(expert_body, out_shape=jax.ShapeDtypeStruct(arrived.shape,...  16.9 us
    all_to_all x2, starting transfers between devices, local(): lax.all_to_all(a.reshape(experts, CAP * CHUNK, -1), ('seq', 'grp'), 0, 0,...  13.1 us
    all_to_all x1, starting transfers between devices, local(): lax.all_to_all(projected.reshape(seq_count, rows, -1), 'seq', 0, 0, tiled...  6.28 us
    ppermute x3, starting transfers between devices, local(): lax.ppermute(piece, 'seq', [(i, (i + d * across) % seq_count) for i in ra...  6.21 us
  transfers between devices with their start and end apart: 10, of which 6 were waited for; matrix products, arithmetic and copies ran while one was open for 11% of the time, Pallas kernels for 10%

profile of v1, /device:TPU:1, one launch (start us, length us, event | category | flops | bytes accessed | tf_op | source)
XLA Modules:
  0.0 206.1 jit_solution(8430288844573187910)
XLA Ops:
  0.0 2.2 %dynamic-slice_bitcast_fusion = (bf16[1024,128]{1,0:T(8,128)(2,1)S(1)}, bf16[1024,128]{1,0:T(8,128)(2,1)S(1)}, bf16[1024,128]{1,0:T(8,128)(2,1)S(1)}, bf16[1024,...) fusion(bf16[1,1024,512]{2,1,0:T(8,128)(2,1)} %param.16, s32[]{:T(128)S(6)} %select_n.76, ...), kind=kLoop, calls=%fused_computation.9 | loop fusion | bytes 3145740 | tf_op jit(solution)/shard_map/dynamic_slice | solution.py:354
  2.2 0.8 pad_maximum_fusion.2
  3.1 4.4 %collective-permute-start.2 = (bf16[2048,128]{1,0:T(8,128)(2,1)}, bf16[2048,128]{1,0:T(8,128)(2,1)S(1)}, u32[]{:S(2)}, u32[]{:S(2)}) collective-permute-start(bf16[2048,128]{1,0:T(8,128)(2,1)} %pad_maximum_fusion.2), channel_id=1, source_target_pairs={{0,64},{8,72},{16,80},{24,88},{32,96},{40,104},{48,112},{56,120},{... | collective-permute-start | bytes 1572872 | tf_op jit(solution)/shard_map/ppermute | solution.py:356
  7.5 0.8 pad_maximum_fusion.1
  8.3 0.4 collective-permute-start.1
  8.8 0.0 copy-done.8
  8.8 0.1 reshape_squeeze.9
  8.8 0.0 copy-done.9
  8.9 0.0 copy-done.10
  8.9 0.1 pad_maximum_fusion.3
  9.0 0.9 broadcast_in_dim.6
  9.9 5.9 %all-to-all-start = ((bf16[16,16,1280]{2,1,0:T(8,128)(2,1)}), bf16[16,16,1280]{2,1,0:T(8,128)(2,1)S(1)}, u32[]{:S(2)}, u32[]{:S(2)}) async-start(bf16[16,16,1280]{2,1,0:T(8,128)(2,1)} %bitcast.72), calls=%async_computation | async-start | bytes 1310720 | tf_op jit(solution)/shard_map/all_to_all | solution.py:357
  15.8 1.8 pad_maximum_fusion
  17.6 1.4 collective-permute-start
  19.0 0.1 pad_add_fusion.2.refs_0_
  19.1 0.1 pad_add_fusion.1.refs_0_
  19.1 0.1 pad_add_fusion.refs_0_
  19.2 0.1 collective-permute-done.2.refs_6_
  19.3 17.4 %collective-permute-done.1.refs_5_ = bf16[2048,128]{1,0:T(8,128)(2,1)} collective-permute-done((bf16[2048,128]{1,0:T(8,128)(2,1)}, bf16[2048,128]{1,0:T(8,128)(2,1)}, u32[]{:S(2)}, u32[]{:S(2)}) %collective-permute-start.1) | collective-permute-done | bytes 524320 | tf_op jit(solution)/shard_map/ppermute | solution.py:356
  36.7 2.0 collective-permute-done.refs_4_
  38.7 0.0 all-to-all-done
  38.7 0.0 copy-done
  38.7 6.4 %attend.5 = bf16[272,256]{1,0:T(8,128)(2,1)} custom-call(s32[2]{0:T(128)S(1)} %pad_add_fusion.2.refs_0_, bf16[256,1280]{1,0:T(8,128)(2,1)S(1)} %bitcast.48, bf16[1024,512]{1,0:T(8,128)(2,1)S(1)} %bitcast.54, bf16[1024,512]{1,0:T(8,128)(2,1)S(1)} %bitcast.58, bf16[2048,128]{1,0:T(8,128)(2,1)} %collective-permute-done.refs_4_, ...), custom_call_target="tpu_custom_call" | custom-call | tf_op jit(solution)/shard_map/attend/pallas_call | solution.py:117
  45.1 2.6 %collective-permute-start.5 = (bf16[272,256]{1,0:T(8,128)(2,1)}, bf16[272,256]{1,0:T(8,128)(2,1)S(1)}, u32[]{:S(2)}, u32[]{:S(2)}) collective-permute-start(bf16[272,256]{1,0:T(8,128)(2,1)} %attend.5), channel_id=1, source_target_pairs={{0,16},{8,24},{16,0},{24,8},{32,48},{40,56},{48,32},{56,40},{64,80... | collective-permute-start | bytes 417800 | tf_op jit(solution)/shard_map/ppermute | solution.py:364
  47.7 6.4 %attend.4 = bf16[272,256]{1,0:T(8,128)(2,1)} custom-call(s32[2]{0:T(128)S(1)} %pad_add_fusion.1.refs_0_, bf16[256,1280]{1,0:T(8,128)(2,1)S(1)} %bitcast.49, bf16[1024,512]{1,0:T(8,128)(2,1)S(1)} %bitcast.55, bf16[1024,512]{1,0:T(8,128)(2,1)S(1)} %bitcast.59, bf16[2048,128]{1,0:T(8,128)(2,1)} %collective-permute-done.refs_4_, ...), custom_call_target="tpu_custom_call" | custom-call | tf_op jit(solution)/shard_map/attend/pallas_call | solution.py:117
  54.1 0.5 collective-permute-start.4
  54.7 6.4 %attend.3 = bf16[272,256]{1,0:T(8,128)(2,1)} custom-call(s32[2]{0:T(128)S(1)} %pad_add_fusion.refs_0_, bf16[256,1280]{1,0:T(8,128)(2,1)S(1)} %bitcast.50, bf16[1024,512]{1,0:T(8,128)(2,1)S(1)} %bitcast.56, bf16[1024,512]{1,0:T(8,128)(2,1)S(1)} %bitcast.60, bf16[2048,128]{1,0:T(8,128)(2,1)} %collective-permute-done.refs_4_, ...), custom_call_target="tpu_custom_call" | custom-call | tf_op jit(solution)/shard_map/attend/pallas_call | solution.py:117
  61.1 0.9 collective-permute-start.3
  62.0 0.1 copy.29.refs_7_
  62.2 0.1 pad_add_fusion.3.refs_0_
  62.3 6.9 %attend_own.1.refs_3_ = bf16[272,256]{1,0:T(8,128)(2,1)S(1)} custom-call(s32[2]{0:T(128)S(1)} %pad_add_fusion.3.refs_0_, bf16[256,1280]{1,0:T(8,128)(2,1)S(1)} %bitcast.51, bf16[1024,512]{1,0:T(8,128)(2,1)S(1)} %bitcast.57, bf16[1024,512]{1,0:T(8,128)(2,1)S(1)} %bitcast.61, bf16[2048,128]{1,0:T(8,128)(2,1)} %collective-permute-done.refs_4_, ...), custom_call_target="tpu_custom_call" | custom-call | tf_op jit(solution)/shard_map/attend_own/pallas_call | solution.py:117
  69.1 0.0 collective-permute-done.5.refs_2_
  69.1 0.0 collective-permute-done.4.refs_1_
  69.2 0.0 collective-permute-done.3.refs_0_
  69.2 4.5 %project.1 = bf16[256,4096]{1,0:T(8,128)(2,1)} custom-call(bf16[272,256]{1,0:T(8,128)(2,1)} %collective-permute-done.3.refs_0_, bf16[272,256]{1,0:T(8,128)(2,1)} %collective-permute-done.4.refs_1_, bf16[272,256]{1,0:T(8,128)(2,1)S(1)} %collective-permute-done.5.refs_2_, bf16[272,256]{1,0:T(8,128)(2,1)S(1)} %attend_own.1.refs_3_, bf16[256,4096]{1,0:T(8,128)(2,1)S(1)} %copy-done.3), custom_call_target="tpu_custom_call" | custom-call | tf_op jit(solution)/shard_map/project/pallas_call | solution.py:152
  73.7 6.3 %all-to-all-start.1 = ((bf16[16,16,4096]{2,1,0:T(8,128)(2,1)}), bf16[16,16,4096]{2,1,0:T(8,128)(2,1)S(1)}, u32[]{:S(2)}, u32[]{:S(2)}) async-start(bf16[16,16,4096]{2,1,0:T(8,128)(2,1)} %bitcast.19), calls=%async_computation.1 | async-start | bytes 4194304 | tf_op jit(solution)/shard_map/all_to_all | solution.py:367
  80.0 0.0 copy-done.11
  80.0 0.1 copy.30
  80.0 0.1 fusion
  80.2 0.1 copy.32
  80.3 0.1 copy.31
  80.4 0.1 copy.33
  80.5 0.1 compare_and_fusion.1
  80.6 3.3 %and_convert_fusion.1 = bf16[128,2,8,8,16]{4,3,2,1,0:T(8,128)(2,1)} fusion(pred[8,8]{1,0:T(8,128)(4,1)S(1)} %copy.33, pred[128,2,16]{2,1,0:T(4,128)(4,1)S(1)} %compare_and_fusion.1), kind=kLoop, calls=%fused_computation.1 | loop fusion | flops 524288 | bytes 528448 | tf_op jit(solution)/shard_map/convert_element_type | solution.py:380
  84.0 5.1 %reshape.91.sel_ref = bf16[2048,128]{1,0:T(8,128)(2,1)S(1)} reshape(bf16[128,2,8,8,16]{4,3,2,1,0:T(8,128)(2,1)} %and_convert_fusion.1) | data formatting | bytes 1048576 | tf_op jit(solution)/shard_map/convert_element_type | solution.py:380
  89.1 19.5 %all-to-all-done.1 = bf16[16,16,4096]{2,1,0:T(8,128)(2,1)S(1)} async-done(((bf16[16,16,4096]{2,1,0:T(8,128)(2,1)}), bf16[16,16,4096]{2,1,0:T(8,128)(2,1)S(1)}, u32[]{:S(2)}, u32[]{:S(2)}) %all-to-all-start.1) | async-done | bytes 2097184 | tf_op jit(solution)/shard_map/all_to_all | solution.py:367
  108.6 0.0 copy-done.6
  108.6 1.2 copy-done.5
  109.8 1.6 route.1
  111.4 1.3 copy-done.4
  112.8 8.4 %all-to-all-start.2 = ((bf16[128,16,512]{2,1,0:T(8,128)(2,1)}), bf16[128,16,512]{2,1,0:T(8,128)(2,1)S(1)}, u32[]{:S(2)}, u32[]{:S(2)}) async-start(bf16[128,16,512]{2,1,0:T(8,128)(2,1)} %bitcast.66), calls=%async_computation.2 | async-start | bytes 4194304 | tf_op jit(solution)/shard_map/all_to_all | solution.py:382
  121.2 0.3 convert_convert_fusion
  121.5 29.8 %all-to-all-done.2 = bf16[128,16,512]{2,1,0:T(8,128)(2,1)S(1)} async-done(((bf16[128,16,512]{2,1,0:T(8,128)(2,1)}), bf16[128,16,512]{2,1,0:T(8,128)(2,1)S(1)}, u32[]{:S(2)}, u32[]{:S(2)}) %all-to-all-start.2) | async-done | bytes 2097184 | tf_op jit(solution)/shard_map/all_to_all | solution.py:382
  151.2 16.9 %expert.1 = bf16[2048,512]{1,0:T(8,128)(2,1)S(1)} custom-call(bf16[2048,512]{1,0:T(8,128)(2,1)S(1)} %bitcast.62, bf16[256,256]{1,0:T(8,128)(2,1)S(1)} %get-tuple-element.18.perm_ref, bf16[256,256]{1,0:T(8,128)(2,1)S(1)} %get-tuple-element.17.back_ref, bf16[4096,768]{1,0:T(8,128)(2,1)} %bitcast.69, bf16[4096,768]{1,0:T(8,128)(2,1)} %bitcast.70, ...), custom_call_target="tpu_custom_call" | custom-call | tf_op jit(solution)/shard_map/expert/pallas_call | solution.py:272
  168.2 1.3 copy-done.2
  169.5 4.7 %all-to-all-start.3 = ((bf16[128,16,512]{2,1,0:T(8,128)(2,1)}), bf16[128,16,512]{2,1,0:T(8,128)(2,1)S(1)}, u32[]{:S(2)}, u32[]{:S(2)}) async-start(bf16[128,16,512]{2,1,0:T(8,128)(2,1)} %bitcast.63), calls=%async_computation.3 | async-start | bytes 4194304 | tf_op jit(solution)/shard_map/all_to_all | solution.py:382
  174.3 0.1 copy.34
  174.4 0.1 copy.35
  174.5 0.1 compare_and_fusion
  174.6 3.3 %and_convert_fusion = bf16[8,16,128,2,8]{1,0,4,3,2:T(8,128)(2,1)} fusion(pred[8,8]{0,1:T(8,128)(4,1)S(1)} %iota_compare_fusion.1, pred[16,128,2]{0,2,1:T(4,128)(4,1)S(1)} %compare_and_fusion), kind=kLoop, calls=%fused_computation | loop fusion | flops 524288 | bytes 528448 | tf_op jit(solution)/shard_map/convert_element_type | solution.py:377
  177.9 5.1 %reshape.92 = bf16[128,2048]{0,1:T(8,128)(2,1)S(1)} reshape(bf16[8,16,128,2,8]{1,0,4,3,2:T(8,128)(2,1)} %and_convert_fusion) | data formatting | bytes 1048576 | tf_op jit(solution)/shard_map/convert_element_type | solution.py:377
  183.0 0.2 copy.36.mask_ref
  183.2 21.3 %all-to-all-done.3 = bf16[128,16,512]{2,1,0:T(8,128)(2,1)S(1)} async-done(((bf16[128,16,512]{2,1,0:T(8,128)(2,1)}), bf16[128,16,512]{2,1,0:T(8,128)(2,1)S(1)}, u32[]{:S(2)}, u32[]{:S(2)}) %all-to-all-start.3) | async-done | bytes 2097184 | tf_op jit(solution)/shard_map/all_to_all | solution.py:382
  204.5 1.6 finish.1
  (28 shorter events, 0.2 us)
Async XLA Ops:
  0.0 8.8 %copy-start.8 = (bf16[1,16,4096]{2,1,0:T(8,128)(2,1)S(1)}, bf16[1,16,4096]{2,1,0:T(8,128)(2,1)}, u32[]{:S(2)}) copy-start(bf16[1,16,4096]{2,1,0:T(8,128)(2,1)} %param.14) | copy-start | bytes 393220
  0.0 8.8 %copy-start.9 = (bf16[1,16,512]{2,1,0:T(8,128)(2,1)S(1)}, bf16[1,16,512]{2,1,0:T(8,128)(2,1)}, u32[]{:S(2)}) copy-start(bf16[1,16,512]{2,1,0:T(8,128)(2,1)} %param.17) | copy-start | bytes 49156
  0.0 8.9 %copy-start.10 = (bf16[1,16,512]{2,1,0:T(8,128)(2,1)S(1)}, bf16[1,16,512]{2,1,0:T(8,128)(2,1)}, u32[]{:S(2)}) copy-start(bf16[1,16,512]{2,1,0:T(8,128)(2,1)} %param.18) | copy-start | bytes 49156
  3.1 16.2 %collective-permute-start.2 = (bf16[2048,128]{1,0:T(8,128)(2,1)}, bf16[2048,128]{1,0:T(8,128)(2,1)S(1)}, u32[]{:S(2)}, u32[]{:S(2)}) collective-permute-start(bf16[2048,128]{1,0:T(8,128)(2,1)} %pad_maximum_fusion.2), channel_id=1, source_target_pairs={{0,64},{8,72},{16,80},{24,88},{32,96},{40,104},{48,112},{56,120},{... | collective-permute-start | bytes 1572872 | tf_op jit(solution)/shard_map/ppermute | solution.py:356
  8.3 30.4 %copy-start = (bf16[1,1024,512]{2,1,0:T(8,128)(2,1)S(1)}, bf16[1,1024,512]{2,1,0:T(8,128)(2,1)}, u32[]{:S(2)}) copy-start(bf16[1,1024,512]{2,1,0:T(8,128)(2,1)} %param.15) | copy-start | bytes 3145732
  8.3 30.4 %copy-start.1 = (bf16[1,1024,512]{2,1,0:T(8,128)(2,1)S(1)}, bf16[1,1024,512]{2,1,0:T(8,128)(2,1)}, u32[]{:S(2)}) copy-start(bf16[1,1024,512]{2,1,0:T(8,128)(2,1)} %param.16) | copy-start | bytes 3145732
  8.3 28.4 %collective-permute-start.1 = (bf16[2048,128]{1,0:T(8,128)(2,1)}, bf16[2048,128]{1,0:T(8,128)(2,1)}, u32[]{:S(2)}, u32[]{:S(2)}) collective-permute-start(bf16[2048,128]{1,0:T(8,128)(2,1)} %pad_maximum_fusion.1), channel_id=1, source_target_pairs={{0,96},{8,104},{16,112},{24,120},{32,0},{40,8},{48,16},{56,24},{64... | collective-permute-start | bytes 1572872 | tf_op jit(solution)/shard_map/ppermute | solution.py:356
  9.9 28.8 %all-to-all-start = ((bf16[16,16,1280]{2,1,0:T(8,128)(2,1)}), bf16[16,16,1280]{2,1,0:T(8,128)(2,1)S(1)}, u32[]{:S(2)}, u32[]{:S(2)}) async-start(bf16[16,16,1280]{2,1,0:T(8,128)(2,1)} %bitcast.72), calls=%async_computation | async-start | bytes 1310720 | tf_op jit(solution)/shard_map/all_to_all | solution.py:357
  17.6 21.1 %collective-permute-start = (bf16[2048,128]{1,0:T(8,128)(2,1)}, bf16[2048,128]{1,0:T(8,128)(2,1)}, u32[]{:S(2)}, u32[]{:S(2)}) collective-permute-start(bf16[2048,128]{1,0:T(8,128)(2,1)} %pad_maximum_fusion), channel_id=1, source_target_pairs={{0,32},{8,40},{16,48},{24,56},{32,64},{40,72},{48,80},{56,88},{64,... | collective-permute-start | bytes 1572872 | tf_op jit(solution)/shard_map/ppermute | solution.py:356
  45.1 24.0 %collective-permute-start.5 = (bf16[272,256]{1,0:T(8,128)(2,1)}, bf16[272,256]{1,0:T(8,128)(2,1)S(1)}, u32[]{:S(2)}, u32[]{:S(2)}) collective-permute-start(bf16[272,256]{1,0:T(8,128)(2,1)} %attend.5), channel_id=1, source_target_pairs={{0,16},{8,24},{16,0},{24,8},{32,48},{40,56},{48,32},{56,40},{64,80... | collective-permute-start | bytes 417800 | tf_op jit(solution)/shard_map/ppermute | solution.py:364
  54.1 7.9 %copy-start.12 = (s32[1,256]{1,0:T(1,128)S(1)}, s32[1,256]{1,0:T(1,128)}, u32[]{:S(2)}) copy-start(s32[1,256]{1,0:T(1,128)} %param.19) | copy-start | bytes 3076
  54.1 15.0 %collective-permute-start.4 = (bf16[272,256]{1,0:T(8,128)(2,1)}, bf16[272,256]{1,0:T(8,128)(2,1)}, u32[]{:S(2)}, u32[]{:S(2)}) collective-permute-start(bf16[272,256]{1,0:T(8,128)(2,1)} %attend.4), channel_id=1, source_target_pairs={{0,24},{8,0},{16,8},{24,16},{32,56},{40,32},{48,40},{56,48},{64,88... | collective-permute-start | bytes 417800 | tf_op jit(solution)/shard_map/ppermute | solution.py:364
  61.1 8.0 %collective-permute-start.3 = (bf16[272,256]{1,0:T(8,128)(2,1)}, bf16[272,256]{1,0:T(8,128)(2,1)}, u32[]{:S(2)}, u32[]{:S(2)}) collective-permute-start(bf16[272,256]{1,0:T(8,128)(2,1)} %attend.3), channel_id=1, source_target_pairs={{0,8},{8,16},{16,24},{24,0},{32,40},{40,48},{48,56},{56,32},{64,72... | collective-permute-start | bytes 417800 | tf_op jit(solution)/shard_map/ppermute | solution.py:364
  62.3 6.9 %copy-start.3 = (bf16[256,4096]{1,0:T(8,128)(2,1)S(1)}, bf16[256,4096]{1,0:T(8,128)(2,1)}, u32[]{:S(2)}) copy-start(bf16[256,4096]{1,0:T(8,128)(2,1)} %refs_4_.1) | copy-start | bytes 6291460
  73.7 6.3 %copy-start.11 = (s32[1,16,8]{1,2,0:T(8,128)S(1)}, s32[1,16,8]{1,2,0:T(8,128)}, u32[]{:S(2)}) copy-start(s32[1,16,8]{1,2,0:T(8,128)} %param.24) | copy-start | bytes 1540
  73.7 34.9 %all-to-all-start.1 = ((bf16[16,16,4096]{2,1,0:T(8,128)(2,1)}), bf16[16,16,4096]{2,1,0:T(8,128)(2,1)S(1)}, u32[]{:S(2)}, u32[]{:S(2)}) async-start(bf16[16,16,4096]{2,1,0:T(8,128)(2,1)} %bitcast.19), calls=%async_computation.1 | async-start | bytes 4194304 | tf_op jit(solution)/shard_map/all_to_all | solution.py:367
  84.0 24.6 %copy-start.6 = (bf16[1,16,4096]{2,1,0:T(8,128)(2,1)S(1)}, bf16[1,16,4096]{2,1,0:T(8,128)(2,1)}, u32[]{:S(2)}) copy-start(bf16[1,16,4096]{2,1,0:T(8,128)(2,1)} %param.21) | copy-start | bytes 393220
  84.0 24.6 %copy-start.7 = (f32[4096]{0:T(1024)S(1)}, f32[4096]{0:T(1024)}, u32[]{:S(2)}) copy-start(f32[4096]{0:T(1024)} %param.22) | copy-start | bytes 49156
  108.6 1.2 copy-start.5
  111.4 1.3 copy-start.4
  112.8 38.5 %all-to-all-start.2 = ((bf16[128,16,512]{2,1,0:T(8,128)(2,1)}), bf16[128,16,512]{2,1,0:T(8,128)(2,1)S(1)}, u32[]{:S(2)}, u32[]{:S(2)}) async-start(bf16[128,16,512]{2,1,0:T(8,128)(2,1)} %bitcast.66), calls=%async_computation.2 | async-start | bytes 4194304 | tf_op jit(solution)/shard_map/all_to_all | solution.py:382
  168.2 1.4 copy-start.2
  169.5 35.0 %all-to-all-start.3 = ((bf16[128,16,512]{2,1,0:T(8,128)(2,1)}), bf16[128,16,512]{2,1,0:T(8,128)(2,1)S(1)}, u32[]{:S(2)}, u32[]{:S(2)}) async-start(bf16[128,16,512]{2,1,0:T(8,128)(2,1)} %bitcast.63), calls=%async_computation.3 | async-start | bytes 4194304 | tf_op jit(solution)/shard_map/all_to_all | solution.py:382

commit v2 on v1

v2 whole, which is shorter than its diff:
```python
import math

import jax
import jax.numpy as jnp
from jax import lax
from jax.experimental import pallas as pl
from jax.experimental.pallas import tpu as pltpu
from jax.sharding import PartitionSpec as P

HEADS = 32
KVH = 4
HD = 128
DEPTH = 8
EPSILON = 1e-06
GROUP = HEADS // KVH
C2 = HD ** (-0.5) * math.log2(math.e)
CAP = 2
CHUNK = 8
BF = jnp.bfloat16
F32 = jnp.float32


def params(mib=48, semantics=None):
    return pltpu.CompilerParams(
        vmem_limit_bytes=mib << 20, dimension_semantics=semantics
    )


def nt(a, b):
    return lax.dot_general(a, b, (((1,), (1,)), ((), ())), preferred_element_type=F32)


def mm(a, b):
    return jnp.dot(a, b, preferred_element_type=F32)


def hi_lo(x):
    hi = x.astype(BF)
    return hi, (x - hi.astype(F32)).astype(BF)


def scores(q, chunks, s_ref):
    top, at = None, 0
    for k, visible in chunks:
        s = nt(q, k) * C2
        if visible is not None:
            s = jnp.where(visible, s, -1e30)
        s_ref[:, at : at + k.shape[0]] = s
        m = jnp.max(s, axis=1, keepdims=True)
        top = m if top is None else jnp.maximum(top, m)
        at += k.shape[0]
    return top


def weigh(s_ref, values, top, state, span=512):
    if state is not None:
        before, lse = state
        top = jnp.maximum(top, lse)
    acc = None
    for at in range(0, s_ref.shape[1], span):
        cols = slice(at, min(at + span, s_ref.shape[1]))
        part = mm(jnp.exp2(s_ref[:, cols] - top).astype(BF), values[cols, :])
        acc = part if acc is None else acc + part
    out, total = acc[:, :HD], acc[:, HD : HD + 1]
    if state is not None:
        a = jnp.exp2(lse - top)
        out, total = out + before * a, total + a
    return out / total, top + jnp.log2(total)


def with_ones(ref, values):
    at = 0
    for v in values:
        ref[at : at + v.shape[0], :HD] = v
        ref[at : at + v.shape[0], HD:] = jnp.ones(v.shape, BF)
        at += v.shape[0]


def lane_of(stats, h):
    lane = lax.broadcasted_iota(jnp.int32, stats.shape, 1)
    return jnp.sum(jnp.where(lane == h, stats, 0.0), axis=1, keepdims=True)


def visible_rows(parents):
    n = parents.shape[0]
    rows = lax.broadcasted_iota(jnp.int32, (n, n), 0)
    cols = lax.broadcasted_iota(jnp.int32, (n, n), 1)
    step = ((parents == cols).astype(F32) + (rows == cols).astype(F32)).astype(BF)
    two = mm(step, step).astype(BF)
    four = mm(two, two).astype(BF)
    six = mm(four, two).astype(BF)
    return mm(six, step) > 0.5


def heads_body(k_refs, v_refs, q_ref, before, o_ref, l_ref, v1, s0, s1):
    chunks = [(r[...], None) for r in k_refs]
    with_ones(v1, [r[...] for r in v_refs])

    def q_of(h):
        return q_ref[:, pl.ds(pl.multiple_of(h * HD, HD), HD)]

    def one(h, s_ref, top, stats):
        cols = pl.ds(pl.multiple_of(h * HD, HD), HD)
        state = None if before is None else (before[0][:, cols], lane_of(before[1][...], h))
        o, lse = weigh(s_ref, v1, top, state)
        o_ref[:, cols] = o
        lane = lax.broadcasted_iota(jnp.int32, stats.shape, 1)
        return jnp.where(lane == h, lse, stats)

    def pair(i, carry):
        top, stats = carry
        h = 2 * i
        after = scores(q_of(h + 1), chunks, s1)
        stats = one(h, s0, top, stats)
        top = scores(q_of(jnp.minimum(h + 2, GROUP - 1)), chunks, s0)
        return top, one(h + 1, s1, after, stats)

    first = scores(q_of(0), chunks, s0)
    l_ref[...] = lax.fori_loop(0, GROUP // 2, pair, (first, jnp.zeros(l_ref.shape, F32)))[1]


def state_shapes(rows):
    return [jax.ShapeDtypeStruct((rows, GROUP * HD), F32), jax.ShapeDtypeStruct((rows, HD), F32)]


def heads_scratch(rows, count):
    return [pltpu.VMEM((count, 2 * HD), BF), pltpu.VMEM((rows, count), F32), pltpu.VMEM((rows, count), F32)]


def start_body(idx, q_ref, k_ref, v_ref, o_ref, l_ref, *scratch):
    del idx
    heads_body([k_ref], [v_ref], q_ref, None, o_ref, l_ref, *scratch)


def attend_start(idx, q_all, keys, values):
    rows, count = q_all.shape[0], keys.shape[0]
    whole = lambda shape: pl.BlockSpec(shape, lambda i, idx: (0, 0))
    return pl.pallas_call(
        start_body,
        out_shape=state_shapes(rows),
        grid_spec=pltpu.PrefetchScalarGridSpec(
            num_scalar_prefetch=1,
            grid=(1,),
            in_specs=[
                whole(q_all.shape),
                pl.BlockSpec((count, HD), lambda i, idx: (0, idx[1])),
                pl.BlockSpec((count, HD), lambda i, idx: (0, idx[1])),
            ],
            out_specs=[whole(v.shape) for v in state_shapes(rows)],
            scratch_shapes=heads_scratch(rows, count),
        ),
        compiler_params=params(24),
        name="attend_start",
    )(idx, q_all, keys, values)


def more_body(q_ref, so_ref, sl_ref, b_ref, c_ref, o_ref, l_ref, *scratch):
    n = b_ref.shape[0] // 2
    keys, values = [[r.at[at] for r in (b_ref, c_ref)] for at in (pl.ds(0, n), pl.ds(n, n))]
    heads_body(keys, values, q_ref, (so_ref, sl_ref), o_ref, l_ref, *scratch)


def attend_more(q_all, state, parts):
    rows = q_all.shape[0]
    return pl.pallas_call(
        more_body,
        out_shape=state_shapes(rows),
        scratch_shapes=heads_scratch(rows, parts[0].shape[0]),
        compiler_params=params(24),
        name="attend_more",
    )(q_all, *state, *parts)


def last_body(own, idx, q_ref, so_ref, sl_ref, b_ref, *rest):
    n = b_ref.shape[0] // 2
    chunks, values = [(b_ref[:n, :], None)], [b_ref[n:, :]]
    if own:
        par_ref, sk_ref, sv_ref, o_ref, v1, s0, s1 = rest
        chunks.append((sk_ref[...], visible_rows(par_ref[...])))
        values.append(sv_ref[...])
    else:
        o_ref, v1, s0, s1 = rest
    with_ones(v1, values)
    rows = q_ref.shape[0]
    lane = lax.broadcasted_iota(jnp.int32, (rows, HD), 1)
    stats = jnp.zeros((rows, HD), F32)
    tops = [scores(q_ref[:, h * HD : (h + 1) * HD], chunks, s) for h, s in enumerate((s0, s1))]
    for h, s in enumerate((s0, s1)):
        cols = slice(h * HD, (h + 1) * HD)
        state = so_ref[:, cols], lane_of(sl_ref[...], 2 * idx[0] + h)
        o, lse = weigh(s, v1, tops[h], state)
        o_ref[:rows, cols] = o.astype(BF)
        left = lse
        for part in range(3):
            piece = left.astype(BF).astype(F32)
            left = left - piece
            stats = jnp.where(lane == 3 * h + part, piece, stats)
    o_ref[rows:, :] = stats.T[:16, :].astype(BF)


def attend_last(own, idx, q_all, state, part, extra):
    rows = q_all.shape[0]
    whole = lambda shape: pl.BlockSpec(shape, lambda i, idx: (0, 0))
    pair = pl.BlockSpec((rows, 2 * HD), lambda i, idx: (0, idx[0]))
    specs = [pair, pair, whole((rows, HD)), whole(part.shape)]
    args = [q_all, *state, part]
    count = part.shape[0] // 2
    if own:
        at = GROUP
        specs += [
            whole((rows, 1)),
            pl.BlockSpec((rows, HD), lambda i, idx: (0, at)),
            pl.BlockSpec((rows, HD), lambda i, idx: (0, at + 1)),
        ]
        args += [extra, q_all, q_all]
        count += rows
    return pl.pallas_call(
        lambda *refs: last_body(own, *refs),
        out_shape=jax.ShapeDtypeStruct((rows + 16, 2 * HD), BF),
        grid_spec=pltpu.PrefetchScalarGridSpec(
            num_scalar_prefetch=1,
            grid=(1,),
            in_specs=specs,
            out_specs=whole((rows + 16, 2 * HD)),
            scratch_shapes=heads_scratch(rows, count),
        ),
        compiler_params=params(24),
        name="attend_own" if own else "attend_last",
    )(idx, *args)


def combine(parts, att):
    rows = att.shape[0]
    r = lax.broadcasted_iota(jnp.int32, (rows, rows), 0)
    c = lax.broadcasted_iota(jnp.int32, (rows, rows), 1)
    eye = (r == c).astype(F32).astype(BF)
    stats = [nt(eye, p[rows:, :]) for p in parts]
    for h in range(2):
        at = 3 * h
        lse = [s[:, at : at + 1] + s[:, at + 1 : at + 2] + s[:, at + 2 : at + 3] for s in stats]
        top = jnp.maximum(jnp.maximum(lse[0], lse[1]), jnp.maximum(lse[2], lse[3]))
        w = [jnp.exp2(v - top) for v in lse]
        inv = 1.0 / (w[0] + w[1] + w[2] + w[3])
        cols = slice(h * HD, (h + 1) * HD)
        acc = sum(p[:rows, cols].astype(F32) * (v * inv) for p, v in zip(parts, w))
        att[:, cols] = acc.astype(BF)


def project_body(*refs):
    *parts, w_ref, o_ref, att = refs

    @pl.when(pl.program_id(0) == 0)
    def _():
        combine(parts, att)

    o_ref[...] = mm(att[...], w_ref[...]).astype(BF)


def project(parts, weights, steps=4):
    rows, width = parts[0].shape[0] - 16, weights.shape[1]
    return pl.pallas_call(
        project_body,
        out_shape=pltpu.HBM((rows, width), BF),
        grid=(steps,),
        in_specs=[
            *[pl.BlockSpec(parts[0].shape, lambda i: (0, 0))] * 4,
            pl.BlockSpec((weights.shape[0], width // steps), lambda i: (0, i)),
        ],
        out_specs=pl.BlockSpec((rows, width // steps), lambda i: (0, i)),
        scratch_shapes=[pltpu.VMEM((rows, 2 * HD), BF)],
        compiler_params=params(24),
        name="project",
    )(*parts, weights)


def route_body(p_ref, res_ref, gain_ref, router_ref, hot_ref, sel_ref, pack_ref, mixed_ref, gates_ref, buf, sem):
    rows, width = res_ref.shape
    step = width // CHUNK
    kept = []
    for c in range(CHUNK):
        cols = slice(c * step, (c + 1) * step)
        acc = res_ref[:, cols].astype(F32)
        for j in range(p_ref.shape[0] // rows):
            acc = acc + p_ref[j * rows : (j + 1) * rows, cols].astype(F32)
        mixed_ref[:, cols] = acc
        kept.append(acc)
    square = sum(jnp.sum(a * a, axis=1, keepdims=True) for a in kept)
    inverse = lax.rsqrt(square / width + EPSILON)
    normed = [(a * inverse * gain_ref[:, c * step : (c + 1) * step]).astype(BF) for c, a in enumerate(kept)]
    rows = jnp.concatenate(normed, axis=0)
    pieces = pack_ref.shape[0] // 4
    copies = []
    for j in range(4):
        at = pl.ds(j * pieces, pieces)
        buf[at, :] = mm(sel_ref[at, :], rows).astype(BF)
        copies.append(pltpu.make_async_copy(buf.at[at], pack_ref.at[at], sem.at[j]))
        copies[-1].start()
    logits = sum(mm(n, router_ref[c * step : (c + 1) * step, :]) for c, n in enumerate(normed))
    sig = hot_ref[...] * jax.nn.sigmoid(logits)
    gates_ref[...] = sig / jnp.sum(sig, axis=1, keepdims=True)
    for copy in copies:
        copy.wait()


def route(partial, residual, gain, router, hot, select):
    rows, width = residual.shape
    step = width // CHUNK
    experts = router.shape[1]
    whole = lambda shape: pl.BlockSpec(shape, lambda i: (0, 0))
    args = (partial, residual, gain, router, hot, select)
    return pl.pallas_call(
        route_body,
        out_shape=(
            pltpu.HBM((select.shape[0], step), BF),
            jax.ShapeDtypeStruct((rows, width), F32),
            jax.ShapeDtypeStruct((rows, experts), F32),
        ),
        grid=(1,),
        in_specs=[whole(v.shape) for v in args],
        out_specs=(
            pl.BlockSpec(memory_space=pltpu.HBM),
            whole((rows, width)),
            whole((rows, experts)),
        ),
        scratch_shapes=[pltpu.VMEM((select.shape[0], step), BF), pltpu.SemaphoreType.DMA((4,))],
        compiler_params=params(),
        name="route",
    )(*args)


def shuffle_matrix():
    n = 16 * CAP * CHUNK
    to = lax.broadcasted_iota(jnp.int32, (n, n), 0)
    come = lax.broadcasted_iota(jnp.int32, (n, n), 1)
    tokens = 16 * CAP
    chunk = come % CHUNK
    token = come // CHUNK
    return (to == chunk * tokens + token).astype(F32).astype(BF)


STEPS = 4


def expert_body(perm_ref, back_ref, x_in, g_hbm, u_hbm, d_hbm, o_hbm, x, g, u, d, act, y, out, sems, out_sems):
    block = perm_ref.shape[0]
    tokens = block // CHUNK
    depth = g.shape[1]
    span = d.shape[2]
    count = x_in.shape[0] // block
    fetch = []
    for k in range(STEPS):
        for j, (src, dst) in enumerate(((g_hbm, g), (u_hbm, u))):
            at = pl.ds(k * depth, depth)
            fetch.append(pltpu.make_async_copy(src.at[at, :], dst.at[k], sems.at[2 * k + j]))
    for k in range(STEPS):
        at = pl.ds(k * span, span)
        fetch.append(pltpu.make_async_copy(d_hbm.at[:, at], d.at[k], sems.at[2 * STEPS + k]))
    for copy in fetch:
        copy.start()
    step = x_in.shape[1]
    for b in range(count):
        z = mm(perm_ref[...], x_in[b * block : (b + 1) * block, :]).astype(BF)
        for c in range(CHUNK):
            x[b * tokens : (b + 1) * tokens, c * step : (c + 1) * step] = z[c * tokens : (c + 1) * tokens, :]
    gate = up = None
    for k in range(STEPS):
        piece = x[:, k * depth : (k + 1) * depth]
        fetch[2 * k].wait()
        part = mm(piece, g[k])
        gate = part if gate is None else gate + part
        fetch[2 * k + 1].wait()
        part = mm(piece, u[k])
        up = part if up is None else up + part
    act[...] = (jax.nn.silu(gate) * up).astype(BF)
    for k in range(STEPS):
        fetch[2 * STEPS + k].wait()
        y[:, k * span : (k + 1) * span] = mm(act[...], d[k]).astype(BF)
    sends = []
    for b in range(count):
        rows = slice(b * tokens, (b + 1) * tokens)
        z = jnp.concatenate([y[rows, c * step : (c + 1) * step] for c in range(CHUNK)], axis=0)
        at = pl.ds(b * block, block)
        out[at, :] = mm(back_ref[...], z).astype(BF)
        sends.append(pltpu.make_async_copy(out.at[at], o_hbm.at[at], out_sems.at[b]))
        sends[-1].start()
    for copy in sends:
        copy.wait()


def expert(arrived, perm, back, gate_w, up_w, down_w):
    width, hidden = gate_w.shape
    total, step = arrived.shape
    tokens = total // CHUNK
    blocks = total // perm.shape[0]
    whole = lambda shape: pl.BlockSpec(shape, lambda i: (0, 0))
    hbm = pl.BlockSpec(memory_space=pltpu.HBM)
    return pl.pallas_call(
        expert_body,
        out_shape=pltpu.HBM(arrived.shape, BF),
        grid=(1,),
        in_specs=[whole(perm.shape), whole(back.shape), whole(arrived.shape), hbm, hbm, hbm],
        out_specs=hbm,
        scratch_shapes=[
            pltpu.VMEM((tokens, width), BF),
            pltpu.VMEM((STEPS, width // STEPS, hidden), BF),
            pltpu.VMEM((STEPS, width // STEPS, hidden), BF),
            pltpu.VMEM((STEPS, hidden, width // STEPS), BF),
            pltpu.VMEM((tokens, hidden), BF),
            pltpu.VMEM((tokens, width), BF),
            pltpu.VMEM((total, step), BF),
            pltpu.SemaphoreType.DMA((3 * STEPS,)),
            pltpu.SemaphoreType.DMA((blocks,)),
        ],
        compiler_params=params(),
        name="expert",
    )(perm, back, arrived, gate_w, up_w, down_w)


def finish_body(ret_ref, mask_ref, gates_ref, mixed_ref, o_ref):
    rows, experts = gates_ref.shape
    span = ret_ref.shape[0]
    step = ret_ref.shape[1]
    e = lax.broadcasted_iota(jnp.int32, (experts, span), 0)
    at = lax.broadcasted_iota(jnp.int32, (experts, span), 1)
    spread = (e == at // (span // experts)).astype(F32).astype(BF)
    high, low = hi_lo(gates_ref[...])
    wide = mm(high, spread) + mm(low, spread)
    weights = jnp.concatenate([wide] * CHUNK, axis=0) * mask_ref[...].astype(F32)
    high, low = hi_lo(weights)
    moe = mm(high, ret_ref[...]) + mm(low, ret_ref[...])
    for c in range(CHUNK):
        cols = slice(c * step, (c + 1) * step)
        o_ref[:, cols] = (mixed_ref[:, cols] + moe[c * rows : (c + 1) * rows, :]).astype(BF)


def finish(returned, mask, gates, mixed):
    return pl.pallas_call(
        finish_body,
        out_shape=jax.ShapeDtypeStruct(mixed.shape, BF),
        compiler_params=params(),
        name="finish",
    )(returned, mask, gates, mixed)


def ready_body(q_ref, k_ref, v_ref, o_ref):
    rows, side = q_ref.shape[0], KVH
    across = o_ref.shape[0] // rows // side
    wide = q_ref.shape[1] // side
    for z in range(side):
        for x in range(across):
            at = slice((z * across + x) * rows, (z * across + x + 1) * rows)
            o_ref[at, :wide] = q_ref[:, z * wide : (z + 1) * wide]
            o_ref[at, wide : wide + HD] = k_ref[:, z * HD : (z + 1) * HD]
            o_ref[at, wide + HD :] = v_ref[:, z * HD : (z + 1) * HD]


def ready(q, k, v, devices):
    rows = q.shape[0]
    return pl.pallas_call(
        ready_body,
        out_shape=pltpu.HBM((devices * rows, (GROUP + 2) * HD), BF),
        compiler_params=params(24),
        name="ready",
    )(q, k, v)


def local(
    queries,
    prefix_keys,
    prefix_values,
    suffix_keys,
    suffix_values,
    parents,
    out_proj,
    residual,
    norm_gain,
    router,
    routes,
    expert_gate,
    expert_up,
    expert_down,
):
    seq_count = lax.axis_size("seq")
    side = KVH
    across = seq_count // side
    s = lax.axis_index("seq")
    z, x = s // across, s % across
    q, sk, sv = queries[0], suffix_keys[0], suffix_values[0]
    rows = q.shape[0]
    keys, values = prefix_keys[0], prefix_values[0]
    copies = ready(q, sk, sv, seq_count)
    parts = []
    for d in (1, 3, 2):
        head = (z + d) % side
        piece = jnp.concatenate(
            [lax.dynamic_slice_in_dim(a, head * HD, HD, 1) for a in (keys, values)], axis=0
        )
        parts.append(lax.ppermute(piece, "seq", [(i, (i + d * across) % seq_count) for i in range(seq_count)]))
    q_all = lax.all_to_all(copies.reshape(seq_count, rows, -1), "seq", 0, 0, tiled=True).reshape(copies.shape)
    place = jnp.stack([x, z]).astype(jnp.int32)
    state = attend_start(place, q_all, keys, values)
    state = attend_more(q_all, state, parts[:2])
    along_x = lambda a, d: lax.ppermute(
        a, "seq", [(i, i // across * across + (i + d) % across) for i in range(seq_count)]
    )
    blocks = []
    for d in (2, 1, 3, 0):
        idx = jnp.stack([(x + d) % across, z]).astype(jnp.int32)
        block = attend_last(d == 0, idx, q_all, state, parts[2], parents[0][:, None])
        blocks.append(along_x(block, d) if d else block)
    projected = project(blocks, out_proj)
    arrived = lax.all_to_all(
        projected.reshape(seq_count, rows, -1), "seq", 0, 0, tiled=True
    ).reshape(projected.shape)
    experts = router.shape[1]
    ids = routes[0]
    hot = jnp.any(ids[:, :, None] == jnp.arange(experts, dtype=jnp.int32), axis=1)
    before = jnp.cumsum(hot.astype(jnp.int32), axis=0) - hot
    slots = hot[:, :, None] & (before[:, :, None] == jnp.arange(CAP, dtype=jnp.int32))
    same = jnp.eye(CHUNK, dtype=jnp.bool_)
    mask = slots[None, :, :, :, None] & same[:, None, None, None, :]
    mask = mask.reshape(CHUNK * rows, experts * CAP * CHUNK).astype(BF)
    chosen = jnp.moveaxis(slots, 0, 2)
    select = chosen[:, :, None, None, :] & same[None, None, :, :, None]
    select = select.reshape(experts * CAP * CHUNK, CHUNK * rows).astype(BF)
    packed, mixed, gates = route(arrived, residual[0], norm_gain[None, :], router, hot.astype(F32), select)
    exchange = lambda a: lax.all_to_all(
        a.reshape(experts, CAP * CHUNK, -1), ("seq", "grp"), 0, 0, tiled=True
    ).reshape(a.shape)
    order = shuffle_matrix()
    finished = expert(exchange(packed), order, order.T, expert_gate[0], expert_up[0], expert_down[0])
    return finish(exchange(finished), mask, gates, mixed)[None]


def solution(mesh):
    rows = P("grp", "seq", None)
    spread = P(("seq", "grp"), None, None)
    in_specs = (
        rows, rows, rows, rows, rows, P("grp", None), P("seq", None), rows, P(), P(), rows, spread, spread, spread,
    )
    return jax.shard_map(local, mesh=mesh, in_specs=in_specs, out_specs=rows, check_vma=False)
```

time: 207 us -> 192 us (0.928)
  starting transfers between devices: 35.6 us -> 48.7 us
  waiting for transfers between devices: 90.1 us -> 77.8 us
  Pallas kernels: 50.7 us -> 40.5 us
  local copies, waits for them, and re-layouts: 18.3 us -> 13.9 us
    ppermute x3, waiting for transfers between devices: 19.5 us -> 0.01 us  [local(): lax.ppermute(piece, 'seq', [(i, (i + d * across) % seq_count) for i in ra...]
    pallas_call x7 -> x10, Pallas kernels: 49.2 us -> 38.9 us  [the longest x1 11.7 us: expert(): pl.pallas_call(expert_body, out_shape=pltpu.HBM(arrived.shape, BF), grid=...]
    all_to_all x1, waiting for transfers between devices: 0.01 us -> 10.1 us  [local(): lax.all_to_all(copies.reshape(seq_count, rows, -1), 'seq', 0, 0, tiled=True)]
    ppermute x3, starting transfers between devices: 4.03 us -> 11.1 us  [local(): lax.ppermute(a, 'seq', [(i, i // across * across + (i + d) % across) for...]
    all_to_all x1, waiting for transfers between devices: 19.5 us -> 15.6 us  [local(): lax.all_to_all(projected.reshape(seq_count, rows, -1), 'seq', 0, 0, tiled...]
    all_to_all x2, starting transfers between devices: 13.1 us -> 16.1 us  [local(): lax.all_to_all(a.reshape(experts, CAP * CHUNK, -1), ('seq', 'grp'), 0, 0,...]
    unnamed x26 -> x22, local copies, waits for them, and re-layouts: 3.94 us -> 1.27 us
  transfers between devices with their start and end apart: 10 -> 10, of which waited for: 6 -> 5; matrix products, arithmetic and copies ran while one was open for 11% -> 11% of each run, Pallas kernels for 10% -> 10%
where the time goes in v2:
time: 192 us; the launch traced here: 191 us
  waiting for transfers between devices  77.8 us (41%)
  starting transfers between devices  48.7 us (25%)
  Pallas kernels  40.5 us (21%)
  local copies, waits for them, and re-layouts  13.9 us (7%)
  other arithmetic  10.2 us (5%)
    all_to_all x2, waiting for transfers between devices, local(): lax.all_to_all(a.reshape(experts, CAP * CHUNK, -1), ('seq', 'grp'), 0, 0,...  51 us
    all_to_all x2, starting transfers between devices, local(): lax.all_to_all(a.reshape(experts, CAP * CHUNK, -1), ('seq', 'grp'), 0, 0,...  16.1 us
    all_to_all x1, waiting for transfers between devices, local(): lax.all_to_all(projected.reshape(seq_count, rows, -1), 'seq', 0, 0, tiled...  15.6 us
    pallas_call x1, Pallas kernels, expert(): pl.pallas_call(expert_body, out_shape=pltpu.HBM(arrived.shape, BF), grid=...  11.7 us
    ppermute x3, starting transfers between devices, local(): lax.ppermute(a, 'seq', [(i, i // across * across + (i + d) % across) for...  11.1 us
    all_to_all x1, waiting for transfers between devices, local(): lax.all_to_all(copies.reshape(seq_count, rows, -1), 'seq', 0, 0, tiled=True)  10.1 us
    pallas_call x1, Pallas kernels, attend_more(): pl.pallas_call(more_body, out_shape=state_shapes(rows), scratch_shapes=he...  8.3 us
    all_to_all x1, starting transfers between devices, local(): lax.all_to_all(projected.reshape(seq_count, rows, -1), 'seq', 0, 0, tiled...  7.47 us
  transfers between devices with their start and end apart: 10, of which 5 were waited for; matrix products, arithmetic and copies ran while one was open for 11% of the time, Pallas kernels for 10%

profile of v2, /device:TPU:1, one launch (start us, length us, event | category | flops | bytes accessed | tf_op | source)
XLA Modules:
  0.0 191.3 jit_solution(17215502209579730835)
XLA Ops:
  0.0 1.5 dynamic-slice_bitcast_fusion
  1.5 0.8 pad_maximum_fusion.1
  2.4 4.6 %collective-permute-start.1 = (bf16[2048,128]{1,0:T(8,128)(2,1)}, bf16[2048,128]{1,0:T(8,128)(2,1)}, u32[]{:S(2)}, u32[]{:S(2)}) collective-permute-start(bf16[2048,128]{1,0:T(8,128)(2,1)} %pad_maximum_fusion.1), channel_id=1, source_target_pairs={{0,96},{8,104},{16,112},{24,120},{32,0},{40,8},{48,16},{56,24},{64... | collective-permute-start | bytes 1572872 | tf_op jit(solution)/shard_map/ppermute | solution.py:498
  7.0 0.8 pad_maximum_fusion
  7.8 0.0 collective-permute-start
  7.8 0.0 copy-done.4
  7.8 0.0 copy-done.7
  7.8 0.0 copy-done.8
  7.8 0.9 ready.1
  8.7 6.5 %all-to-all-start = ((bf16[16,16,1280]{2,1,0:T(8,128)(2,1)}), bf16[16,16,1280]{2,1,0:T(8,128)(2,1)S(1)}, u32[]{:S(2)}, u32[]{:S(2)}) async-start(bf16[16,16,1280]{2,1,0:T(8,128)(2,1)} %bitcast.72), calls=%async_computation | async-start | bytes 1310720 | tf_op jit(solution)/shard_map/all_to_all | solution.py:499
  15.2 0.8 pad_maximum_fusion.2
  16.0 2.9 %collective-permute-start.2 = (bf16[2048,128]{1,0:T(8,128)(2,1)}, bf16[2048,128]{1,0:T(8,128)(2,1)S(1)}, u32[]{:S(2)}, u32[]{:S(2)}) collective-permute-start(bf16[2048,128]{1,0:T(8,128)(2,1)} %pad_maximum_fusion.2), channel_id=1, source_target_pairs={{0,64},{8,72},{16,80},{24,88},{32,96},{40,104},{48,112},{56,120},{... | collective-permute-start | bytes 1572872 | tf_op jit(solution)/shard_map/ppermute | solution.py:498
  18.9 0.1 pad_add_fusion.1.idx
  19.0 0.1 pad_add_fusion.3.refs_0_
  19.1 0.1 pad_add_fusion.2.refs_0_
  19.1 0.1 pad_add_fusion.refs_0_
  19.2 10.1 %all-to-all-done = bf16[16,16,1280]{2,1,0:T(8,128)(2,1)S(1)} async-done(((bf16[16,16,1280]{2,1,0:T(8,128)(2,1)}), bf16[16,16,1280]{2,1,0:T(8,128)(2,1)S(1)}, u32[]{:S(2)}, u32[]{:S(2)}) %all-to-all-start) | async-done | bytes 655392 | tf_op jit(solution)/shard_map/all_to_all | solution.py:499
  29.4 0.0 copy-done
  29.4 0.0 copy-done.1
  29.4 5.0 %attend_start.1 = (f32[256,1024]{1,0:T(8,128)S(1)}, f32[256,128]{1,0:T(8,128)S(1)}) custom-call(s32[2]{0:T(128)S(1)} %pad_add_fusion.1.idx, bf16[256,1280]{1,0:T(8,128)(2,1)S(1)} %bitcast.49, bf16[1024,512]{1,0:T(8,128)(2,1)S(1)} %bitcast.60, bf16[1024,512]{1,0:T(8,128)(2,1)S(1)} %bitcast.61), custom_call_target="tpu_custom_call" | custom-call | tf_op jit(solution)/shard_map/attend_start/pallas_call | solution.py:138
  34.4 0.0 collective-permute-done.1.c_ref
  34.4 0.0 collective-permute-done.b_ref
  34.4 8.3 %attend_more.1 = (f32[256,1024]{1,0:T(8,128)S(1)}, f32[256,128]{1,0:T(8,128)S(1)}) custom-call(bf16[256,1280]{1,0:T(8,128)(2,1)S(1)} %bitcast.50, f32[256,1024]{1,0:T(8,128)S(1)} %get-tuple-element.12.so_ref, f32[256,128]{1,0:T(8,128)S(1)} %get-tuple-element.13.sl_ref, bf16[2048,128]{1,0:T(8,128)(2,1)} %collective-permute-done.b_ref, ...), custom_call_target="tpu_custom_call" | custom-call | tf_op jit(solution)/shard_map/attend_more/pallas_call | solution.py:165
  42.7 0.0 collective-permute-done.2.refs_4_
  42.7 1.7 attend_last.5
  44.4 9.2 %collective-permute-start.5 = (bf16[272,256]{1,0:T(8,128)(2,1)S(1)}, bf16[272,256]{1,0:T(8,128)(2,1)S(1)}, u32[]{:S(2)}, u32[]{:S(2)}) collective-permute-start(bf16[272,256]{1,0:T(8,128)(2,1)S(1)} %attend_last.5), channel_id=1, source_target_pairs={{0,24},{8,0},{16,8},{24,16},{32,56},{40,32},{48,40},{56,48},{64,88... | collective-permute-start | bytes 417800 | tf_op jit(solution)/shard_map/ppermute | solution.py:503
  53.5 1.7 attend_last.4
  55.2 0.0 collective-permute-start.4
  55.3 1.7 attend_last.3
  56.9 1.9 %collective-permute-start.3 = (bf16[272,256]{1,0:T(8,128)(2,1)S(1)}, bf16[272,256]{1,0:T(8,128)(2,1)S(1)}, u32[]{:S(2)}, u32[]{:S(2)}) collective-permute-start(bf16[272,256]{1,0:T(8,128)(2,1)S(1)} %attend_last.3), channel_id=1, source_target_pairs={{0,16},{8,24},{16,0},{24,8},{32,48},{40,56},{48,32},{56,40},{64,80... | collective-permute-start | bytes 417800 | tf_op jit(solution)/shard_map/ppermute | solution.py:503
  58.9 0.1 copy.26.refs_5_
  59.0 0.0 copy-start.2
  59.1 0.1 pad_add_fusion.4.refs_0_
  59.1 2.4 %attend_own.1.refs_3_ = bf16[272,256]{1,0:T(8,128)(2,1)S(1)} custom-call(s32[2]{0:T(128)S(1)} %pad_add_fusion.4.refs_0_, bf16[256,1280]{1,0:T(8,128)(2,1)S(1)} %bitcast.54, f32[256,1024]{1,0:T(8,128)S(1)} %get-tuple-element.14.refs_2_, f32[256,128]{1,0:T(8,128)S(1)} %get-tuple-element.15.refs_3_, bf16[2048,128]{1,0:T(8,128)(2,1)S(1)} %collective-permute-done.2.refs_4_, ...), custom_call_target="tpu_custom_call" | custom-call | tf_op jit(solution)/shard_map/attend_own/pallas_call | solution.py:217
  61.6 0.0 collective-permute-done.5.refs_2_
  61.6 0.0 collective-permute-done.4.refs_1_
  61.6 1.0 collective-permute-done.3.refs_0_
  62.6 0.0 copy-done.2
  62.6 3.5 %project.1 = bf16[256,4096]{1,0:T(8,128)(2,1)} custom-call(bf16[272,256]{1,0:T(8,128)(2,1)S(1)} %collective-permute-done.3.refs_0_, bf16[272,256]{1,0:T(8,128)(2,1)S(1)} %collective-permute-done.4.refs_1_, bf16[272,256]{1,0:T(8,128)(2,1)S(1)} %collective-permute-done.5.refs_2_, bf16[272,256]{1,0:T(8,128)(2,1)S(1)} %attend_own.1.refs_3_, ...), custom_call_target="tpu_custom_call" | custom-call | tf_op jit(solution)/shard_map/project/pallas_call | solution.py:261
  66.1 7.5 %all-to-all-start.1 = ((bf16[16,16,4096]{2,1,0:T(8,128)(2,1)}), bf16[16,16,4096]{2,1,0:T(8,128)(2,1)S(1)}, u32[]{:S(2)}, u32[]{:S(2)}) async-start(bf16[16,16,4096]{2,1,0:T(8,128)(2,1)} %bitcast.68), calls=%async_computation.1 | async-start | bytes 4194304 | tf_op jit(solution)/shard_map/all_to_all | solution.py:512
  73.6 0.1 copy.27
  73.7 0.1 fusion
  73.9 0.1 copy.29
  74.0 0.1 copy.28
  74.1 0.1 copy.30
  74.2 0.1 compare_and_fusion.1
  74.3 3.3 %and_convert_fusion.1 = bf16[128,2,8,8,16]{4,3,2,1,0:T(8,128)(2,1)} fusion(pred[8,8]{1,0:T(8,128)(4,1)S(1)} %copy.30, pred[128,2,16]{2,1,0:T(4,128)(4,1)S(1)} %compare_and_fusion.1), kind=kLoop, calls=%fused_computation.1 | loop fusion | flops 524288 | bytes 528448 | tf_op jit(solution)/shard_map/convert_element_type | solution.py:525
  77.6 5.1 %reshape.90.sel_ref = bf16[2048,128]{1,0:T(8,128)(2,1)S(1)} reshape(bf16[128,2,8,8,16]{4,3,2,1,0:T(8,128)(2,1)} %and_convert_fusion.1) | data formatting | bytes 1048576 | tf_op jit(solution)/shard_map/convert_element_type | solution.py:525
  82.7 15.6 %all-to-all-done.1 = bf16[16,16,4096]{2,1,0:T(8,128)(2,1)S(1)} async-done(((bf16[16,16,4096]{2,1,0:T(8,128)(2,1)}), bf16[16,16,4096]{2,1,0:T(8,128)(2,1)S(1)}, u32[]{:S(2)}, u32[]{:S(2)}) %all-to-all-start.1) | async-done | bytes 2097184 | tf_op jit(solution)/shard_map/all_to_all | solution.py:512
  98.3 1.2 copy-done.3
  99.6 2.0 %route.1 = (bf16[2048,512]{1,0:T(8,128)(2,1)}, f32[16,4096]{1,0:T(8,128)S(1)}, f32[16,128]{1,0:T(8,128)S(1)}) custom-call(bf16[256,4096]{1,0:T(8,128)(2,1)S(1)} %bitcast.58, bf16[16,4096]{1,0:T(8,128)(2,1)S(1)} %bitcast.63, f32[1,4096]{1,0:T(1,128)S(1)} %bitcast.64, bf16[4096,128]{1,0:T(8,128)(2,1)S(1)} %copy-done.3, ...), custom_call_target="tpu_custom_call" | custom-call | tf_op jit(solution)/shard_map/route/pallas_call | solution.py:311
  101.6 11.4 %all-to-all-start.2 = ((bf16[128,16,512]{2,1,0:T(8,128)(2,1)}), bf16[128,16,512]{2,1,0:T(8,128)(2,1)S(1)}, u32[]{:S(2)}, u32[]{:S(2)}) async-start(bf16[128,16,512]{2,1,0:T(8,128)(2,1)} %bitcast.73), calls=%async_computation.2 | async-start | bytes 4194304 | tf_op jit(solution)/shard_map/all_to_all | solution.py:527
  113.0 0.3 convert_convert_fusion
  113.3 29.8 %all-to-all-done.2 = bf16[128,16,512]{2,1,0:T(8,128)(2,1)S(1)} async-done(((bf16[128,16,512]{2,1,0:T(8,128)(2,1)}), bf16[128,16,512]{2,1,0:T(8,128)(2,1)S(1)}, u32[]{:S(2)}, u32[]{:S(2)}) %all-to-all-start.2) | async-done | bytes 2097184 | tf_op jit(solution)/shard_map/all_to_all | solution.py:527
  143.1 11.7 %expert.1 = bf16[2048,512]{1,0:T(8,128)(2,1)} custom-call(bf16[256,256]{1,0:T(8,128)(2,1)S(1)} %get-tuple-element.26.perm_ref, bf16[256,256]{1,0:T(8,128)(2,1)S(1)} %get-tuple-element.25.back_ref, bf16[2048,512]{1,0:T(8,128)(2,1)S(1)} %bitcast.57, bf16[4096,768]{1,0:T(8,128)(2,1)} %bitcast.69, bf16[4096,768]{1,0:T(8,128)(2,1)} %bitcast.70, ...), custom_call_target="tpu_custom_call" | custom-call | tf_op jit(solution)/shard_map/expert/pallas_call | solution.py:397
  154.8 4.8 %all-to-all-start.3 = ((bf16[128,16,512]{2,1,0:T(8,128)(2,1)}), bf16[128,16,512]{2,1,0:T(8,128)(2,1)S(1)}, u32[]{:S(2)}, u32[]{:S(2)}) async-start(bf16[128,16,512]{2,1,0:T(8,128)(2,1)} %bitcast.67), calls=%async_computation.3 | async-start | bytes 4194304 | tf_op jit(solution)/shard_map/all_to_all | solution.py:527
  159.5 0.1 copy.31
  159.7 0.1 copy.32
  159.8 0.1 compare_and_fusion
  159.9 3.3 %and_convert_fusion = bf16[8,16,128,2,8]{1,0,4,3,2:T(8,128)(2,1)} fusion(pred[8,8]{0,1:T(8,128)(4,1)S(1)} %iota_compare_fusion.1, pred[16,128,2]{0,2,1:T(4,128)(4,1)S(1)} %compare_and_fusion), kind=kLoop, calls=%fused_computation | loop fusion | flops 524288 | bytes 528448 | tf_op jit(solution)/shard_map/convert_element_type | solution.py:522
  163.2 5.1 %reshape.91 = bf16[128,2048]{0,1:T(8,128)(2,1)S(1)} reshape(bf16[8,16,128,2,8]{1,0,4,3,2:T(8,128)(2,1)} %and_convert_fusion) | data formatting | bytes 1048576 | tf_op jit(solution)/shard_map/convert_element_type | solution.py:522
  168.3 0.2 copy.33.mask_ref
  168.5 21.3 %all-to-all-done.3 = bf16[128,16,512]{2,1,0:T(8,128)(2,1)S(1)} async-done(((bf16[128,16,512]{2,1,0:T(8,128)(2,1)}), bf16[128,16,512]{2,1,0:T(8,128)(2,1)S(1)}, u32[]{:S(2)}, u32[]{:S(2)}) %all-to-all-start.3) | async-done | bytes 2097184 | tf_op jit(solution)/shard_map/all_to_all | solution.py:527
  189.8 1.6 finish.1
  (22 shorter events, 0.1 us)
Async XLA Ops:
  0.0 7.8 %copy-start.4 = (bf16[1,16,4096]{2,1,0:T(8,128)(2,1)S(1)}, bf16[1,16,4096]{2,1,0:T(8,128)(2,1)}, u32[]{:S(2)}) copy-start(bf16[1,16,4096]{2,1,0:T(8,128)(2,1)} %param.14) | copy-start | bytes 393220
  0.0 7.8 %copy-start.7 = (bf16[1,16,512]{2,1,0:T(8,128)(2,1)S(1)}, bf16[1,16,512]{2,1,0:T(8,128)(2,1)}, u32[]{:S(2)}) copy-start(bf16[1,16,512]{2,1,0:T(8,128)(2,1)} %param.17) | copy-start | bytes 49156
  0.0 7.8 %copy-start.8 = (bf16[1,16,512]{2,1,0:T(8,128)(2,1)S(1)}, bf16[1,16,512]{2,1,0:T(8,128)(2,1)}, u32[]{:S(2)}) copy-start(bf16[1,16,512]{2,1,0:T(8,128)(2,1)} %param.18) | copy-start | bytes 49156
  2.4 32.0 %collective-permute-start.1 = (bf16[2048,128]{1,0:T(8,128)(2,1)}, bf16[2048,128]{1,0:T(8,128)(2,1)}, u32[]{:S(2)}, u32[]{:S(2)}) collective-permute-start(bf16[2048,128]{1,0:T(8,128)(2,1)} %pad_maximum_fusion.1), channel_id=1, source_target_pairs={{0,96},{8,104},{16,112},{24,120},{32,0},{40,8},{48,16},{56,24},{64... | collective-permute-start | bytes 1572872 | tf_op jit(solution)/shard_map/ppermute | solution.py:498
  6.9 22.4 %copy-start = (bf16[1,1024,512]{2,1,0:T(8,128)(2,1)S(1)}, bf16[1,1024,512]{2,1,0:T(8,128)(2,1)}, u32[]{:S(2)}) copy-start(bf16[1,1024,512]{2,1,0:T(8,128)(2,1)} %param.15) | copy-start | bytes 3145732
  7.0 22.4 %copy-start.1 = (bf16[1,1024,512]{2,1,0:T(8,128)(2,1)S(1)}, bf16[1,1024,512]{2,1,0:T(8,128)(2,1)}, u32[]{:S(2)}) copy-start(bf16[1,1024,512]{2,1,0:T(8,128)(2,1)} %param.16) | copy-start | bytes 3145732
  7.8 26.6 %collective-permute-start = (bf16[2048,128]{1,0:T(8,128)(2,1)}, bf16[2048,128]{1,0:T(8,128)(2,1)}, u32[]{:S(2)}, u32[]{:S(2)}) collective-permute-start(bf16[2048,128]{1,0:T(8,128)(2,1)} %pad_maximum_fusion), channel_id=1, source_target_pairs={{0,32},{8,40},{16,48},{24,56},{32,64},{40,72},{48,80},{56,88},{64,... | collective-permute-start | bytes 1572872 | tf_op jit(solution)/shard_map/ppermute | solution.py:498
  8.7 20.6 %all-to-all-start = ((bf16[16,16,1280]{2,1,0:T(8,128)(2,1)}), bf16[16,16,1280]{2,1,0:T(8,128)(2,1)S(1)}, u32[]{:S(2)}, u32[]{:S(2)}) async-start(bf16[16,16,1280]{2,1,0:T(8,128)(2,1)} %bitcast.72), calls=%async_computation | async-start | bytes 1310720 | tf_op jit(solution)/shard_map/all_to_all | solution.py:499
  16.0 26.6 %collective-permute-start.2 = (bf16[2048,128]{1,0:T(8,128)(2,1)}, bf16[2048,128]{1,0:T(8,128)(2,1)S(1)}, u32[]{:S(2)}, u32[]{:S(2)}) collective-permute-start(bf16[2048,128]{1,0:T(8,128)(2,1)} %pad_maximum_fusion.2), channel_id=1, source_target_pairs={{0,64},{8,72},{16,80},{24,88},{32,96},{40,104},{48,112},{56,120},{... | collective-permute-start | bytes 1572872 | tf_op jit(solution)/shard_map/ppermute | solution.py:498
  44.4 14.5 %copy-start.10 = (s32[1,256]{1,0:T(1,128)S(1)}, s32[1,256]{1,0:T(1,128)}, u32[]{:S(2)}) copy-start(s32[1,256]{1,0:T(1,128)} %param.19) | copy-start | bytes 3076
  44.4 17.2 %collective-permute-start.5 = (bf16[272,256]{1,0:T(8,128)(2,1)S(1)}, bf16[272,256]{1,0:T(8,128)(2,1)S(1)}, u32[]{:S(2)}, u32[]{:S(2)}) collective-permute-start(bf16[272,256]{1,0:T(8,128)(2,1)S(1)} %attend_last.5), channel_id=1, source_target_pairs={{0,24},{8,0},{16,8},{24,16},{32,56},{40,32},{48,40},{56,48},{64,88... | collective-permute-start | bytes 417800 | tf_op jit(solution)/shard_map/ppermute | solution.py:503
  55.2 6.3 %collective-permute-start.4 = (bf16[272,256]{1,0:T(8,128)(2,1)S(1)}, bf16[272,256]{1,0:T(8,128)(2,1)S(1)}, u32[]{:S(2)}, u32[]{:S(2)}) collective-permute-start(bf16[272,256]{1,0:T(8,128)(2,1)S(1)} %attend_last.4), channel_id=1, source_target_pairs={{0,8},{8,16},{16,24},{24,0},{32,40},{40,48},{48,56},{56,32},{64,72... | collective-permute-start | bytes 417800 | tf_op jit(solution)/shard_map/ppermute | solution.py:503
  56.9 5.6 %collective-permute-start.3 = (bf16[272,256]{1,0:T(8,128)(2,1)S(1)}, bf16[272,256]{1,0:T(8,128)(2,1)S(1)}, u32[]{:S(2)}, u32[]{:S(2)}) collective-permute-start(bf16[272,256]{1,0:T(8,128)(2,1)S(1)} %attend_last.3), channel_id=1, source_target_pairs={{0,16},{8,24},{16,0},{24,8},{32,48},{40,56},{48,32},{56,40},{64,80... | collective-permute-start | bytes 417800 | tf_op jit(solution)/shard_map/ppermute | solution.py:503
  59.0 3.5 %copy-start.2 = (bf16[256,4096]{1,0:T(8,128)(2,1)S(1)}, bf16[256,4096]{1,0:T(8,128)(2,1)}, u32[]{:S(2)}) copy-start(bf16[256,4096]{1,0:T(8,128)(2,1)} %refs_4_.1) | copy-start | bytes 6291460
  66.1 7.5 %copy-start.9 = (s32[1,16,8]{1,2,0:T(8,128)S(1)}, s32[1,16,8]{1,2,0:T(8,128)}, u32[]{:S(2)}) copy-start(s32[1,16,8]{1,2,0:T(8,128)} %param.24) | copy-start | bytes 1540
  66.1 32.2 %all-to-all-start.1 = ((bf16[16,16,4096]{2,1,0:T(8,128)(2,1)}), bf16[16,16,4096]{2,1,0:T(8,128)(2,1)S(1)}, u32[]{:S(2)}, u32[]{:S(2)}) async-start(bf16[16,16,4096]{2,1,0:T(8,128)(2,1)} %bitcast.68), calls=%async_computation.1 | async-start | bytes 4194304 | tf_op jit(solution)/shard_map/all_to_all | solution.py:512
  77.6 20.7 %copy-start.5 = (bf16[1,16,4096]{2,1,0:T(8,128)(2,1)S(1)}, bf16[1,16,4096]{2,1,0:T(8,128)(2,1)}, u32[]{:S(2)}) copy-start(bf16[1,16,4096]{2,1,0:T(8,128)(2,1)} %param.21) | copy-start | bytes 393220
  77.6 20.7 %copy-start.6 = (f32[4096]{0:T(1024)S(1)}, f32[4096]{0:T(1024)}, u32[]{:S(2)}) copy-start(f32[4096]{0:T(1024)} %param.22) | copy-start | bytes 49156
  98.3 1.2 copy-start.3
  101.6 41.5 %all-to-all-start.2 = ((bf16[128,16,512]{2,1,0:T(8,128)(2,1)}), bf16[128,16,512]{2,1,0:T(8,128)(2,1)S(1)}, u32[]{:S(2)}, u32[]{:S(2)}) async-start(bf16[128,16,512]{2,1,0:T(8,128)(2,1)} %bitcast.73), calls=%async_computation.2 | async-start | bytes 4194304 | tf_op jit(solution)/shard_map/all_to_all | solution.py:527
  154.8 35.0 %all-to-all-start.3 = ((bf16[128,16,512]{2,1,0:T(8,128)(2,1)}), bf16[128,16,512]{2,1,0:T(8,128)(2,1)S(1)}, u32[]{:S(2)}, u32[]{:S(2)}) async-start(bf16[128,16,512]{2,1,0:T(8,128)(2,1)} %bitcast.67), calls=%async_computation.3 | async-start | bytes 4194304 | tf_op jit(solution)/shard_map/all_to_all | solution.py:527

commit v3 on v2

--- a/solution.py
+++ b/solution.py
@@ -7,10 +7,10 @@
 from jax.experimental.pallas import tpu as pltpu
 from jax.sharding import PartitionSpec as P
 
+
 HEADS = 32
 KVH = 4
 HD = 128
-DEPTH = 8
 EPSILON = 1e-06
 GROUP = HEADS // KVH
 C2 = HD ** (-0.5) * math.log2(math.e)
@@ -116,7 +116,7 @@
         return top, one(h + 1, s1, after, stats)
 
     first = scores(q_of(0), chunks, s0)
-    l_ref[...] = lax.fori_loop(0, GROUP // 2, pair, (first, jnp.zeros(l_ref.shape, F32)))[1]
+    l_ref[...] = lax.fori_loop(0, GROUP // 2, pair, (first, jnp.zeros(l_ref.shape, F32)), unroll=2)[1]
 
 
 def state_shapes(rows):
@@ -273,7 +273,9 @@
     )(*parts, weights)
 
 
-def route_body(p_ref, res_ref, gain_ref, router_ref, hot_ref, sel_ref, pack_ref, mixed_ref, gates_ref, buf, sem):
+def route_body(p_ref, res_ref, gain_ref, router_ref, hot_ref, sel_ref, pack_ref, mixed_ref, gates_ref, buf, router_buf, sem):
+    fetch = pltpu.make_async_copy(router_ref, router_buf, sem.at[4])
+    fetch.start()
     rows, width = res_ref.shape
     step = width // CHUNK
     kept = []
@@ -295,7 +297,8 @@
         buf[at, :] = mm(sel_ref[at, :], rows).astype(BF)
         copies.append(pltpu.make_async_copy(buf.at[at], pack_ref.at[at], sem.at[j]))
         copies[-1].start()
-    logits = sum(mm(n, router_ref[c * step : (c + 1) * step, :]) for c, n in enumerate(normed))
+    fetch.wait()
+    logits = sum(mm(n, router_buf[c * step : (c + 1) * step, :]) for c, n in enumerate(normed))
     sig = hot_ref[...] * jax.nn.sigmoid(logits)
     gates_ref[...] = sig / jnp.sum(sig, axis=1, keepdims=True)
     for copy in copies:
@@ -307,6 +310,7 @@
     step = width // CHUNK
     experts = router.shape[1]
     whole = lambda shape: pl.BlockSpec(shape, lambda i: (0, 0))
+    router = pltpu.with_memory_space_constraint(router, pltpu.HBM)
     args = (partial, residual, gain, router, hot, select)
     return pl.pallas_call(
         route_body,
@@ -316,13 +320,17 @@
             jax.ShapeDtypeStruct((rows, experts), F32),
         ),
         grid=(1,),
-        in_specs=[whole(v.shape) for v in args],
+        in_specs=[pl.BlockSpec(memory_space=pltpu.HBM) if v is router else whole(v.shape) for v in args],
         out_specs=(
             pl.BlockSpec(memory_space=pltpu.HBM),
             whole((rows, width)),
             whole((rows, experts)),
         ),
-        scratch_shapes=[pltpu.VMEM((select.shape[0], step), BF), pltpu.SemaphoreType.DMA((4,))],
+        scratch_shapes=[
+            pltpu.VMEM((select.shape[0], step), BF),
+            pltpu.VMEM(router.shape, BF),
+            pltpu.SemaphoreType.DMA((5,)),
+        ],
         compiler_params=params(),
         name="route",
     )(*args)
@@ -442,7 +450,15 @@
     )(returned, mask, gates, mixed)
 
 
-def ready_body(q_ref, k_ref, v_ref, o_ref):
+def ready_body(q_hbm, k_hbm, v_hbm, o_ref, q_ref, k_ref, v_ref, sems):
+    fetch = [
+        pltpu.make_async_copy(src, dst, sems.at[i])
+        for i, (src, dst) in enumerate(((q_hbm, q_ref), (k_hbm, k_ref), (v_hbm, v_ref)))
+    ]
+    for copy in fetch:
+        copy.start()
+    for copy in fetch:
+        copy.wait()
     rows, side = q_ref.shape[0], KVH
     across = o_ref.shape[0] // rows // side
     wide = q_ref.shape[1] // side
@@ -454,14 +470,20 @@
             o_ref[at, wide + HD :] = v_ref[:, z * HD : (z + 1) * HD]
 
 
-def ready(q, k, v, devices):
-    rows = q.shape[0]
+def ready(*arrays, devices):
+    rows = arrays[0].shape[0]
+    arrays = [pltpu.with_memory_space_constraint(a, pltpu.HBM) for a in arrays]
+    shape = (devices * rows, (GROUP + 2) * HD)
     return pl.pallas_call(
         ready_body,
-        out_shape=pltpu.HBM((devices * rows, (GROUP + 2) * HD), BF),
+        out_shape=pltpu.HBM(shape, BF),
+        grid=(1,),
+        in_specs=[pl.BlockSpec(memory_space=pltpu.HBM)] * len(arrays),
+        out_specs=pl.BlockSpec(shape, lambda i: (0, 0)),
+        scratch_shapes=[*[pltpu.VMEM(a.shape, BF) for a in arrays], pltpu.SemaphoreType.DMA((len(arrays),))],
         compiler_params=params(24),
         name="ready",
-    )(q, k, v)
+    )(*arrays)
 
 
 def local(
@@ -488,7 +510,7 @@
     q, sk, sv = queries[0], suffix_keys[0], suffix_values[0]
     rows = q.shape[0]
     keys, values = prefix_keys[0], prefix_values[0]
-    copies = ready(q, sk, sv, seq_count)
+    copies = ready(q, sk, sv, devices=seq_count)
     parts = []
     for d in (1, 3, 2):
         head = (z + d) % side
@@ -496,7 +518,8 @@
             [lax.dynamic_slice_in_dim(a, head * HD, HD, 1) for a in (keys, values)], axis=0
         )
         parts.append(lax.ppermute(piece, "seq", [(i, (i + d * across) % seq_count) for i in range(seq_count)]))
-    q_all = lax.all_to_all(copies.reshape(seq_count, rows, -1), "seq", 0, 0, tiled=True).reshape(copies.shape)
+    q_all = lax.all_to_all(copies.reshape(seq_count, rows, -1), "seq", 0, 0, tiled=True)
+    q_all = q_all.reshape(copies.shape)
     place = jnp.stack([x, z]).astype(jnp.int32)
     state = attend_start(place, q_all, keys, values)
     state = attend_more(q_all, state, parts[:2])
@@ -538,4 +561,5 @@
     in_specs = (
         rows, rows, rows, rows, rows, P("grp", None), P("seq", None), rows, P(), P(), rows, spread, spread, spread,
     )
+
     return jax.shard_map(local, mesh=mesh, in_specs=in_specs, out_specs=rows, check_vma=False)

time: 192 us -> 186 us (0.969)
  waiting for transfers between devices: 77.8 us -> 69.8 us
  starting transfers between devices: 48.7 us -> 52 us
    all_to_all x2, starting transfers between devices: 16.1 us -> 28.9 us  [local(): lax.all_to_all(a.reshape(experts, CAP * CHUNK, -1), ('seq', 'grp'), 0, 0,...]
    all_to_all x1, waiting for transfers between devices: 15.6 us -> 9.03 us  [local(): lax.all_to_all(projected.reshape(seq_count, rows, -1), 'seq', 0, 0, tiled...]
    ppermute x3, starting transfers between devices: 11.1 us -> 4.98 us  [local(): lax.ppermute(a, 'seq', [(i, i // across * across + (i + d) % across) for...]
    all_to_all x1, starting transfers between devices: 7.47 us -> 4.18 us  [local(): lax.all_to_all(projected.reshape(seq_count, rows, -1), 'seq', 0, 0, tiled...]
  transfers between devices with their start and end apart: 10 -> 10, of which waited for: 5 -> 5; matrix products, arithmetic and copies ran while one was open for 11% -> 11% of each run, Pallas kernels for 10% -> 11%
where the time goes in v3:
time: 186 us; the launch traced here: 185 us
  waiting for transfers between devices  69.8 us (38%)
  starting transfers between devices  52 us (28%)
  Pallas kernels  40.2 us (22%)
  local copies, waits for them, and re-layouts  12.7 us (7%)
  other arithmetic  10.2 us (5%)
    all_to_all x2, waiting for transfers between devices, local(): lax.all_to_all(a.reshape(experts, CAP * CHUNK, -1), ('seq', 'grp'), 0, 0,...  51 us
    all_to_all x2, starting transfers between devices, local(): lax.all_to_all(a.reshape(experts, CAP * CHUNK, -1), ('seq', 'grp'), 0, 0,...  28.9 us
    pallas_call x1, Pallas kernels, expert(): pl.pallas_call(expert_body, out_shape=pltpu.HBM(arrived.shape, BF), grid=...  11.7 us
    all_to_all x1, waiting for transfers between devices, local(): lax.all_to_all(projected.reshape(seq_count, rows, -1), 'seq', 0, 0, tiled...  9.03 us
    all_to_all x1, waiting for transfers between devices, local(): lax.all_to_all(copies.reshape(seq_count, rows, -1), 'seq', 0, 0, tiled=True)  8.61 us
    pallas_call x1, Pallas kernels, attend_more(): pl.pallas_call(more_body, out_shape=state_shapes(rows), scratch_shapes=he...  7.78 us
    pallas_call x4, Pallas kernels, attend_last(): pl.pallas_call(lambda *refs: last_body(own, *refs), out_shape=jax.ShapeDt...  7.47 us
    ppermute x3, starting transfers between devices, local(): lax.ppermute(piece, 'seq', [(i, (i + d * across) % seq_count) for i in ra...  7.45 us
  transfers between devices with their start and end apart: 10, of which 5 were waited for; matrix products, arithmetic and copies ran while one was open for 11% of the time, Pallas kernels for 11%

profile of v3, /device:TPU:1, one launch (start us, length us, event | category | flops | bytes accessed | tf_op | source)
XLA Modules:
  0.0 185.1 jit_solution(4604178764493050538)
XLA Ops:
  0.0 1.5 dynamic-slice_bitcast_fusion
  1.5 0.8 pad_maximum_fusion.1
  2.3 4.6 %collective-permute-start.1 = (bf16[2048,128]{1,0:T(8,128)(2,1)}, bf16[2048,128]{1,0:T(8,128)(2,1)}, u32[]{:S(2)}, u32[]{:S(2)}) collective-permute-start(bf16[2048,128]{1,0:T(8,128)(2,1)} %pad_maximum_fusion.1), channel_id=1, source_target_pairs={{0,96},{8,104},{16,112},{24,120},{32,0},{40,8},{48,16},{56,24},{64... | collective-permute-start | bytes 1572872 | tf_op jit(solution)/shard_map/ppermute | solution.py:520
  6.9 0.8 pad_maximum_fusion
  7.7 0.0 collective-permute-start
  7.7 1.8 ready.1
  9.6 6.5 %all-to-all-start = ((bf16[16,16,1280]{2,1,0:T(8,128)(2,1)}), bf16[16,16,1280]{2,1,0:T(8,128)(2,1)S(1)}, u32[]{:S(2)}, u32[]{:S(2)}) async-start(bf16[16,16,1280]{2,1,0:T(8,128)(2,1)} %bitcast.69), calls=%async_computation | async-start | bytes 1310720 | tf_op jit(solution)/shard_map/all_to_all | solution.py:521
  16.1 0.8 pad_maximum_fusion.2
  17.0 2.9 %collective-permute-start.2 = (bf16[2048,128]{1,0:T(8,128)(2,1)}, bf16[2048,128]{1,0:T(8,128)(2,1)S(1)}, u32[]{:S(2)}, u32[]{:S(2)}) collective-permute-start(bf16[2048,128]{1,0:T(8,128)(2,1)} %pad_maximum_fusion.2), channel_id=1, source_target_pairs={{0,64},{8,72},{16,80},{24,88},{32,96},{40,104},{48,112},{56,120},{... | collective-permute-start | bytes 1572872 | tf_op jit(solution)/shard_map/ppermute | solution.py:520
  19.8 0.1 pad_add_fusion.1.idx
  19.9 0.1 pad_add_fusion.3.refs_0_
  20.0 0.1 pad_add_fusion.2.refs_0_
  20.1 0.1 pad_add_fusion.refs_0_
  20.1 8.6 %all-to-all-done = bf16[16,16,1280]{2,1,0:T(8,128)(2,1)S(1)} async-done(((bf16[16,16,1280]{2,1,0:T(8,128)(2,1)}), bf16[16,16,1280]{2,1,0:T(8,128)(2,1)S(1)}, u32[]{:S(2)}, u32[]{:S(2)}) %all-to-all-start) | async-done | bytes 655392 | tf_op jit(solution)/shard_map/all_to_all | solution.py:521
  28.7 0.0 copy-done
  28.8 0.0 copy-done.1
  28.8 4.3 %attend_start.1 = (f32[256,1024]{1,0:T(8,128)S(1)}, f32[256,128]{1,0:T(8,128)S(1)}) custom-call(s32[2]{0:T(128)S(1)} %pad_add_fusion.1.idx, bf16[256,1280]{1,0:T(8,128)(2,1)S(1)} %bitcast.49, bf16[1024,512]{1,0:T(8,128)(2,1)S(1)} %bitcast.60, bf16[1024,512]{1,0:T(8,128)(2,1)S(1)} %bitcast.61), custom_call_target="tpu_custom_call" | custom-call | tf_op jit(solution)/shard_map/attend_start/pallas_call | solution.py:138
  33.0 0.0 collective-permute-done.1.c_ref
  33.1 0.0 collective-permute-done.b_ref
  33.1 7.8 %attend_more.1 = (f32[256,1024]{1,0:T(8,128)S(1)}, f32[256,128]{1,0:T(8,128)S(1)}) custom-call(bf16[256,1280]{1,0:T(8,128)(2,1)S(1)} %bitcast.50, f32[256,1024]{1,0:T(8,128)S(1)} %get-tuple-element.12.so_ref, f32[256,128]{1,0:T(8,128)S(1)} %get-tuple-element.13.sl_ref, bf16[2048,128]{1,0:T(8,128)(2,1)} %collective-permute-done.b_ref, ...), custom_call_target="tpu_custom_call" | custom-call | tf_op jit(solution)/shard_map/attend_more/pallas_call | solution.py:165
  40.9 0.0 collective-permute-done.2.refs_4_
  40.9 1.7 attend_last.5
  42.5 3.0 %collective-permute-start.5 = (bf16[272,256]{1,0:T(8,128)(2,1)S(1)}, bf16[272,256]{1,0:T(8,128)(2,1)S(1)}, u32[]{:S(2)}, u32[]{:S(2)}) collective-permute-start(bf16[272,256]{1,0:T(8,128)(2,1)S(1)} %attend_last.5), channel_id=1, source_target_pairs={{0,24},{8,0},{16,8},{24,16},{32,56},{40,32},{48,40},{56,48},{64,88... | collective-permute-start | bytes 417800 | tf_op jit(solution)/shard_map/ppermute | solution.py:526
  45.6 1.7 attend_last.4
  47.3 0.0 collective-permute-start.4
  47.3 1.7 attend_last.3
  49.0 1.9 %collective-permute-start.3 = (bf16[272,256]{1,0:T(8,128)(2,1)S(1)}, bf16[272,256]{1,0:T(8,128)(2,1)S(1)}, u32[]{:S(2)}, u32[]{:S(2)}) collective-permute-start(bf16[272,256]{1,0:T(8,128)(2,1)S(1)} %attend_last.3), channel_id=1, source_target_pairs={{0,16},{8,24},{16,0},{24,8},{32,48},{40,56},{48,32},{56,40},{64,80... | collective-permute-start | bytes 417800 | tf_op jit(solution)/shard_map/ppermute | solution.py:526
  50.9 0.0 copy-done.6
  50.9 0.1 copy.26.refs_5_
  51.1 0.0 copy-start.2
  51.1 0.1 pad_add_fusion.4.refs_0_
  51.1 2.4 %attend_own.1.refs_3_ = bf16[272,256]{1,0:T(8,128)(2,1)S(1)} custom-call(s32[2]{0:T(128)S(1)} %pad_add_fusion.4.refs_0_, bf16[256,1280]{1,0:T(8,128)(2,1)S(1)} %bitcast.54, f32[256,1024]{1,0:T(8,128)S(1)} %get-tuple-element.14.refs_2_, f32[256,128]{1,0:T(8,128)S(1)} %get-tuple-element.15.refs_3_, bf16[2048,128]{1,0:T(8,128)(2,1)S(1)} %collective-permute-done.2.refs_4_, ...), custom_call_target="tpu_custom_call" | custom-call | tf_op jit(solution)/shard_map/attend_own/pallas_call | solution.py:217
  53.6 0.0 collective-permute-done.5.refs_2_
  53.6 0.0 collective-permute-done.4.refs_1_
  53.6 1.1 collective-permute-done.3.refs_0_
  54.6 0.0 copy-done.2
  54.6 3.5 %project.1 = bf16[256,4096]{1,0:T(8,128)(2,1)} custom-call(bf16[272,256]{1,0:T(8,128)(2,1)S(1)} %collective-permute-done.3.refs_0_, bf16[272,256]{1,0:T(8,128)(2,1)S(1)} %collective-permute-done.4.refs_1_, bf16[272,256]{1,0:T(8,128)(2,1)S(1)} %collective-permute-done.5.refs_2_, bf16[272,256]{1,0:T(8,128)(2,1)S(1)} %attend_own.1.refs_3_, ...), custom_call_target="tpu_custom_call" | custom-call | tf_op jit(solution)/shard_map/project/pallas_call | solution.py:261
  58.2 4.2 %all-to-all-start.1 = ((bf16[16,16,4096]{2,1,0:T(8,128)(2,1)}), bf16[16,16,4096]{2,1,0:T(8,128)(2,1)S(1)}, u32[]{:S(2)}, u32[]{:S(2)}) async-start(bf16[16,16,4096]{2,1,0:T(8,128)(2,1)} %bitcast.65), calls=%async_computation.1 | async-start | bytes 4194304 | tf_op jit(solution)/shard_map/all_to_all | solution.py:535
  62.4 0.0 copy-done.5
  62.4 0.1 copy.27
  62.5 0.1 fusion
  62.6 0.1 copy.29
  62.7 0.1 copy.28
  62.9 0.1 copy.30
  62.9 0.1 compare_and_fusion.1
  63.1 3.3 %and_convert_fusion.1 = bf16[128,2,8,8,16]{4,3,2,1,0:T(8,128)(2,1)} fusion(pred[8,8]{1,0:T(8,128)(4,1)S(1)} %copy.30, pred[128,2,16]{2,1,0:T(4,128)(4,1)S(1)} %compare_and_fusion.1), kind=kLoop, calls=%fused_computation.1 | loop fusion | flops 524288 | bytes 528448 | tf_op jit(solution)/shard_map/convert_element_type | solution.py:548
  66.4 5.1 %reshape.90.sel_ref = bf16[2048,128]{1,0:T(8,128)(2,1)S(1)} reshape(bf16[128,2,8,8,16]{4,3,2,1,0:T(8,128)(2,1)} %and_convert_fusion.1) | data formatting | bytes 1048576 | tf_op jit(solution)/shard_map/convert_element_type | solution.py:548
  71.5 9.0 %all-to-all-done.1 = bf16[16,16,4096]{2,1,0:T(8,128)(2,1)S(1)} async-done(((bf16[16,16,4096]{2,1,0:T(8,128)(2,1)}), bf16[16,16,4096]{2,1,0:T(8,128)(2,1)S(1)}, u32[]{:S(2)}, u32[]{:S(2)}) %all-to-all-start.1) | async-done | bytes 2097184 | tf_op jit(solution)/shard_map/all_to_all | solution.py:535
  80.5 0.0 copy-done.3
  80.5 0.0 copy-done.4
  80.5 2.0 %route.1 = (bf16[2048,512]{1,0:T(8,128)(2,1)}, f32[16,4096]{1,0:T(8,128)S(1)}, f32[16,128]{1,0:T(8,128)S(1)}) custom-call(bf16[256,4096]{1,0:T(8,128)(2,1)S(1)} %bitcast.58, bf16[16,4096]{1,0:T(8,128)(2,1)S(1)} %bitcast.62, f32[1,4096]{1,0:T(1,128)S(1)} %bitcast.63, bf16[4096,128]{1,0:T(8,128)(2,1)} %router_ref.1, f32[16,128]{1,0:T(8,128)S(1)} %get-tuple-element.28.hot_ref, ...), custom_call_target="tpu_custom_call" | custom-call | tf_op jit(solution)/shard_map/route/pallas_call | solution.py:315
  82.6 24.1 %all-to-all-start.2 = ((bf16[128,16,512]{2,1,0:T(8,128)(2,1)}), bf16[128,16,512]{2,1,0:T(8,128)(2,1)S(1)}, u32[]{:S(2)}, u32[]{:S(2)}) async-start(bf16[128,16,512]{2,1,0:T(8,128)(2,1)} %bitcast.70), calls=%async_computation.2 | async-start | bytes 4194304 | tf_op jit(solution)/shard_map/all_to_all | solution.py:550
  106.8 0.3 convert_convert_fusion
  107.0 29.8 %all-to-all-done.2 = bf16[128,16,512]{2,1,0:T(8,128)(2,1)S(1)} async-done(((bf16[128,16,512]{2,1,0:T(8,128)(2,1)}), bf16[128,16,512]{2,1,0:T(8,128)(2,1)S(1)}, u32[]{:S(2)}, u32[]{:S(2)}) %all-to-all-start.2) | async-done | bytes 2097184 | tf_op jit(solution)/shard_map/all_to_all | solution.py:550
  136.8 11.7 %expert.1 = bf16[2048,512]{1,0:T(8,128)(2,1)} custom-call(bf16[256,256]{1,0:T(8,128)(2,1)S(1)} %get-tuple-element.26.perm_ref, bf16[256,256]{1,0:T(8,128)(2,1)S(1)} %get-tuple-element.25.back_ref, bf16[2048,512]{1,0:T(8,128)(2,1)S(1)} %bitcast.57, bf16[4096,768]{1,0:T(8,128)(2,1)} %bitcast.66, bf16[4096,768]{1,0:T(8,128)(2,1)} %bitcast.67, ...), custom_call_target="tpu_custom_call" | custom-call | tf_op jit(solution)/shard_map/expert/pallas_call | solution.py:405
  148.5 4.8 %all-to-all-start.3 = ((bf16[128,16,512]{2,1,0:T(8,128)(2,1)}), bf16[128,16,512]{2,1,0:T(8,128)(2,1)S(1)}, u32[]{:S(2)}, u32[]{:S(2)}) async-start(bf16[128,16,512]{2,1,0:T(8,128)(2,1)} %bitcast.64), calls=%async_computation.3 | async-start | bytes 4194304 | tf_op jit(solution)/shard_map/all_to_all | solution.py:550
  153.3 0.1 copy.31
  153.4 0.1 copy.32
  153.5 0.1 compare_and_fusion
  153.6 3.3 %and_convert_fusion = bf16[8,16,128,2,8]{1,0,4,3,2:T(8,128)(2,1)} fusion(pred[8,8]{0,1:T(8,128)(4,1)S(1)} %iota_compare_fusion.1, pred[16,128,2]{0,2,1:T(4,128)(4,1)S(1)} %compare_and_fusion), kind=kLoop, calls=%fused_computation | loop fusion | flops 524288 | bytes 528448 | tf_op jit(solution)/shard_map/convert_element_type | solution.py:545
  156.9 5.1 %reshape.91 = bf16[128,2048]{0,1:T(8,128)(2,1)S(1)} reshape(bf16[8,16,128,2,8]{1,0,4,3,2:T(8,128)(2,1)} %and_convert_fusion) | data formatting | bytes 1048576 | tf_op jit(solution)/shard_map/convert_element_type | solution.py:545
  162.0 0.2 copy.33.mask_ref
  162.2 21.3 %all-to-all-done.3 = bf16[128,16,512]{2,1,0:T(8,128)(2,1)S(1)} async-done(((bf16[128,16,512]{2,1,0:T(8,128)(2,1)}), bf16[128,16,512]{2,1,0:T(8,128)(2,1)S(1)}, u32[]{:S(2)}, u32[]{:S(2)}) %all-to-all-start.3) | async-done | bytes 2097184 | tf_op jit(solution)/shard_map/all_to_all | solution.py:550
  183.5 1.6 finish.1
  (14 shorter events, 0.1 us)
Async XLA Ops:
  2.3 30.7 %collective-permute-start.1 = (bf16[2048,128]{1,0:T(8,128)(2,1)}, bf16[2048,128]{1,0:T(8,128)(2,1)}, u32[]{:S(2)}, u32[]{:S(2)}) collective-permute-start(bf16[2048,128]{1,0:T(8,128)(2,1)} %pad_maximum_fusion.1), channel_id=1, source_target_pairs={{0,96},{8,104},{16,112},{24,120},{32,0},{40,8},{48,16},{56,24},{64... | collective-permute-start | bytes 1572872 | tf_op jit(solution)/shard_map/ppermute | solution.py:520
  6.9 21.8 %copy-start = (bf16[1,1024,512]{2,1,0:T(8,128)(2,1)S(1)}, bf16[1,1024,512]{2,1,0:T(8,128)(2,1)}, u32[]{:S(2)}) copy-start(bf16[1,1024,512]{2,1,0:T(8,128)(2,1)} %param.15) | copy-start | bytes 3145732
  6.9 21.9 %copy-start.1 = (bf16[1,1024,512]{2,1,0:T(8,128)(2,1)S(1)}, bf16[1,1024,512]{2,1,0:T(8,128)(2,1)}, u32[]{:S(2)}) copy-start(bf16[1,1024,512]{2,1,0:T(8,128)(2,1)} %param.16) | copy-start | bytes 3145732
  7.7 25.3 %collective-permute-start = (bf16[2048,128]{1,0:T(8,128)(2,1)}, bf16[2048,128]{1,0:T(8,128)(2,1)}, u32[]{:S(2)}, u32[]{:S(2)}) collective-permute-start(bf16[2048,128]{1,0:T(8,128)(2,1)} %pad_maximum_fusion), channel_id=1, source_target_pairs={{0,32},{8,40},{16,48},{24,56},{32,64},{40,72},{48,80},{56,88},{64,... | collective-permute-start | bytes 1572872 | tf_op jit(solution)/shard_map/ppermute | solution.py:520
  9.6 19.1 %all-to-all-start = ((bf16[16,16,1280]{2,1,0:T(8,128)(2,1)}), bf16[16,16,1280]{2,1,0:T(8,128)(2,1)S(1)}, u32[]{:S(2)}, u32[]{:S(2)}) async-start(bf16[16,16,1280]{2,1,0:T(8,128)(2,1)} %bitcast.69), calls=%async_computation | async-start | bytes 1310720 | tf_op jit(solution)/shard_map/all_to_all | solution.py:521
  17.0 23.9 %collective-permute-start.2 = (bf16[2048,128]{1,0:T(8,128)(2,1)}, bf16[2048,128]{1,0:T(8,128)(2,1)S(1)}, u32[]{:S(2)}, u32[]{:S(2)}) collective-permute-start(bf16[2048,128]{1,0:T(8,128)(2,1)} %pad_maximum_fusion.2), channel_id=1, source_target_pairs={{0,64},{8,72},{16,80},{24,88},{32,96},{40,104},{48,112},{56,120},{... | collective-permute-start | bytes 1572872 | tf_op jit(solution)/shard_map/ppermute | solution.py:520
  42.5 8.4 %copy-start.6 = (s32[1,256]{1,0:T(1,128)S(1)}, s32[1,256]{1,0:T(1,128)}, u32[]{:S(2)}) copy-start(s32[1,256]{1,0:T(1,128)} %param.19) | copy-start | bytes 3076
  42.5 11.0 %collective-permute-start.5 = (bf16[272,256]{1,0:T(8,128)(2,1)S(1)}, bf16[272,256]{1,0:T(8,128)(2,1)S(1)}, u32[]{:S(2)}, u32[]{:S(2)}) collective-permute-start(bf16[272,256]{1,0:T(8,128)(2,1)S(1)} %attend_last.5), channel_id=1, source_target_pairs={{0,24},{8,0},{16,8},{24,16},{32,56},{40,32},{48,40},{56,48},{64,88... | collective-permute-start | bytes 417800 | tf_op jit(solution)/shard_map/ppermute | solution.py:526
  47.3 6.3 %collective-permute-start.4 = (bf16[272,256]{1,0:T(8,128)(2,1)S(1)}, bf16[272,256]{1,0:T(8,128)(2,1)S(1)}, u32[]{:S(2)}, u32[]{:S(2)}) collective-permute-start(bf16[272,256]{1,0:T(8,128)(2,1)S(1)} %attend_last.4), channel_id=1, source_target_pairs={{0,8},{8,16},{16,24},{24,0},{32,40},{40,48},{48,56},{56,32},{64,72... | collective-permute-start | bytes 417800 | tf_op jit(solution)/shard_map/ppermute | solution.py:526
  49.0 5.6 %collective-permute-start.3 = (bf16[272,256]{1,0:T(8,128)(2,1)S(1)}, bf16[272,256]{1,0:T(8,128)(2,1)S(1)}, u32[]{:S(2)}, u32[]{:S(2)}) collective-permute-start(bf16[272,256]{1,0:T(8,128)(2,1)S(1)} %attend_last.3), channel_id=1, source_target_pairs={{0,16},{8,24},{16,0},{24,8},{32,48},{40,56},{48,32},{56,40},{64,80... | collective-permute-start | bytes 417800 | tf_op jit(solution)/shard_map/ppermute | solution.py:526
  51.1 3.6 %copy-start.2 = (bf16[256,4096]{1,0:T(8,128)(2,1)S(1)}, bf16[256,4096]{1,0:T(8,128)(2,1)}, u32[]{:S(2)}) copy-start(bf16[256,4096]{1,0:T(8,128)(2,1)} %refs_4_.1) | copy-start | bytes 6291460
  58.2 4.2 %copy-start.5 = (s32[1,16,8]{1,2,0:T(8,128)S(1)}, s32[1,16,8]{1,2,0:T(8,128)}, u32[]{:S(2)}) copy-start(s32[1,16,8]{1,2,0:T(8,128)} %param.24) | copy-start | bytes 1540
  58.2 22.3 %all-to-all-start.1 = ((bf16[16,16,4096]{2,1,0:T(8,128)(2,1)}), bf16[16,16,4096]{2,1,0:T(8,128)(2,1)S(1)}, u32[]{:S(2)}, u32[]{:S(2)}) async-start(bf16[16,16,4096]{2,1,0:T(8,128)(2,1)} %bitcast.65), calls=%async_computation.1 | async-start | bytes 4194304 | tf_op jit(solution)/shard_map/all_to_all | solution.py:535
  66.4 14.1 %copy-start.3 = (bf16[1,16,4096]{2,1,0:T(8,128)(2,1)S(1)}, bf16[1,16,4096]{2,1,0:T(8,128)(2,1)}, u32[]{:S(2)}) copy-start(bf16[1,16,4096]{2,1,0:T(8,128)(2,1)} %param.21) | copy-start | bytes 393220
  66.4 14.1 %copy-start.4 = (f32[4096]{0:T(1024)S(1)}, f32[4096]{0:T(1024)}, u32[]{:S(2)}) copy-start(f32[4096]{0:T(1024)} %param.22) | copy-start | bytes 49156
  82.6 54.2 %all-to-all-start.2 = ((bf16[128,16,512]{2,1,0:T(8,128)(2,1)}), bf16[128,16,512]{2,1,0:T(8,128)(2,1)S(1)}, u32[]{:S(2)}, u32[]{:S(2)}) async-start(bf16[128,16,512]{2,1,0:T(8,128)(2,1)} %bitcast.70), calls=%async_computation.2 | async-start | bytes 4194304 | tf_op jit(solution)/shard_map/all_to_all | solution.py:550
  148.5 35.0 %all-to-all-start.3 = ((bf16[128,16,512]{2,1,0:T(8,128)(2,1)}), bf16[128,16,512]{2,1,0:T(8,128)(2,1)S(1)}, u32[]{:S(2)}, u32[]{:S(2)}) async-start(bf16[128,16,512]{2,1,0:T(8,128)(2,1)} %bitcast.64), calls=%async_computation.3 | async-start | bytes 4194304 | tf_op jit(solution)/shard_map/all_to_all | solution.py:550

commit v4 on v3

--- a/solution.py
+++ b/solution.py
@@ -81,11 +81,16 @@
     return jnp.sum(jnp.where(lane == h, stats, 0.0), axis=1, keepdims=True)
 
 
-def visible_rows(parents):
-    n = parents.shape[0]
+def visible_rows(par_ref):
+    n = par_ref.shape[0]
     rows = lax.broadcasted_iota(jnp.int32, (n, n), 0)
     cols = lax.broadcasted_iota(jnp.int32, (n, n), 1)
-    step = ((parents == cols).astype(F32) + (rows == cols).astype(F32)).astype(BF)
+    side = n // 4
+    block = side // 4
+    starts = [z * side + x * block for x in range(4) for z in range(4)]
+    parents = jnp.concatenate([par_ref[at : at + block, :] for at in starts], axis=0)
+    number = cols // block % 4 * side + cols // side * block + cols % block
+    step = ((parents == number).astype(F32) + (rows == cols).astype(F32)).astype(BF)
     two = mm(step, step).astype(BF)
     four = mm(two, two).astype(BF)
     six = mm(four, two).astype(BF)
@@ -171,41 +176,44 @@
     )(q_all, *state, *parts)
 
 
-def last_body(own, idx, q_ref, so_ref, sl_ref, b_ref, *rest):
+def last_body(shifts, idx, q_ref, so_ref, sl_ref, b_ref, *rest):
     n = b_ref.shape[0] // 2
     chunks, values = [(b_ref[:n, :], None)], [b_ref[n:, :]]
-    if own:
-        par_ref, sk_ref, sv_ref, o_ref, v1, s0, s1 = rest
-        chunks.append((sk_ref[...], visible_rows(par_ref[...])))
+    if shifts == (0,):
+        par_ref, sk_ref, sv_ref, *rest = rest
+        chunks.append((sk_ref[...], visible_rows(par_ref)))
         values.append(sv_ref[...])
-    else:
-        o_ref, v1, s0, s1 = rest
+    outs, (v1, *held) = rest[: len(shifts)], rest[len(shifts) :]
     with_ones(v1, values)
     rows = q_ref.shape[0]
     lane = lax.broadcasted_iota(jnp.int32, (rows, HD), 1)
-    stats = jnp.zeros((rows, HD), F32)
-    tops = [scores(q_ref[:, h * HD : (h + 1) * HD], chunks, s) for h, s in enumerate((s0, s1))]
-    for h, s in enumerate((s0, s1)):
-        cols = slice(h * HD, (h + 1) * HD)
-        state = so_ref[:, cols], lane_of(sl_ref[...], 2 * idx[0] + h)
-        o, lse = weigh(s, v1, tops[h], state)
-        o_ref[:rows, cols] = o.astype(BF)
+    heads = [(idx[0] + d) % (GROUP // 2) * 2 + h for d in shifts for h in range(2)]
+    columns = [pl.ds(pl.multiple_of(h * HD, HD), HD) for h in heads]
+    tops = {0: scores(q_ref[:, columns[0]], chunks, held[0])}
+    for i, (head, cols) in enumerate(zip(heads, columns)):
+        if i + 1 < len(heads):
+            tops[i + 1] = scores(q_ref[:, columns[i + 1]], chunks, held[(i + 1) % len(held)])
+        state = so_ref[:, cols], lane_of(sl_ref[...], head)
+        o, lse = weigh(held[i % len(held)], v1, tops[i], state)
+        h, o_ref = i % 2, outs[i // 2]
+        stats = jnp.zeros((rows, HD), F32) if h == 0 else stats
+        o_ref[:rows, h * HD : (h + 1) * HD] = o.astype(BF)
         left = lse
         for part in range(3):
             piece = left.astype(BF).astype(F32)
             left = left - piece
             stats = jnp.where(lane == 3 * h + part, piece, stats)
-    o_ref[rows:, :] = stats.T[:16, :].astype(BF)
-
-
-def attend_last(own, idx, q_all, state, part, extra):
+        if h == 1:
+            o_ref[rows:, :] = stats.T[:16, :].astype(BF)
+
+
+def attend_last(shifts, idx, q_all, state, part, extra):
     rows = q_all.shape[0]
     whole = lambda shape: pl.BlockSpec(shape, lambda i, idx: (0, 0))
-    pair = pl.BlockSpec((rows, 2 * HD), lambda i, idx: (0, idx[0]))
-    specs = [pair, pair, whole((rows, HD)), whole(part.shape)]
     args = [q_all, *state, part]
+    specs = [whole(v.shape) for v in args]
     count = part.shape[0] // 2
-    if own:
+    if shifts == (0,):
         at = GROUP
         specs += [
             whole((rows, 1)),
@@ -214,18 +222,19 @@
         ]
         args += [extra, q_all, q_all]
         count += rows
-    return pl.pallas_call(
-        lambda *refs: last_body(own, *refs),
-        out_shape=jax.ShapeDtypeStruct((rows + 16, 2 * HD), BF),
+    shape = (rows + 16, 2 * HD)
+    return pl.pallas_call(
+        lambda *refs: last_body(shifts, *refs),
+        out_shape=[jax.ShapeDtypeStruct(shape, BF)] * len(shifts),
         grid_spec=pltpu.PrefetchScalarGridSpec(
             num_scalar_prefetch=1,
             grid=(1,),
             in_specs=specs,
-            out_specs=whole((rows + 16, 2 * HD)),
-            scratch_shapes=heads_scratch(rows, count),
+            out_specs=[whole(shape)] * len(shifts),
+            scratch_shapes=[pltpu.VMEM((count, 2 * HD), BF), *[pltpu.VMEM((rows, count), F32)] * 2],
         ),
         compiler_params=params(24),
-        name="attend_own" if own else "attend_last",
+        name="attend_own" if shifts == (0,) else "attend_last",
     )(idx, *args)
 
 
@@ -247,11 +256,17 @@
 
 
 def project_body(*refs):
-    *parts, w_ref, o_ref, att = refs
+    *parts, w_ref, o_ref, mixed_rows, att = refs
 
     @pl.when(pl.program_id(0) == 0)
     def _():
-        combine(parts, att)
+        combine(parts, mixed_rows)
+        side = att.shape[0] // 4
+        block = side // 4
+        for z in range(4):
+            for x in range(4):
+                to, come = z * side + x * block, x * side + z * block
+                att[to : to + block, :] = mixed_rows[come : come + block, :]
 
     o_ref[...] = mm(att[...], w_ref[...]).astype(BF)
 
@@ -267,7 +282,7 @@
             pl.BlockSpec((weights.shape[0], width // steps), lambda i: (0, i)),
         ],
         out_specs=pl.BlockSpec((rows, width // steps), lambda i: (0, i)),
-        scratch_shapes=[pltpu.VMEM((rows, 2 * HD), BF)],
+        scratch_shapes=[pltpu.VMEM((rows, 2 * HD), BF), pltpu.VMEM((rows, 2 * HD), BF)],
         compiler_params=params(24),
         name="project",
     )(*parts, weights)
@@ -450,40 +465,60 @@
     )(returned, mask, gates, mixed)
 
 
-def ready_body(q_hbm, k_hbm, v_hbm, o_ref, q_ref, k_ref, v_ref, sems):
+SHIFTS = (1, 3, 2)
+
+
+def ready_body(idx, q_hbm, k_hbm, v_hbm, keys_hbm, values_hbm, o_ref, *rest):
+    *pieces, q_ref, k_ref, v_ref, sems = rest
     fetch = [
         pltpu.make_async_copy(src, dst, sems.at[i])
         for i, (src, dst) in enumerate(((q_hbm, q_ref), (k_hbm, k_ref), (v_hbm, v_ref)))
     ]
-    for copy in fetch:
+    count = keys_hbm.shape[0]
+    send = []
+    for d, piece in zip(SHIFTS, pieces):
+        cols = pl.ds(pl.multiple_of((idx[1] + d) % KVH * HD, HD), HD)
+        for j, src in enumerate((keys_hbm, values_hbm)):
+            to = piece.at[pl.ds(j * count, count), :]
+            send.append(pltpu.make_async_copy(src.at[:, cols], to, sems.at[len(fetch) + len(send)]))
+    for copy in fetch + send:
         copy.start()
     for copy in fetch:
         copy.wait()
-    rows, side = q_ref.shape[0], KVH
-    across = o_ref.shape[0] // rows // side
-    wide = q_ref.shape[1] // side
-    for z in range(side):
-        for x in range(across):
-            at = slice((z * across + x) * rows, (z * across + x + 1) * rows)
-            o_ref[at, :wide] = q_ref[:, z * wide : (z + 1) * wide]
-            o_ref[at, wide : wide + HD] = k_ref[:, z * HD : (z + 1) * HD]
-            o_ref[at, wide + HD :] = v_ref[:, z * HD : (z + 1) * HD]
-
-
-def ready(*arrays, devices):
-    rows = arrays[0].shape[0]
+    rows, wide = q_ref.shape[0], q_ref.shape[1] // KVH
+    for z in range(KVH):
+        at = slice(z * rows, (z + 1) * rows)
+        o_ref[at, :wide] = q_ref[:, z * wide : (z + 1) * wide]
+        o_ref[at, wide : wide + HD] = k_ref[:, z * HD : (z + 1) * HD]
+        o_ref[at, wide + HD :] = v_ref[:, z * HD : (z + 1) * HD]
+    for copy in send:
+        copy.wait()
+
+
+def ready(idx, *arrays):
+    rows, count = arrays[0].shape[0], arrays[3].shape[0]
     arrays = [pltpu.with_memory_space_constraint(a, pltpu.HBM) for a in arrays]
-    shape = (devices * rows, (GROUP + 2) * HD)
+    shape = (KVH * rows, (GROUP + 2) * HD)
+    hbm = pl.BlockSpec(memory_space=pltpu.HBM)
     return pl.pallas_call(
         ready_body,
-        out_shape=pltpu.HBM(shape, BF),
-        grid=(1,),
-        in_specs=[pl.BlockSpec(memory_space=pltpu.HBM)] * len(arrays),
-        out_specs=pl.BlockSpec(shape, lambda i: (0, 0)),
-        scratch_shapes=[*[pltpu.VMEM(a.shape, BF) for a in arrays], pltpu.SemaphoreType.DMA((len(arrays),))],
+        out_shape=[pltpu.HBM(shape, BF), *[pltpu.HBM((2 * count, HD), BF)] * len(SHIFTS)],
+        grid_spec=pltpu.PrefetchScalarGridSpec(
+            num_scalar_prefetch=1,
+            grid=(1,),
+            in_specs=[hbm] * len(arrays),
+            out_specs=[
+                pl.BlockSpec(shape, lambda i, idx: (0, 0)),
+                *[pl.BlockSpec((2 * count, HD), lambda i, idx: (0, 0))] * len(SHIFTS),
+            ],
+            scratch_shapes=[
+                *[pltpu.VMEM(a.shape, BF) for a in arrays[:3]],
+                pltpu.SemaphoreType.DMA((3 + 2 * len(SHIFTS),)),
+            ],
+        ),
         compiler_params=params(24),
         name="ready",
-    )(*arrays)
+    )(idx, *arrays)
 
 
 def local(
@@ -510,27 +545,29 @@
     q, sk, sv = queries[0], suffix_keys[0], suffix_values[0]
     rows = q.shape[0]
     keys, values = prefix_keys[0], prefix_values[0]
-    copies = ready(q, sk, sv, devices=seq_count)
+    place = jnp.stack([x, z]).astype(jnp.int32)
+    copies, *pieces = ready(place, q, sk, sv, keys, values)
     parts = []
-    for d in (1, 3, 2):
-        head = (z + d) % side
-        piece = jnp.concatenate(
-            [lax.dynamic_slice_in_dim(a, head * HD, HD, 1) for a in (keys, values)], axis=0
-        )
+    for d, piece in zip(SHIFTS, pieces):
         parts.append(lax.ppermute(piece, "seq", [(i, (i + d * across) % seq_count) for i in range(seq_count)]))
-    q_all = lax.all_to_all(copies.reshape(seq_count, rows, -1), "seq", 0, 0, tiled=True)
-    q_all = q_all.reshape(copies.shape)
-    place = jnp.stack([x, z]).astype(jnp.int32)
+    columns = [[i * across + j for i in range(side)] for j in range(across)]
+    lines = [[i * across + j for j in range(across)] for i in range(side)]
+    mine = lax.all_to_all(
+        copies.reshape(side, rows, -1), "seq", 0, 0, tiled=True, axis_index_groups=columns
+    ).reshape(copies.shape)
+    q_all = lax.all_to_all(
+        jnp.broadcast_to(mine, (across, *mine.shape)), "seq", 0, 0, tiled=True, axis_index_groups=lines
+    )
+    q_all = q_all.reshape(across * mine.shape[0], -1)
     state = attend_start(place, q_all, keys, values)
     state = attend_more(q_all, state, parts[:2])
     along_x = lambda a, d: lax.ppermute(
         a, "seq", [(i, i // across * across + (i + d) % across) for i in range(seq_count)]
     )
-    blocks = []
-    for d in (2, 1, 3, 0):
-        idx = jnp.stack([(x + d) % across, z]).astype(jnp.int32)
-        block = attend_last(d == 0, idx, q_all, state, parts[2], parents[0][:, None])
-        blocks.append(along_x(block, d) if d else block)
+    others = (2, 1, 3)
+    blocks = attend_last(others, place, q_all, state, parts[2], None)
+    blocks = [along_x(block, d) for d, block in zip(others, blocks)]
+    blocks += attend_last((0,), place, q_all, state, parts[2], parents[0][:, None])
     projected = project(blocks, out_proj)
     arrived = lax.all_to_all(
         projected.reshape(seq_count, rows, -1), "seq", 0, 0, tiled=True

time: 186 us -> 179 us (0.962)
  blocking collectives: 0 us -> 11.4 us
  starting transfers between devices: 52 us -> 42.1 us
  waiting for transfers between devices: 69.8 us -> 65.9 us
  other arithmetic: 10.2 us -> 7.36 us
    all_to_all x0 -> x1, blocking collectives: none -> 11.4 us  [local(): lax.all_to_all(jnp.broadcast_to(mine, (across, *mine.shape)), 'seq', 0, 0...]
    all_to_all x1, waiting for transfers between devices: 8.61 us -> 0.67 us  [local(): lax.all_to_all(copies.reshape(side, rows, -1), 'seq', 0, 0, tiled=True, a...]
    all_to_all x2, starting transfers between devices: 28.9 us -> 21.1 us  [local(): lax.all_to_all(a.reshape(experts, CAP * CHUNK, -1), ('seq', 'grp'), 0, 0,...]
    all_to_all x1, waiting for transfers between devices: 9.03 us -> 13.9 us  [local(): lax.all_to_all(projected.reshape(seq_count, rows, -1), 'seq', 0, 0, tiled...]
    ppermute x3, starting transfers between devices: 7.45 us -> 4.43 us  [local(): lax.ppermute(piece, 'seq', [(i, (i + d * across) % seq_count) for i in ra...]
    concatenate x3 -> x0, other arithmetic: 2.5 us -> none  [local(): jnp.concatenate([lax.dynamic_slice_in_dim(a, head * HD, HD, 1) for a in (...]
    all_to_all x1, starting transfers between devices: 4.18 us -> 6.6 us  [local(): lax.all_to_all(projected.reshape(seq_count, rows, -1), 'seq', 0, 0, tiled...]
    pallas_call x5 -> x3, Pallas kernels: 9.31 us -> 9.31 us  [the longest x2 5.93 us: attend_last(): pl.pallas_call(lambda *refs: last_body(shifts, *refs), out_shape=[jax.Sha...]
  transfers between devices with their start and end apart: 10 -> 10, of which waited for: 5 -> 5; matrix products, arithmetic and copies ran while one was open for 11% -> 10% of each run, Pallas kernels for 11% -> 8%
where the time goes in v4:
time: 179 us; the launch traced here: 178 us
  waiting for transfers between devices  65.9 us (37%)
  starting transfers between devices  42.1 us (24%)
  Pallas kernels  40.2 us (22%)
  blocking collectives  11.4 us (6%)
  local copies, waits for them, and re-layouts  11.2 us (6%)
  other arithmetic  7.36 us (4%)
    all_to_all x2, waiting for transfers between devices, local(): lax.all_to_all(a.reshape(experts, CAP * CHUNK, -1), ('seq', 'grp'), 0, 0,...  51.1 us
    all_to_all x2, starting transfers between devices, local(): lax.all_to_all(a.reshape(experts, CAP * CHUNK, -1), ('seq', 'grp'), 0, 0,...  21.1 us
    all_to_all x1, waiting for transfers between devices, local(): lax.all_to_all(projected.reshape(seq_count, rows, -1), 'seq', 0, 0, tiled...  13.9 us
    pallas_call x1, Pallas kernels, expert(): pl.pallas_call(expert_body, out_shape=pltpu.HBM(arrived.shape, BF), grid=...  11.7 us
    all_to_all x1, blocking collectives, local(): lax.all_to_all(jnp.broadcast_to(mine, (across, *mine.shape)), 'seq', 0, 0...  11.4 us
    pallas_call x1, Pallas kernels, attend_more(): pl.pallas_call(more_body, out_shape=state_shapes(rows), scratch_shapes=he...  7.74 us
    all_to_all x1, starting transfers between devices, local(): lax.all_to_all(projected.reshape(seq_count, rows, -1), 'seq', 0, 0, tiled...  6.6 us
    pallas_call x2, Pallas kernels, attend_last(): pl.pallas_call(lambda *refs: last_body(shifts, *refs), out_shape=[jax.Sha...  5.93 us
  transfers between devices with their start and end apart: 10, of which 5 were waited for; matrix products, arithmetic and copies ran while one was open for 10% of the time, Pallas kernels for 8%

profile of v4, /device:TPU:1, one launch (start us, length us, event | category | flops | bytes accessed | tf_op | source)
XLA Modules:
  0.0 178.4 jit_solution(306550825477981405)
XLA Ops:
  0.0 0.1 pad_add_fusion.idx.refs_0_
  0.1 0.0 copy-start
  0.1 0.0 copy-start.1
  0.1 3.4 %ready.1 = (bf16[64,1280]{1,0:T(8,128)(2,1)}, bf16[2048,128]{1,0:T(8,128)(2,1)}, bf16[2048,128]{1,0:T(8,128)(2,1)}, bf16[2048,128]{1,0:T(8,128)(2,1)}) custom-call(s32[2]{0:T(128)S(1)} %pad_add_fusion.idx.refs_0_, bf16[16,4096]{1,0:T(8,128)(2,1)} %bitcast.57, bf16[16,512]{1,0:T(8,128)(2,1)} %bitcast.59, bf16[16,512]{1,0:T(8,128)(2,1)} %bitcast.60, ...), custom_call_target="tpu_custom_call" | custom-call | tf_op jit(solution)/shard_map/ready/pallas_call | solution.py:503
  3.5 5.9 %all-to-all-start = ((bf16[4,16,1280]{2,1,0:T(8,128)(2,1)}), bf16[4,16,1280]{2,1,0:T(8,128)(2,1)S(1)}, u32[]{:S(2)}, u32[]{:S(2)}) async-start(bf16[4,16,1280]{2,1,0:T(8,128)(2,1)} %bitcast.56), calls=%async_computation | async-start | bytes 327680 | tf_op jit(solution)/shard_map/all_to_all | solution.py:555
  9.3 1.5 collective-permute-start
  10.8 1.2 collective-permute-start.1
  12.0 1.7 collective-permute-start.2
  13.8 0.7 all-to-all-done
  14.5 11.4 %all_to_all.25 = bf16[4,64,1280]{2,1,0:T(8,128)(2,1)S(1)} all-to-all(bf16[4,64,1280]{2,1,0:T(8,128)(2,1)S(1)} %broadcast_in_dim.6), channel_id=1, replica_groups={{0,8,16,24},{32,40,48,56},{64,72,80,88},{96,104,112,120},{1,9,17,25},{3..., dimensions={0} | all-to-all | bytes 1310720 | tf_op jit(solution)/shard_map/all_to_all | solution.py:558
  25.9 0.0 copy-done
  25.9 0.0 copy-done.1
  25.9 4.3 %attend_start.1 = (f32[256,1024]{1,0:T(8,128)S(1)}, f32[256,128]{1,0:T(8,128)S(1)}) custom-call(s32[2]{0:T(128)S(1)} %pad_add_fusion.idx.refs_0_, bf16[256,1280]{1,0:T(8,128)(2,1)S(1)} %bitcast.34, bf16[1024,512]{1,0:T(8,128)(2,1)S(1)} %bitcast.44, bf16[1024,512]{1,0:T(8,128)(2,1)S(1)} %bitcast.46), custom_call_target="tpu_custom_call" | custom-call | tf_op jit(solution)/shard_map/attend_start/pallas_call | solution.py:143
  30.2 0.0 collective-permute-done.b_ref
  30.2 0.0 collective-permute-done.1.c_ref
  30.2 0.0 copy-start.6
  30.2 7.7 %attend_more.1 = (f32[256,1024]{1,0:T(8,128)S(1)}, f32[256,128]{1,0:T(8,128)S(1)}) custom-call(bf16[256,1280]{1,0:T(8,128)(2,1)S(1)} %bitcast.35, f32[256,1024]{1,0:T(8,128)S(1)} %get-tuple-element.20.so_ref, f32[256,128]{1,0:T(8,128)S(1)} %get-tuple-element.21.sl_ref, bf16[2048,128]{1,0:T(8,128)(2,1)} %collective-permute-done.b_ref, ...), custom_call_target="tpu_custom_call" | custom-call | tf_op jit(solution)/shard_map/attend_more/pallas_call | solution.py:170
  38.0 0.0 collective-permute-done.2.refs_4_
  38.0 3.5 %attend_last.1 = (bf16[272,256]{1,0:T(8,128)(2,1)S(1)}, bf16[272,256]{1,0:T(8,128)(2,1)S(1)}, bf16[272,256]{1,0:T(8,128)(2,1)S(1)}) custom-call(s32[2]{0:T(128)S(1)} %pad_add_fusion.idx.refs_0_, bf16[256,1280]{1,0:T(8,128)(2,1)S(1)} %bitcast.36, f32[256,1024]{1,0:T(8,128)S(1)} %get-tuple-element.24.refs_2_, f32[256,128]{1,0:T(8,128)S(1)} %get-tuple-element.25.refs_3_, ...), custom_call_target="tpu_custom_call" | custom-call | tf_op jit(solution)/shard_map/attend_last/pallas_call | solution.py:226
  41.5 1.4 collective-permute-start.3
  42.9 0.3 collective-permute-start.4
  43.2 2.4 %collective-permute-start.5 = (bf16[272,256]{1,0:T(8,128)(2,1)S(1)}, bf16[272,256]{1,0:T(8,128)(2,1)S(1)}, u32[]{:S(2)}, u32[]{:S(2)}) collective-permute-start(bf16[272,256]{1,0:T(8,128)(2,1)S(1)} %get-tuple-element.29), channel_id=1, source_target_pairs={{0,24},{8,0},{16,8},{24,16},{32,56},{40,32},{48,40},{56,48},{64,88... | collective-permute-start | bytes 417800 | tf_op jit(solution)/shard_map/ppermute | solution.py:564
  45.5 0.0 copy-done.6
  45.5 0.1 copy.26.refs_5_
  45.7 0.0 copy-start.2
  45.7 2.4 %attend_own.1.refs_3_ = bf16[272,256]{1,0:T(8,128)(2,1)S(1)} custom-call(s32[2]{0:T(128)S(1)} %pad_add_fusion.idx.refs_0_, bf16[256,1280]{1,0:T(8,128)(2,1)S(1)} %bitcast.37, f32[256,1024]{1,0:T(8,128)S(1)} %get-tuple-element.24.refs_2_, f32[256,128]{1,0:T(8,128)S(1)} %get-tuple-element.25.refs_3_, bf16[2048,128]{1,0:T(8,128)(2,1)S(1)} %collective-permute-done.2.refs_4_, ...), custom_call_target="tpu_custom_call" | custom-call | tf_op jit(solution)/shard_map/attend_own/pallas_call | solution.py:226
  48.1 0.0 collective-permute-done.3.refs_0_
  48.1 0.3 collective-permute-done.4.refs_1_
  48.4 0.0 collective-permute-done.5.refs_2_
  48.4 0.0 copy-done.2
  48.4 3.6 %project.1 = bf16[256,4096]{1,0:T(8,128)(2,1)} custom-call(bf16[272,256]{1,0:T(8,128)(2,1)S(1)} %collective-permute-done.3.refs_0_, bf16[272,256]{1,0:T(8,128)(2,1)S(1)} %collective-permute-done.4.refs_1_, bf16[272,256]{1,0:T(8,128)(2,1)S(1)} %collective-permute-done.5.refs_2_, bf16[272,256]{1,0:T(8,128)(2,1)S(1)} %attend_own.1.refs_3_, ...), custom_call_target="tpu_custom_call" | custom-call | tf_op jit(solution)/shard_map/project/pallas_call | solution.py:276
  52.0 0.0 copy-start.5
  52.0 6.6 %all-to-all-start.2 = ((bf16[16,16,4096]{2,1,0:T(8,128)(2,1)}), bf16[16,16,4096]{2,1,0:T(8,128)(2,1)S(1)}, u32[]{:S(2)}, u32[]{:S(2)}) async-start(bf16[16,16,4096]{2,1,0:T(8,128)(2,1)} %bitcast.50), calls=%async_computation.2 | async-start | bytes 4194304 | tf_op jit(solution)/shard_map/all_to_all | solution.py:572
  58.6 0.0 copy-done.5
  58.6 0.1 copy.27
  58.7 0.1 fusion
  58.9 0.1 copy.29
  59.0 0.1 copy.28
  59.1 0.1 copy.30
  59.2 0.1 compare_and_fusion.1
  59.3 3.3 %and_convert_fusion.1 = bf16[128,2,8,8,16]{4,3,2,1,0:T(8,128)(2,1)} fusion(pred[8,8]{1,0:T(8,128)(4,1)S(1)} %copy.30, pred[128,2,16]{2,1,0:T(4,128)(4,1)S(1)} %compare_and_fusion.1), kind=kLoop, calls=%fused_computation.1 | loop fusion | flops 524288 | bytes 528448 | tf_op jit(solution)/shard_map/convert_element_type | solution.py:585
  62.6 0.0 copy-start.3
  62.6 0.0 copy-start.4
  62.6 5.1 %reshape.88.sel_ref = bf16[2048,128]{1,0:T(8,128)(2,1)S(1)} reshape(bf16[128,2,8,8,16]{4,3,2,1,0:T(8,128)(2,1)} %and_convert_fusion.1) | data formatting | bytes 1048576 | tf_op jit(solution)/shard_map/convert_element_type | solution.py:585
  67.7 13.9 %all-to-all-done.2 = bf16[16,16,4096]{2,1,0:T(8,128)(2,1)S(1)} async-done(((bf16[16,16,4096]{2,1,0:T(8,128)(2,1)}), bf16[16,16,4096]{2,1,0:T(8,128)(2,1)S(1)}, u32[]{:S(2)}, u32[]{:S(2)}) %all-to-all-start.2) | async-done | bytes 2097184 | tf_op jit(solution)/shard_map/all_to_all | solution.py:572
  81.6 0.0 copy-done.3
  81.6 0.0 copy-done.4
  81.6 2.0 %route.1 = (bf16[2048,512]{1,0:T(8,128)(2,1)}, f32[16,4096]{1,0:T(8,128)S(1)}, f32[16,128]{1,0:T(8,128)S(1)}) custom-call(bf16[256,4096]{1,0:T(8,128)(2,1)S(1)} %bitcast.41, bf16[16,4096]{1,0:T(8,128)(2,1)S(1)} %bitcast.47, f32[1,4096]{1,0:T(1,128)S(1)} %bitcast.48, bf16[4096,128]{1,0:T(8,128)(2,1)} %router_ref.1, f32[16,128]{1,0:T(8,128)S(1)} %get-tuple-element.36.hot_ref, ...), custom_call_target="tpu_custom_call" | custom-call | tf_op jit(solution)/shard_map/route/pallas_call | solution.py:330
  83.7 16.4 %all-to-all-start.3 = ((bf16[128,16,512]{2,1,0:T(8,128)(2,1)}), bf16[128,16,512]{2,1,0:T(8,128)(2,1)S(1)}, u32[]{:S(2)}, u32[]{:S(2)}) async-start(bf16[128,16,512]{2,1,0:T(8,128)(2,1)} %bitcast.54), calls=%async_computation.3 | async-start | bytes 4194304 | tf_op jit(solution)/shard_map/all_to_all | solution.py:587
  100.1 0.3 convert_convert_fusion
  100.3 29.8 %all-to-all-done.3 = bf16[128,16,512]{2,1,0:T(8,128)(2,1)S(1)} async-done(((bf16[128,16,512]{2,1,0:T(8,128)(2,1)}), bf16[128,16,512]{2,1,0:T(8,128)(2,1)S(1)}, u32[]{:S(2)}, u32[]{:S(2)}) %all-to-all-start.3) | async-done | bytes 2097184 | tf_op jit(solution)/shard_map/all_to_all | solution.py:587
  130.1 11.7 %expert.1 = bf16[2048,512]{1,0:T(8,128)(2,1)} custom-call(bf16[256,256]{1,0:T(8,128)(2,1)S(1)} %get-tuple-element.34.perm_ref, bf16[256,256]{1,0:T(8,128)(2,1)S(1)} %get-tuple-element.33.back_ref, bf16[2048,512]{1,0:T(8,128)(2,1)S(1)} %bitcast.40, bf16[4096,768]{1,0:T(8,128)(2,1)} %bitcast.51, bf16[4096,768]{1,0:T(8,128)(2,1)} %bitcast.52, ...), custom_call_target="tpu_custom_call" | custom-call | tf_op jit(solution)/shard_map/expert/pallas_call | solution.py:420
  141.8 4.8 %all-to-all-start.4 = ((bf16[128,16,512]{2,1,0:T(8,128)(2,1)}), bf16[128,16,512]{2,1,0:T(8,128)(2,1)S(1)}, u32[]{:S(2)}, u32[]{:S(2)}) async-start(bf16[128,16,512]{2,1,0:T(8,128)(2,1)} %bitcast.49), calls=%async_computation.4 | async-start | bytes 4194304 | tf_op jit(solution)/shard_map/all_to_all | solution.py:587
  146.6 0.1 copy.31
  146.7 0.1 copy.32
  146.8 0.1 compare_and_fusion
  146.9 3.3 %and_convert_fusion = bf16[8,16,128,2,8]{1,0,4,3,2:T(8,128)(2,1)} fusion(pred[8,8]{0,1:T(8,128)(4,1)S(1)} %iota_compare_fusion.1, pred[16,128,2]{0,2,1:T(4,128)(4,1)S(1)} %compare_and_fusion), kind=kLoop, calls=%fused_computation | loop fusion | flops 524288 | bytes 528448 | tf_op jit(solution)/shard_map/convert_element_type | solution.py:582
  150.2 5.1 %reshape.89 = bf16[128,2048]{0,1:T(8,128)(2,1)S(1)} reshape(bf16[8,16,128,2,8]{1,0,4,3,2:T(8,128)(2,1)} %and_convert_fusion) | data formatting | bytes 1048576 | tf_op jit(solution)/shard_map/convert_element_type | solution.py:582
  155.3 0.2 copy.33.mask_ref
  155.5 21.3 %all-to-all-done.4 = bf16[128,16,512]{2,1,0:T(8,128)(2,1)S(1)} async-done(((bf16[128,16,512]{2,1,0:T(8,128)(2,1)}), bf16[128,16,512]{2,1,0:T(8,128)(2,1)S(1)}, u32[]{:S(2)}, u32[]{:S(2)}) %all-to-all-start.4) | async-done | bytes 2097184 | tf_op jit(solution)/shard_map/all_to_all | solution.py:587
  176.8 1.6 finish.1
  (9 shorter events, 0.1 us)
Async XLA Ops:
  0.1 25.9 %copy-start = (bf16[1,1024,512]{2,1,0:T(8,128)(2,1)S(1)}, bf16[1,1024,512]{2,1,0:T(8,128)(2,1)}, u32[]{:S(2)}) copy-start(bf16[1,1024,512]{2,1,0:T(8,128)(2,1)} %param.15) | copy-start | bytes 3145732
  0.1 25.9 %copy-start.1 = (bf16[1,1024,512]{2,1,0:T(8,128)(2,1)S(1)}, bf16[1,1024,512]{2,1,0:T(8,128)(2,1)}, u32[]{:S(2)}) copy-start(bf16[1,1024,512]{2,1,0:T(8,128)(2,1)} %param.16) | copy-start | bytes 3145732
  3.5 11.0 %all-to-all-start = ((bf16[4,16,1280]{2,1,0:T(8,128)(2,1)}), bf16[4,16,1280]{2,1,0:T(8,128)(2,1)S(1)}, u32[]{:S(2)}, u32[]{:S(2)}) async-start(bf16[4,16,1280]{2,1,0:T(8,128)(2,1)} %bitcast.56), calls=%async_computation | async-start | bytes 327680 | tf_op jit(solution)/shard_map/all_to_all | solution.py:555
  9.3 20.9 %collective-permute-start = (bf16[2048,128]{1,0:T(8,128)(2,1)}, bf16[2048,128]{1,0:T(8,128)(2,1)}, u32[]{:S(2)}, u32[]{:S(2)}) collective-permute-start(bf16[2048,128]{1,0:T(8,128)(2,1)} %get-tuple-element.22), channel_id=1, source_target_pairs={{0,32},{8,40},{16,48},{24,56},{32,64},{40,72},{48,80},{56,88},{64,... | collective-permute-start | bytes 1572872 | tf_op jit(solution)/shard_map/ppermute | solution.py:552
  10.8 19.4 %collective-permute-start.1 = (bf16[2048,128]{1,0:T(8,128)(2,1)}, bf16[2048,128]{1,0:T(8,128)(2,1)}, u32[]{:S(2)}, u32[]{:S(2)}) collective-permute-start(bf16[2048,128]{1,0:T(8,128)(2,1)} %get-tuple-element.23), channel_id=1, source_target_pairs={{0,96},{8,104},{16,112},{24,120},{32,0},{40,8},{48,16},{56,24},{64... | collective-permute-start | bytes 1572872 | tf_op jit(solution)/shard_map/ppermute | solution.py:552
  12.0 26.0 %collective-permute-start.2 = (bf16[2048,128]{1,0:T(8,128)(2,1)}, bf16[2048,128]{1,0:T(8,128)(2,1)S(1)}, u32[]{:S(2)}, u32[]{:S(2)}) collective-permute-start(bf16[2048,128]{1,0:T(8,128)(2,1)} %get-tuple-element.26), channel_id=1, source_target_pairs={{0,64},{8,72},{16,80},{24,88},{32,96},{40,104},{48,112},{56,120},{... | collective-permute-start | bytes 1572872 | tf_op jit(solution)/shard_map/ppermute | solution.py:552
  30.2 15.3 %copy-start.6 = (s32[1,256]{1,0:T(1,128)S(1)}, s32[1,256]{1,0:T(1,128)}, u32[]{:S(2)}) copy-start(s32[1,256]{1,0:T(1,128)} %param.19) | copy-start | bytes 3076
  41.5 6.7 %collective-permute-start.3 = (bf16[272,256]{1,0:T(8,128)(2,1)S(1)}, bf16[272,256]{1,0:T(8,128)(2,1)S(1)}, u32[]{:S(2)}, u32[]{:S(2)}) collective-permute-start(bf16[272,256]{1,0:T(8,128)(2,1)S(1)} %get-tuple-element.27), channel_id=1, source_target_pairs={{0,16},{8,24},{16,0},{24,8},{32,48},{40,56},{48,32},{56,40},{64,80... | collective-permute-start | bytes 417800 | tf_op jit(solution)/shard_map/ppermute | solution.py:564
  42.9 5.6 %collective-permute-start.4 = (bf16[272,256]{1,0:T(8,128)(2,1)S(1)}, bf16[272,256]{1,0:T(8,128)(2,1)S(1)}, u32[]{:S(2)}, u32[]{:S(2)}) collective-permute-start(bf16[272,256]{1,0:T(8,128)(2,1)S(1)} %get-tuple-element.28), channel_id=1, source_target_pairs={{0,8},{8,16},{16,24},{24,0},{32,40},{40,48},{48,56},{56,32},{64,72... | collective-permute-start | bytes 417800 | tf_op jit(solution)/shard_map/ppermute | solution.py:564
  43.2 5.3 %collective-permute-start.5 = (bf16[272,256]{1,0:T(8,128)(2,1)S(1)}, bf16[272,256]{1,0:T(8,128)(2,1)S(1)}, u32[]{:S(2)}, u32[]{:S(2)}) collective-permute-start(bf16[272,256]{1,0:T(8,128)(2,1)S(1)} %get-tuple-element.29), channel_id=1, source_target_pairs={{0,24},{8,0},{16,8},{24,16},{32,56},{40,32},{48,40},{56,48},{64,88... | collective-permute-start | bytes 417800 | tf_op jit(solution)/shard_map/ppermute | solution.py:564
  45.7 2.8 %copy-start.2 = (bf16[256,4096]{1,0:T(8,128)(2,1)S(1)}, bf16[256,4096]{1,0:T(8,128)(2,1)}, u32[]{:S(2)}) copy-start(bf16[256,4096]{1,0:T(8,128)(2,1)} %refs_4_.1) | copy-start | bytes 6291460
  52.0 6.6 %copy-start.5 = (s32[1,16,8]{1,2,0:T(8,128)S(1)}, s32[1,16,8]{1,2,0:T(8,128)}, u32[]{:S(2)}) copy-start(s32[1,16,8]{1,2,0:T(8,128)} %param.24) | copy-start | bytes 1540
  52.0 29.6 %all-to-all-start.2 = ((bf16[16,16,4096]{2,1,0:T(8,128)(2,1)}), bf16[16,16,4096]{2,1,0:T(8,128)(2,1)S(1)}, u32[]{:S(2)}, u32[]{:S(2)}) async-start(bf16[16,16,4096]{2,1,0:T(8,128)(2,1)} %bitcast.50), calls=%async_computation.2 | async-start | bytes 4194304 | tf_op jit(solution)/shard_map/all_to_all | solution.py:572
  62.6 19.0 %copy-start.3 = (bf16[1,16,4096]{2,1,0:T(8,128)(2,1)S(1)}, bf16[1,16,4096]{2,1,0:T(8,128)(2,1)}, u32[]{:S(2)}) copy-start(bf16[1,16,4096]{2,1,0:T(8,128)(2,1)} %param.21) | copy-start | bytes 393220
  62.6 19.0 %copy-start.4 = (f32[4096]{0:T(1024)S(1)}, f32[4096]{0:T(1024)}, u32[]{:S(2)}) copy-start(f32[4096]{0:T(1024)} %param.22) | copy-start | bytes 49156
  83.7 46.5 %all-to-all-start.3 = ((bf16[128,16,512]{2,1,0:T(8,128)(2,1)}), bf16[128,16,512]{2,1,0:T(8,128)(2,1)S(1)}, u32[]{:S(2)}, u32[]{:S(2)}) async-start(bf16[128,16,512]{2,1,0:T(8,128)(2,1)} %bitcast.54), calls=%async_computation.3 | async-start | bytes 4194304 | tf_op jit(solution)/shard_map/all_to_all | solution.py:587
  141.8 35.0 %all-to-all-start.4 = ((bf16[128,16,512]{2,1,0:T(8,128)(2,1)}), bf16[128,16,512]{2,1,0:T(8,128)(2,1)S(1)}, u32[]{:S(2)}, u32[]{:S(2)}) async-start(bf16[128,16,512]{2,1,0:T(8,128)(2,1)} %bitcast.49), calls=%async_computation.4 | async-start | bytes 4194304 | tf_op jit(solution)/shard_map/all_to_all | solution.py:587

commit v5 on v4

--- a/solution.py
+++ b/solution.py
@@ -121,7 +121,7 @@
         return top, one(h + 1, s1, after, stats)
 
     first = scores(q_of(0), chunks, s0)
-    l_ref[...] = lax.fori_loop(0, GROUP // 2, pair, (first, jnp.zeros(l_ref.shape, F32)), unroll=2)[1]
+    l_ref[...] = lax.fori_loop(0, GROUP // 2, pair, (first, jnp.zeros(l_ref.shape, F32)), unroll=4)[1]
 
 
 def state_shapes(rows):
@@ -243,15 +243,20 @@
     r = lax.broadcasted_iota(jnp.int32, (rows, rows), 0)
     c = lax.broadcasted_iota(jnp.int32, (rows, rows), 1)
     eye = (r == c).astype(F32).astype(BF)
-    stats = [nt(eye, p[rows:, :]) for p in parts]
+    stats = [p[rows:, :].astype(F32) for p in parts]
+    shares = []
     for h in range(2):
         at = 3 * h
-        lse = [s[:, at : at + 1] + s[:, at + 1 : at + 2] + s[:, at + 2 : at + 3] for s in stats]
+        lse = [s[at : at + 1, :] + s[at + 1 : at + 2, :] + s[at + 2 : at + 3, :] for s in stats]
         top = jnp.maximum(jnp.maximum(lse[0], lse[1]), jnp.maximum(lse[2], lse[3]))
         w = [jnp.exp2(v - top) for v in lse]
         inv = 1.0 / (w[0] + w[1] + w[2] + w[3])
+        shares += [v * inv for v in w]
+    high, low = hi_lo(jnp.concatenate(shares + shares, axis=0))
+    columns = nt(eye, high) + nt(eye, low)
+    for h in range(2):
         cols = slice(h * HD, (h + 1) * HD)
-        acc = sum(p[:rows, cols].astype(F32) * (v * inv) for p, v in zip(parts, w))
+        acc = sum(p[:rows, cols].astype(F32) * columns[:, 4 * h + i : 4 * h + i + 1] for i, p in enumerate(parts))
         att[:, cols] = acc.astype(BF)
 
 

time: 179 us -> 179 us (level)
  transfers between devices with their start and end apart: 10 -> 10, of which waited for: 5 -> 4; matrix products, arithmetic and copies ran while one was open for 10% -> 10% of each run, Pallas kernels for 8% -> 8%
where the time goes in v5:
time: 179 us; the launch traced here: 178 us
  waiting for transfers between devices  65.4 us (37%)
  starting transfers between devices  43 us (24%)
  Pallas kernels  39.5 us (22%)
  blocking collectives  11.4 us (6%)
  local copies, waits for them, and re-layouts  11.2 us (6%)
  other arithmetic  7.36 us (4%)
    all_to_all x2, waiting for transfers between devices, local(): lax.all_to_all(a.reshape(experts, CAP * CHUNK, -1), ('seq', 'grp'), 0, 0,...  51.1 us
    all_to_all x2, starting transfers between devices, local(): lax.all_to_all(a.reshape(experts, CAP * CHUNK, -1), ('seq', 'grp'), 0, 0,...  21.2 us
    all_to_all x1, waiting for transfers between devices, local(): lax.all_to_all(projected.reshape(seq_count, rows, -1), 'seq', 0, 0, tiled...  13.7 us
    pallas_call x1, Pallas kernels, expert(): pl.pallas_call(expert_body, out_shape=pltpu.HBM(arrived.shape, BF), grid=...  11.7 us
    all_to_all x1, blocking collectives, local(): lax.all_to_all(jnp.broadcast_to(mine, (across, *mine.shape)), 'seq', 0, 0...  11.4 us
    pallas_call x1, Pallas kernels, attend_more(): pl.pallas_call(more_body, out_shape=state_shapes(rows), scratch_shapes=he...  7.5 us
    all_to_all x1, starting transfers between devices, local(): lax.all_to_all(projected.reshape(seq_count, rows, -1), 'seq', 0, 0, tiled...  6.85 us
    pallas_call x2, Pallas kernels, attend_last(): pl.pallas_call(lambda *refs: last_body(shifts, *refs), out_shape=[jax.Sha...  6.12 us
  transfers between devices with their start and end apart: 10, of which 4 were waited for; matrix products, arithmetic and copies ran while one was open for 10% of the time, Pallas kernels for 8%

profile of v5, /device:TPU:1, one launch (start us, length us, event | category | flops | bytes accessed | tf_op | source)
XLA Modules:
  0.0 178.2 jit_solution(9942100915024155315)
XLA Ops:
  0.0 0.1 pad_add_fusion.idx.refs_0_
  0.1 0.0 copy-start
  0.1 0.0 copy-start.1
  0.1 3.4 %ready.1 = (bf16[64,1280]{1,0:T(8,128)(2,1)}, bf16[2048,128]{1,0:T(8,128)(2,1)}, bf16[2048,128]{1,0:T(8,128)(2,1)}, bf16[2048,128]{1,0:T(8,128)(2,1)}) custom-call(s32[2]{0:T(128)S(1)} %pad_add_fusion.idx.refs_0_, bf16[16,4096]{1,0:T(8,128)(2,1)} %bitcast.57, bf16[16,512]{1,0:T(8,128)(2,1)} %bitcast.59, bf16[16,512]{1,0:T(8,128)(2,1)} %bitcast.60, ...), custom_call_target="tpu_custom_call" | custom-call | tf_op jit(solution)/shard_map/ready/pallas_call | solution.py:508
  3.5 5.9 %all-to-all-start = ((bf16[4,16,1280]{2,1,0:T(8,128)(2,1)}), bf16[4,16,1280]{2,1,0:T(8,128)(2,1)S(1)}, u32[]{:S(2)}, u32[]{:S(2)}) async-start(bf16[4,16,1280]{2,1,0:T(8,128)(2,1)} %bitcast.56), calls=%async_computation | async-start | bytes 327680 | tf_op jit(solution)/shard_map/all_to_all | solution.py:560
  9.3 1.5 collective-permute-start
  10.8 1.2 collective-permute-start.1
  12.0 1.7 collective-permute-start.2
  13.8 0.7 all-to-all-done
  14.5 11.4 %all_to_all.25 = bf16[4,64,1280]{2,1,0:T(8,128)(2,1)S(1)} all-to-all(bf16[4,64,1280]{2,1,0:T(8,128)(2,1)S(1)} %broadcast_in_dim.6), channel_id=1, replica_groups={{0,8,16,24},{32,40,48,56},{64,72,80,88},{96,104,112,120},{1,9,17,25},{3..., dimensions={0} | all-to-all | bytes 1310720 | tf_op jit(solution)/shard_map/all_to_all | solution.py:563
  25.9 0.0 copy-done
  25.9 0.0 copy-done.1
  25.9 3.9 %attend_start.1 = (f32[256,1024]{1,0:T(8,128)S(1)}, f32[256,128]{1,0:T(8,128)S(1)}) custom-call(s32[2]{0:T(128)S(1)} %pad_add_fusion.idx.refs_0_, bf16[256,1280]{1,0:T(8,128)(2,1)S(1)} %bitcast.34, bf16[1024,512]{1,0:T(8,128)(2,1)S(1)} %bitcast.44, bf16[1024,512]{1,0:T(8,128)(2,1)S(1)} %bitcast.46), custom_call_target="tpu_custom_call" | custom-call | tf_op jit(solution)/shard_map/attend_start/pallas_call | solution.py:143
  29.8 0.0 collective-permute-done.b_ref
  29.8 0.0 collective-permute-done.1.c_ref
  29.9 0.0 copy-start.6
  29.9 7.5 %attend_more.1 = (f32[256,1024]{1,0:T(8,128)S(1)}, f32[256,128]{1,0:T(8,128)S(1)}) custom-call(bf16[256,1280]{1,0:T(8,128)(2,1)S(1)} %bitcast.35, f32[256,1024]{1,0:T(8,128)S(1)} %get-tuple-element.20.so_ref, f32[256,128]{1,0:T(8,128)S(1)} %get-tuple-element.21.sl_ref, bf16[2048,128]{1,0:T(8,128)(2,1)} %collective-permute-done.b_ref, ...), custom_call_target="tpu_custom_call" | custom-call | tf_op jit(solution)/shard_map/attend_more/pallas_call | solution.py:170
  37.4 0.0 collective-permute-done.2.refs_4_
  37.4 3.7 %attend_last.1 = (bf16[272,256]{1,0:T(8,128)(2,1)S(1)}, bf16[272,256]{1,0:T(8,128)(2,1)S(1)}, bf16[272,256]{1,0:T(8,128)(2,1)S(1)}) custom-call(s32[2]{0:T(128)S(1)} %pad_add_fusion.idx.refs_0_, bf16[256,1280]{1,0:T(8,128)(2,1)S(1)} %bitcast.36, f32[256,1024]{1,0:T(8,128)S(1)} %get-tuple-element.24.refs_2_, f32[256,128]{1,0:T(8,128)S(1)} %get-tuple-element.25.refs_3_, ...), custom_call_target="tpu_custom_call" | custom-call | tf_op jit(solution)/shard_map/attend_last/pallas_call | solution.py:226
  41.1 2.0 %collective-permute-start.3 = (bf16[272,256]{1,0:T(8,128)(2,1)S(1)}, bf16[272,256]{1,0:T(8,128)(2,1)S(1)}, u32[]{:S(2)}, u32[]{:S(2)}) collective-permute-start(bf16[272,256]{1,0:T(8,128)(2,1)S(1)} %get-tuple-element.27), channel_id=1, source_target_pairs={{0,16},{8,24},{16,0},{24,8},{32,48},{40,56},{48,32},{56,40},{64,80... | collective-permute-start | bytes 417800 | tf_op jit(solution)/shard_map/ppermute | solution.py:569
  43.0 0.3 collective-permute-start.4
  43.4 2.4 %collective-permute-start.5 = (bf16[272,256]{1,0:T(8,128)(2,1)S(1)}, bf16[272,256]{1,0:T(8,128)(2,1)S(1)}, u32[]{:S(2)}, u32[]{:S(2)}) collective-permute-start(bf16[272,256]{1,0:T(8,128)(2,1)S(1)} %get-tuple-element.29), channel_id=1, source_target_pairs={{0,24},{8,0},{16,8},{24,16},{32,56},{40,32},{48,40},{56,48},{64,88... | collective-permute-start | bytes 417800 | tf_op jit(solution)/shard_map/ppermute | solution.py:569
  45.7 0.0 copy-done.6
  45.7 0.1 copy.26.refs_5_
  45.9 0.0 copy-start.2
  45.9 2.4 %attend_own.1.refs_3_ = bf16[272,256]{1,0:T(8,128)(2,1)S(1)} custom-call(s32[2]{0:T(128)S(1)} %pad_add_fusion.idx.refs_0_, bf16[256,1280]{1,0:T(8,128)(2,1)S(1)} %bitcast.37, f32[256,1024]{1,0:T(8,128)S(1)} %get-tuple-element.24.refs_2_, f32[256,128]{1,0:T(8,128)S(1)} %get-tuple-element.25.refs_3_, bf16[2048,128]{1,0:T(8,128)(2,1)S(1)} %collective-permute-done.2.refs_4_, ...), custom_call_target="tpu_custom_call" | custom-call | tf_op jit(solution)/shard_map/attend_own/pallas_call | solution.py:226
  48.3 0.0 collective-permute-done.3.refs_0_
  48.3 0.0 collective-permute-done.4.refs_1_
  48.3 0.0 collective-permute-done.5.refs_2_
  48.3 0.0 copy-done.2
  48.4 3.3 %project.1 = bf16[256,4096]{1,0:T(8,128)(2,1)} custom-call(bf16[272,256]{1,0:T(8,128)(2,1)S(1)} %collective-permute-done.3.refs_0_, bf16[272,256]{1,0:T(8,128)(2,1)S(1)} %collective-permute-done.4.refs_1_, bf16[272,256]{1,0:T(8,128)(2,1)S(1)} %collective-permute-done.5.refs_2_, bf16[272,256]{1,0:T(8,128)(2,1)S(1)} %attend_own.1.refs_3_, ...), custom_call_target="tpu_custom_call" | custom-call | tf_op jit(solution)/shard_map/project/pallas_call | solution.py:281
  51.7 0.0 copy-start.5
  51.7 6.8 %all-to-all-start.2 = ((bf16[16,16,4096]{2,1,0:T(8,128)(2,1)}), bf16[16,16,4096]{2,1,0:T(8,128)(2,1)S(1)}, u32[]{:S(2)}, u32[]{:S(2)}) async-start(bf16[16,16,4096]{2,1,0:T(8,128)(2,1)} %bitcast.50), calls=%async_computation.2 | async-start | bytes 4194304 | tf_op jit(solution)/shard_map/all_to_all | solution.py:577
  58.6 0.0 copy-done.5
  58.6 0.1 copy.27
  58.6 0.1 fusion
  58.8 0.1 copy.29
  58.9 0.1 copy.28
  59.0 0.1 copy.30
  59.1 0.1 compare_and_fusion.1
  59.2 3.3 %and_convert_fusion.1 = bf16[128,2,8,8,16]{4,3,2,1,0:T(8,128)(2,1)} fusion(pred[8,8]{1,0:T(8,128)(4,1)S(1)} %copy.30, pred[128,2,16]{2,1,0:T(4,128)(4,1)S(1)} %compare_and_fusion.1), kind=kLoop, calls=%fused_computation.1 | loop fusion | flops 524288 | bytes 528448 | tf_op jit(solution)/shard_map/convert_element_type | solution.py:590
  62.5 0.0 copy-start.3
  62.5 0.0 copy-start.4
  62.5 5.1 %reshape.88.sel_ref = bf16[2048,128]{1,0:T(8,128)(2,1)S(1)} reshape(bf16[128,2,8,8,16]{4,3,2,1,0:T(8,128)(2,1)} %and_convert_fusion.1) | data formatting | bytes 1048576 | tf_op jit(solution)/shard_map/convert_element_type | solution.py:590
  67.7 13.7 %all-to-all-done.2 = bf16[16,16,4096]{2,1,0:T(8,128)(2,1)S(1)} async-done(((bf16[16,16,4096]{2,1,0:T(8,128)(2,1)}), bf16[16,16,4096]{2,1,0:T(8,128)(2,1)S(1)}, u32[]{:S(2)}, u32[]{:S(2)}) %all-to-all-start.2) | async-done | bytes 2097184 | tf_op jit(solution)/shard_map/all_to_all | solution.py:577
  81.3 0.0 copy-done.3
  81.3 0.0 copy-done.4
  81.3 2.0 %route.1 = (bf16[2048,512]{1,0:T(8,128)(2,1)}, f32[16,4096]{1,0:T(8,128)S(1)}, f32[16,128]{1,0:T(8,128)S(1)}) custom-call(bf16[256,4096]{1,0:T(8,128)(2,1)S(1)} %bitcast.41, bf16[16,4096]{1,0:T(8,128)(2,1)S(1)} %bitcast.47, f32[1,4096]{1,0:T(1,128)S(1)} %bitcast.48, bf16[4096,128]{1,0:T(8,128)(2,1)} %router_ref.1, f32[16,128]{1,0:T(8,128)S(1)} %get-tuple-element.36.hot_ref, ...), custom_call_target="tpu_custom_call" | custom-call | tf_op jit(solution)/shard_map/route/pallas_call | solution.py:335
  83.4 16.5 %all-to-all-start.3 = ((bf16[128,16,512]{2,1,0:T(8,128)(2,1)}), bf16[128,16,512]{2,1,0:T(8,128)(2,1)S(1)}, u32[]{:S(2)}, u32[]{:S(2)}) async-start(bf16[128,16,512]{2,1,0:T(8,128)(2,1)} %bitcast.54), calls=%async_computation.3 | async-start | bytes 4194304 | tf_op jit(solution)/shard_map/all_to_all | solution.py:592
  99.9 0.3 convert_convert_fusion
  100.2 29.8 %all-to-all-done.3 = bf16[128,16,512]{2,1,0:T(8,128)(2,1)S(1)} async-done(((bf16[128,16,512]{2,1,0:T(8,128)(2,1)}), bf16[128,16,512]{2,1,0:T(8,128)(2,1)S(1)}, u32[]{:S(2)}, u32[]{:S(2)}) %all-to-all-start.3) | async-done | bytes 2097184 | tf_op jit(solution)/shard_map/all_to_all | solution.py:592
  130.0 11.7 %expert.1 = bf16[2048,512]{1,0:T(8,128)(2,1)} custom-call(bf16[256,256]{1,0:T(8,128)(2,1)S(1)} %get-tuple-element.34.perm_ref, bf16[256,256]{1,0:T(8,128)(2,1)S(1)} %get-tuple-element.33.back_ref, bf16[2048,512]{1,0:T(8,128)(2,1)S(1)} %bitcast.40, bf16[4096,768]{1,0:T(8,128)(2,1)} %bitcast.51, bf16[4096,768]{1,0:T(8,128)(2,1)} %bitcast.52, ...), custom_call_target="tpu_custom_call" | custom-call | tf_op jit(solution)/shard_map/expert/pallas_call | solution.py:425
  141.6 4.8 %all-to-all-start.4 = ((bf16[128,16,512]{2,1,0:T(8,128)(2,1)}), bf16[128,16,512]{2,1,0:T(8,128)(2,1)S(1)}, u32[]{:S(2)}, u32[]{:S(2)}) async-start(bf16[128,16,512]{2,1,0:T(8,128)(2,1)} %bitcast.49), calls=%async_computation.4 | async-start | bytes 4194304 | tf_op jit(solution)/shard_map/all_to_all | solution.py:592
  146.4 0.1 copy.31
  146.5 0.1 copy.32
  146.6 0.1 compare_and_fusion
  146.8 3.3 %and_convert_fusion = bf16[8,16,128,2,8]{1,0,4,3,2:T(8,128)(2,1)} fusion(pred[8,8]{0,1:T(8,128)(4,1)S(1)} %iota_compare_fusion.1, pred[16,128,2]{0,2,1:T(4,128)(4,1)S(1)} %compare_and_fusion), kind=kLoop, calls=%fused_computation | loop fusion | flops 524288 | bytes 528448 | tf_op jit(solution)/shard_map/convert_element_type | solution.py:587
  150.1 5.1 %reshape.89 = bf16[128,2048]{0,1:T(8,128)(2,1)S(1)} reshape(bf16[8,16,128,2,8]{1,0,4,3,2:T(8,128)(2,1)} %and_convert_fusion) | data formatting | bytes 1048576 | tf_op jit(solution)/shard_map/convert_element_type | solution.py:587
  155.2 0.2 copy.33.mask_ref
  155.4 21.3 %all-to-all-done.4 = bf16[128,16,512]{2,1,0:T(8,128)(2,1)S(1)} async-done(((bf16[128,16,512]{2,1,0:T(8,128)(2,1)}), bf16[128,16,512]{2,1,0:T(8,128)(2,1)S(1)}, u32[]{:S(2)}, u32[]{:S(2)}) %all-to-all-start.4) | async-done | bytes 2097184 | tf_op jit(solution)/shard_map/all_to_all | solution.py:592
  176.6 1.6 finish.1
  (9 shorter events, 0.1 us)
Async XLA Ops:
  0.1 25.9 %copy-start = (bf16[1,1024,512]{2,1,0:T(8,128)(2,1)S(1)}, bf16[1,1024,512]{2,1,0:T(8,128)(2,1)}, u32[]{:S(2)}) copy-start(bf16[1,1024,512]{2,1,0:T(8,128)(2,1)} %param.15) | copy-start | bytes 3145732
  0.1 25.9 %copy-start.1 = (bf16[1,1024,512]{2,1,0:T(8,128)(2,1)S(1)}, bf16[1,1024,512]{2,1,0:T(8,128)(2,1)}, u32[]{:S(2)}) copy-start(bf16[1,1024,512]{2,1,0:T(8,128)(2,1)} %param.16) | copy-start | bytes 3145732
  3.5 11.0 %all-to-all-start = ((bf16[4,16,1280]{2,1,0:T(8,128)(2,1)}), bf16[4,16,1280]{2,1,0:T(8,128)(2,1)S(1)}, u32[]{:S(2)}, u32[]{:S(2)}) async-start(bf16[4,16,1280]{2,1,0:T(8,128)(2,1)} %bitcast.56), calls=%async_computation | async-start | bytes 327680 | tf_op jit(solution)/shard_map/all_to_all | solution.py:560
  9.3 20.5 %collective-permute-start = (bf16[2048,128]{1,0:T(8,128)(2,1)}, bf16[2048,128]{1,0:T(8,128)(2,1)}, u32[]{:S(2)}, u32[]{:S(2)}) collective-permute-start(bf16[2048,128]{1,0:T(8,128)(2,1)} %get-tuple-element.22), channel_id=1, source_target_pairs={{0,32},{8,40},{16,48},{24,56},{32,64},{40,72},{48,80},{56,88},{64,... | collective-permute-start | bytes 1572872 | tf_op jit(solution)/shard_map/ppermute | solution.py:557
  10.8 19.1 %collective-permute-start.1 = (bf16[2048,128]{1,0:T(8,128)(2,1)}, bf16[2048,128]{1,0:T(8,128)(2,1)}, u32[]{:S(2)}, u32[]{:S(2)}) collective-permute-start(bf16[2048,128]{1,0:T(8,128)(2,1)} %get-tuple-element.23), channel_id=1, source_target_pairs={{0,96},{8,104},{16,112},{24,120},{32,0},{40,8},{48,16},{56,24},{64... | collective-permute-start | bytes 1572872 | tf_op jit(solution)/shard_map/ppermute | solution.py:557
  12.0 25.4 %collective-permute-start.2 = (bf16[2048,128]{1,0:T(8,128)(2,1)}, bf16[2048,128]{1,0:T(8,128)(2,1)S(1)}, u32[]{:S(2)}, u32[]{:S(2)}) collective-permute-start(bf16[2048,128]{1,0:T(8,128)(2,1)} %get-tuple-element.26), channel_id=1, source_target_pairs={{0,64},{8,72},{16,80},{24,88},{32,96},{40,104},{48,112},{56,120},{... | collective-permute-start | bytes 1572872 | tf_op jit(solution)/shard_map/ppermute | solution.py:557
  29.9 15.9 %copy-start.6 = (s32[1,256]{1,0:T(1,128)S(1)}, s32[1,256]{1,0:T(1,128)}, u32[]{:S(2)}) copy-start(s32[1,256]{1,0:T(1,128)} %param.19) | copy-start | bytes 3076
  41.1 7.3 %collective-permute-start.3 = (bf16[272,256]{1,0:T(8,128)(2,1)S(1)}, bf16[272,256]{1,0:T(8,128)(2,1)S(1)}, u32[]{:S(2)}, u32[]{:S(2)}) collective-permute-start(bf16[272,256]{1,0:T(8,128)(2,1)S(1)} %get-tuple-element.27), channel_id=1, source_target_pairs={{0,16},{8,24},{16,0},{24,8},{32,48},{40,56},{48,32},{56,40},{64,80... | collective-permute-start | bytes 417800 | tf_op jit(solution)/shard_map/ppermute | solution.py:569
  43.0 5.3 %collective-permute-start.4 = (bf16[272,256]{1,0:T(8,128)(2,1)S(1)}, bf16[272,256]{1,0:T(8,128)(2,1)S(1)}, u32[]{:S(2)}, u32[]{:S(2)}) collective-permute-start(bf16[272,256]{1,0:T(8,128)(2,1)S(1)} %get-tuple-element.28), channel_id=1, source_target_pairs={{0,8},{8,16},{16,24},{24,0},{32,40},{40,48},{48,56},{56,32},{64,72... | collective-permute-start | bytes 417800 | tf_op jit(solution)/shard_map/ppermute | solution.py:569
  43.4 5.0 %collective-permute-start.5 = (bf16[272,256]{1,0:T(8,128)(2,1)S(1)}, bf16[272,256]{1,0:T(8,128)(2,1)S(1)}, u32[]{:S(2)}, u32[]{:S(2)}) collective-permute-start(bf16[272,256]{1,0:T(8,128)(2,1)S(1)} %get-tuple-element.29), channel_id=1, source_target_pairs={{0,24},{8,0},{16,8},{24,16},{32,56},{40,32},{48,40},{56,48},{64,88... | collective-permute-start | bytes 417800 | tf_op jit(solution)/shard_map/ppermute | solution.py:569
  45.9 2.5 %copy-start.2 = (bf16[256,4096]{1,0:T(8,128)(2,1)S(1)}, bf16[256,4096]{1,0:T(8,128)(2,1)}, u32[]{:S(2)}) copy-start(bf16[256,4096]{1,0:T(8,128)(2,1)} %refs_4_.1) | copy-start | bytes 6291460
  51.7 6.9 %copy-start.5 = (s32[1,16,8]{1,2,0:T(8,128)S(1)}, s32[1,16,8]{1,2,0:T(8,128)}, u32[]{:S(2)}) copy-start(s32[1,16,8]{1,2,0:T(8,128)} %param.24) | copy-start | bytes 1540
  51.7 29.6 %all-to-all-start.2 = ((bf16[16,16,4096]{2,1,0:T(8,128)(2,1)}), bf16[16,16,4096]{2,1,0:T(8,128)(2,1)S(1)}, u32[]{:S(2)}, u32[]{:S(2)}) async-start(bf16[16,16,4096]{2,1,0:T(8,128)(2,1)} %bitcast.50), calls=%async_computation.2 | async-start | bytes 4194304 | tf_op jit(solution)/shard_map/all_to_all | solution.py:577
  62.5 18.8 %copy-start.3 = (bf16[1,16,4096]{2,1,0:T(8,128)(2,1)S(1)}, bf16[1,16,4096]{2,1,0:T(8,128)(2,1)}, u32[]{:S(2)}) copy-start(bf16[1,16,4096]{2,1,0:T(8,128)(2,1)} %param.21) | copy-start | bytes 393220
  62.5 18.8 %copy-start.4 = (f32[4096]{0:T(1024)S(1)}, f32[4096]{0:T(1024)}, u32[]{:S(2)}) copy-start(f32[4096]{0:T(1024)} %param.22) | copy-start | bytes 49156
  83.4 46.6 %all-to-all-start.3 = ((bf16[128,16,512]{2,1,0:T(8,128)(2,1)}), bf16[128,16,512]{2,1,0:T(8,128)(2,1)S(1)}, u32[]{:S(2)}, u32[]{:S(2)}) async-start(bf16[128,16,512]{2,1,0:T(8,128)(2,1)} %bitcast.54), calls=%async_computation.3 | async-start | bytes 4194304 | tf_op jit(solution)/shard_map/all_to_all | solution.py:592
  141.6 35.0 %all-to-all-start.4 = ((bf16[128,16,512]{2,1,0:T(8,128)(2,1)}), bf16[128,16,512]{2,1,0:T(8,128)(2,1)S(1)}, u32[]{:S(2)}, u32[]{:S(2)}) async-start(bf16[128,16,512]{2,1,0:T(8,128)(2,1)} %bitcast.49), calls=%async_computation.4 | async-start | bytes 4194304 | tf_op jit(solution)/shard_map/all_to_all | solution.py:592
